TPU v7x, 128 devices: a whole 4x4x4 slice. The times are simulated.
128 devices in a mesh: dp: 8 (over z_hi, x), seq: 16 (over z_lo, y, core).
Axes of the slice: x: 4, y: 4, z: 4 (z_hi: 2, z_lo: 2; z = z_hi * 2 + z_lo), core: 2. Of those that a mesh axis runs over, the one named last changes fastest.
Arguments:
- stream: bfloat16 [8, 512, 1536], P('dp', 'seq'), may hold values from -6 to 6
- queries: bfloat16 [8, 512, 1536], P('dp', 'seq'), may hold values from -30 to 30
- new_keys: bfloat16 [8, 512, 1536], P('dp', 'seq'), may hold values from -6.5 to 6.5
- new_values: bfloat16 [8, 512, 1536], P('dp', 'seq'), may hold values from -6 to 6
- cache_keys: bfloat16 [8, 1536, 1536], P('dp', 'seq'), may hold values from -6.375 to 6.375
- cache_values: bfloat16 [8, 1536, 1536], P('dp', 'seq'), may hold values from -6 to 6
- cache_frames: int32 [8, 1536], P('dp', 'seq'), may hold values from 0 to 20, as said below
- group_index: int32 [8], P('dp'), may hold values from 4 to 7, as said below
- timestep: int32 [8], P('dp'), may hold values from 0 to 3
- gate_table: float32 [4, 1536], replicated, may hold values from 0.1 to 1.9
- attn_out_weight: bfloat16 [1536, 1536], replicated, may hold values from -0.15625 to 0.15625
- critic_in: bfloat16 [131072, 1536], P(('dp', 'seq')), may hold values from -24 to 24
- critic_cot: bfloat16 [131072, 1536], P(('dp', 'seq')), may hold values from -6 to 6
- critic_weight: bfloat16 [1536, 1536], P(('dp', 'seq')), may hold values from -0.15625 to 0.15625
Outputs:
- stream_out: bfloat16 [8, 512, 1536], P('dp', 'seq')
- critic_grad_in: bfloat16 [131072, 1536], P(('dp', 'seq'))
- critic_grad_weight: float32 [1536, 1536], P(('dp', 'seq'))
Inputs may be any that keep to these rules, and one draw needn't show every extreme that they name: `group_index`: index of the frame group; both ends are reached in every draw. `cache_frames`: sample b's cache holds the 12 frames 3 * group_index[b] - 12 to 3 * group_index[b] - 1, each in one contiguous run of slots, runs of equal length up to one slot, in a rotated order.
All inputs are finite; a program needn't handle non-finite values.
Results may differ from a plain program's by a relative error of at most 0.0045.
Values may be sent and summed in bfloat16 or wider, within the bound.
No kernel may reach another device: no remote copies, remote signals or barrier semaphores. Data moves between devices by JAX's collectives and lax.ppermute only.
A program may use at most 128 MiB of HBM per device.

v0:
```python
import jax
import jax.numpy as jnp
from jax import lax
from jax.experimental import pallas as pl
from jax.experimental.pallas import tpu as pltpu
from jax.sharding import Mesh
from jax.sharding import PartitionSpec as P

HEAD = 128
FRAMES_GROUP = 3
WINDOW_FRAMES = 9
BF = jnp.bfloat16
F32 = jnp.float32


SWAP = [(0, 1), (1, 0)]


def turn(k):
    return [(i, (i + k) % 4) for i in range(4)]


def in_vmem(x):
    return pltpu.with_memory_space_constraint(x, pltpu.VMEM)


def in_hbm(x):
    return pltpu.with_memory_space_constraint(x, pltpu.HBM)


def room(mebibytes=16, **more):
    return pltpu.CompilerParams(vmem_limit_bytes=mebibytes * 2**20, **more)


def any_spec():
    return pl.BlockSpec(memory_space=pl.ANY)


def scalars():
    return pl.BlockSpec(memory_space=pltpu.SMEM)


def packed(place, group_index, frames, arrays):
    width = arrays[0].shape[1]
    quarter = width // 4
    starts, total = [], 0
    for a in arrays:
        starts.append(total)
        total += a.shape[0]

    def kernel(place_ref, group_ref, frames_ref, *refs):
        ins, outs, live_ref = refs[:5], refs[5:9], refs[9]
        first = FRAMES_GROUP * group_ref[0]
        f = frames_ref[...]
        live_ref[...] = jnp.zeros_like(live_ref)
        live_ref[:, 0:128] = jnp.ones((16, 128), F32)
        alive = (f < first) & (f >= first - WINDOW_FRAMES)
        live_ref[:, 0:96] = jnp.broadcast_to(alive.astype(F32), (16, 96))
        spot = place_ref[2] * 2 + place_ref[0]
        for here in range(4):

            @pl.when(spot == here)
            def _():
                for n, q in enumerate((here, here ^ 1, here ^ 2, here ^ 3)):
                    for a, at in zip(ins, starts):
                        outs[n][at : at + a.shape[0], :] = a[:, q * quarter : (q + 1) * quarter]

        for out in outs:
            out[total : total + 16, :] = live_ref[...].astype(BF)

    return pl.pallas_call(
        kernel,
        out_shape=[jax.ShapeDtypeStruct((total + 16, quarter), BF)] * 4,
        in_specs=[scalars(), scalars()] + [pl.BlockSpec()] * 6,
        scratch_shapes=[pltpu.VMEM((16, quarter), F32)],
        compiler_params=room(),
        name="packed",
    )(place, group_index, frames, *[in_hbm(a) for a in arrays])


def attend(sets, queries):
    quarter = 3 * HEAD

    def kernel(*refs):
        set_refs, query_refs, outs = refs[:4], refs[4:8], refs[8:]
        rows = 128
        lane = lax.broadcasted_iota(jnp.int32, (rows, HEAD), 1)
        alive = jnp.concatenate([r[288:304, 0:128] for r in set_refs], axis=1)
        alive = alive.astype(F32)[0:1, :] > 0.5
        stats = [jnp.zeros((rows, HEAD), F32) for _ in range(4)]
        for h in range(3):
            cols = slice(h * HEAD, (h + 1) * HEAD)
            k = jnp.concatenate([r[0:128, cols] for r in set_refs], axis=0)
            v = jnp.concatenate([r[128:256, cols] for r in set_refs], axis=0)
            for r in range(4):
                s = lax.dot_general(
                    query_refs[r][:, cols], k, (((1,), (1,)), ((), ())), preferred_element_type=F32
                ) * (HEAD ** (-0.5))
                s = jnp.where(alive, s, -1e30)
                top = jnp.max(s, axis=1, keepdims=True).astype(BF).astype(F32)
                w = jnp.where(alive, jnp.exp(s - top), 0.0)
                total = jnp.sum(w, axis=1, keepdims=True)
                o = jnp.dot(w.astype(BF), v, preferred_element_type=F32)
                outs[r][:, cols] = o.astype(BF)
                high = total.astype(BF).astype(F32)
                stats[r] = jnp.where(lane == h, top, stats[r])
                stats[r] = jnp.where(lane == 4 + h, high, stats[r])
                stats[r] = jnp.where(lane == 8 + h, total - high, stats[r])
        for r in range(4):
            outs[r][:, quarter:] = stats[r].astype(BF)

    return pl.pallas_call(
        kernel,
        out_shape=[jax.ShapeDtypeStruct((128, 4 * HEAD), BF)] * 4,
        compiler_params=room(),
        name="attend",
    )(*[in_vmem(a) for a in sets], *[in_vmem(a) for a in queries])


def merged(parts):
    def kernel(*refs):
        ins, outs = refs[:4], refs[4:]
        base = 3 * HEAD
        stats = [r[:, base:].astype(F32) for r in ins]
        for h in range(3):
            tops = [s[:, h : h + 1] for s in stats]
            totals = [s[:, 4 + h : 5 + h] + s[:, 8 + h : 9 + h] for s in stats]
            top = jnp.maximum(jnp.maximum(tops[0], tops[1]), jnp.maximum(tops[2], tops[3]))
            scales = [jnp.exp(t - top) for t in tops]
            total = sum(a * b for a, b in zip(scales, totals))
            cols = slice(h * HEAD, (h + 1) * HEAD)
            summed = sum(r[:, cols].astype(F32) * a for r, a in zip(ins, scales))
            mixed = (summed / total).astype(BF)
            for n in range(4):
                outs[n][:, cols] = mixed[32 * n : 32 * n + 32]

    return pl.pallas_call(
        kernel,
        out_shape=[jax.ShapeDtypeStruct((32, 3 * HEAD), BF)] * 4,
        compiler_params=room(),
        name="merged",
    )(*[in_vmem(a) for a in parts])


def streamed(place, timestep, stream, gate_table, mixed, weight):
    width = weight.shape[1]
    quarter = width // 4

    def kernel(place_ref, step_ref, stream_ref, gate_ref, a_ref, b_ref, c_ref, d_ref, w_ref, out_ref):
        spot = place_ref[2] * 2 + place_ref[0]
        for here in range(4):

            @pl.when(spot == here)
            def _():
                total = jnp.zeros(out_ref.shape, F32)
                for ref, q in zip((a_ref, b_ref, c_ref, d_ref), (here, here ^ 2, here ^ 1, here ^ 3)):
                    total = total + jnp.dot(
                        ref[...], w_ref[q * quarter : (q + 1) * quarter, :], preferred_element_type=F32
                    )
                gate = gate_ref[pl.ds(step_ref[0], 1), :]
                out_ref[...] = (stream_ref[...].astype(F32) + gate * total).astype(BF)

    return pl.pallas_call(
        kernel,
        out_shape=jax.ShapeDtypeStruct(stream.shape, BF),
        in_specs=[scalars(), scalars()] + [pl.BlockSpec()] * 7,
        compiler_params=room(),
        name="streamed",
    )(place, timestep, stream, gate_table, *[in_vmem(a) for a in mixed], weight)


def grad_of_input(place, cot, pieces):
    rows, width = cot.shape
    block = 256
    keys = [k for k, _ in pieces]
    count = len(pieces)

    def kernel(place_ref, cot_ref, *refs):
        ins, (out_ref, buf, weight, sem) = refs[:count], refs[count:]
        zl, y, c, zh, x = (place_ref[n] for n in range(5))

        @pl.when(pl.program_id(0) == 0)
        def _():
            copies = []
            for n, (far, step, other) in enumerate(keys):
                zz = 1 - zl if far else zl
                yy = (y + step) % 4
                cc = 1 - c if other else c
                copies.append(
                    pltpu.make_async_copy(ins[n], buf.at[zz * 8 + yy * 2 + cc], sem.at[n])
                )
                copies[-1].start()
            for copy in copies:
                copy.wait()
            for far in range(2):
                for step in range(4):
                    zz = 1 - zh if far else zh
                    xx = (x + 4 - step) % 4
                    at = 12 * (4 * far + step)
                    for t in range(4):
                        part = [buf[t * 4 + k, at : at + 12, :] for k in range(4)]
                        base = pl.multiple_of(zz * 768 + xx * 192 + t * 48, 16)
                        weight[pl.ds(base, 48), :] = jnp.concatenate(part, axis=0)

        out_ref[...] = lax.dot_general(
            cot_ref[...], weight[...], (((1,), (1,)), ((), ())), preferred_element_type=F32
        ).astype(BF)

    return pl.pallas_call(
        kernel,
        grid=(rows // block,),
        out_shape=jax.ShapeDtypeStruct((rows, width), BF),
        in_specs=[scalars(), pl.BlockSpec((block, width), lambda i: (i, 0))] + [any_spec()] * count,
        out_specs=pl.BlockSpec((block, width), lambda i: (i, 0)),
        scratch_shapes=[
            pltpu.VMEM((16, 96, width), BF),
            pltpu.VMEM((width, width), BF),
            pltpu.SemaphoreType.DMA((count,)),
        ],
        compiler_params=room(28, dimension_semantics=("arbitrary",)),
        name="grad_of_input",
    )(place, cot, *[in_vmem(p) for _, p in pieces])


def joined(arrays):
    rows = [a.shape[0] for a in arrays]

    def kernel(*refs):
        out_ref, at = refs[-1], 0
        for ref, n in zip(refs[:-1], rows):
            out_ref[at : at + n, :] = ref[...]
            at += n

    return pl.pallas_call(
        kernel,
        out_shape=jax.ShapeDtypeStruct((sum(rows), arrays[0].shape[1]), arrays[0].dtype),
        compiler_params=room(),
        name="joined",
    )(in_hbm(arrays[0]), *[in_vmem(a) for a in arrays[1:]])


def weight_pieces(weight):
    on_x = [weight] + [lax.ppermute(weight, "x", turn(k)) for k in (1, 2, 3)]
    on_x = joined(on_x)
    far = lax.ppermute(on_x, "zh", SWAP)
    near = joined([on_x, far])
    far = lax.ppermute(near, "zl", SWAP)
    pieces = {(0, 0): near, (1, 0): far}
    for f in range(2):
        pieces[f, 3] = lax.ppermute(pieces[f, 0], "y", turn(1))
        pieces[f, 1] = lax.ppermute(pieces[f, 0], "y", turn(-1))
    pieces[0, 2] = lax.ppermute(pieces[0, 1], "y", turn(-1))
    pieces[1, 2] = lax.ppermute(pieces[1, 3], "y", turn(1))
    out = [((f, step, 0), p) for (f, step), p in pieces.items()]
    out += [((f, step, 1), lax.ppermute(p, "c", SWAP)) for (f, step), p in pieces.items()]
    return out


def own_queries_of(sets):
    def kernel(*refs):
        for n in range(4):
            refs[4][32 * n : 32 * n + 32, :] = refs[n][256:288, :]

    return pl.pallas_call(
        kernel,
        out_shape=jax.ShapeDtypeStruct((128, 3 * HEAD), BF),
        compiler_params=room(),
        name="own_queries",
    )(*[in_vmem(a) for a in sets])


def product_and_split(place, critic_in, critic_cot, got, factor):
    tokens, width = critic_cot.shape
    half = width // 2

    def kernel(place_ref, in_ref, cot_ref, got_ref, send_l, send_r, keep_l, keep_r):
        x = place_ref[4]
        p = pl.program_id(0)
        result = lax.dot_general(
            in_ref[...], cot_ref[...], (((0,), (0,)), ((), ())), preferred_element_type=F32
        ) * factor + got_ref[...].astype(F32)
        for u in range(2):
            chunk = 2 * p + u
            left = result[192 * u : 192 * u + 192, :half]
            right = result[192 * u : 192 * u + 192, half:]
            kept_l = (chunk == x) | (chunk == 3 - x)
            kept_r = (chunk == x) | (chunk == (x ^ 1))

            @pl.when(kept_l)
            def _():
                keep_l[jnp.where(chunk == x, 0, 1)] = left

            @pl.when(jnp.logical_not(kept_l))
            def _():
                send_l[jnp.where(chunk == (x ^ 1), 0, 1)] = left.astype(BF)

            @pl.when(kept_r)
            def _():
                keep_r[jnp.where(chunk == x, 0, 1)] = right

            @pl.when(jnp.logical_not(kept_r))
            def _():
                send_r[jnp.where(chunk == 3 - x, 0, 1)] = right.astype(BF)

    whole = pl.BlockSpec((2, 192, half), lambda p, place: (0, 0, 0))
    return pl.pallas_call(
        kernel,
        grid_spec=pltpu.PrefetchScalarGridSpec(
            num_scalar_prefetch=1,
            grid=(2,),
            in_specs=[
                pl.BlockSpec((tokens, width // 4), lambda p, place: (0, 2 * place[2] + p)),
                pl.BlockSpec((tokens, width), lambda p, place: (0, 0)),
                pl.BlockSpec((width // 4, width), lambda p, place: (p, 0)),
            ],
            out_specs=[whole] * 4,
        ),
        out_shape=[jax.ShapeDtypeStruct((2, 192, half), BF)] * 2
        + [jax.ShapeDtypeStruct((2, 192, half), F32)] * 2,
        compiler_params=room(40, dimension_semantics=("arbitrary",)),
        name="product_and_split",
    )(place, in_hbm(critic_in), critic_cot, in_vmem(got))


def onward_of(keep_l, keep_r, got_l, got_r):
    def kernel(kl, kr, gl, gr, out_l, out_r):
        out_l[...] = (kl[0] + gl[1].astype(F32)).astype(BF)
        out_r[...] = (kr[0] + gr[1].astype(F32)).astype(BF)

    _, rows, cols = keep_l.shape
    block = pl.BlockSpec((1, rows, cols), lambda i: (1, 0, 0))
    return pl.pallas_call(
        kernel,
        grid=(1,),
        in_specs=[block] * 2 + [pl.BlockSpec(memory_space=pltpu.VMEM)] * 2,
        out_specs=[pl.BlockSpec((rows, cols), lambda i: (0, 0))] * 2,
        out_shape=[jax.ShapeDtypeStruct((rows, cols), BF)] * 2,
        compiler_params=room(),
        name="onward",
    )(keep_l, keep_r, in_vmem(got_l), in_vmem(got_r))


def cut_along_y(place, keep_l, keep_r, got_l, got_r, last_l, last_r):
    half = keep_l.shape[2]

    def kernel(place_ref, kl, kr, gl, gr, ll, lr, own, one, two, three, total):
        total[:, :half] = kl[0] + gl[0].astype(F32) + ll[...].astype(F32)
        total[:, half:] = kr[0] + gr[0].astype(F32) + lr[...].astype(F32)
        y = place_ref[1]
        for k, ref in enumerate((own, one, two, three)):
            at = ((y + k) % 4) * 24
            for z in range(2):
                rows = total[pl.ds(pl.multiple_of(z * 96 + at, 8), 24), :]
                ref[z] = rows.astype(ref.dtype)

    first = pl.BlockSpec((1, 192, half), lambda i: (0, 0, 0))
    out = pl.BlockSpec((2, 24, 2 * half), lambda i: (0, 0, 0))
    return pl.pallas_call(
        kernel,
        grid=(1,),
        in_specs=[scalars()] + [first] * 2 + [pl.BlockSpec(memory_space=pltpu.VMEM)] * 4,
        out_specs=[out] * 4,
        out_shape=[jax.ShapeDtypeStruct((2, 24, 2 * half), F32)]
        + [jax.ShapeDtypeStruct((2, 24, 2 * half), BF)] * 3,
        scratch_shapes=[pltpu.VMEM((192, 2 * half), F32)],
        compiler_params=room(),
        name="cut_along_y",
    )(place, keep_l, keep_r, *[in_vmem(a) for a in (got_l, got_r, last_l, last_r)])


def cut_to_owners(place, own, others):
    width = own.shape[2]

    def kernel(place_ref, own_ref, a, b, d, *outs):
        total = own_ref[...]
        for ref in (a, b, d):
            total = total + ref[...].astype(F32)
        spot = place_ref[0] * 2 + place_ref[3]
        for here in range(4):

            @pl.when(spot == here)
            def _():
                for n in range(4):
                    z, k = (here ^ n) // 2, (here ^ n) % 2
                    outs[n][...] = total[z, 12 * k : 12 * k + 12, :]

    return pl.pallas_call(
        kernel,
        in_specs=[scalars()] + [pl.BlockSpec()] * 4,
        out_shape=[jax.ShapeDtypeStruct((12, width), F32)] * 4,
        compiler_params=room(),
        name="cut_to_owners",
    )(place, own, *[in_vmem(a) for a in others])


def added(arrays):
    def kernel(*refs):
        refs[-1][...] = (refs[0][...] + refs[1][...]) + (refs[2][...] + refs[3][...])

    return pl.pallas_call(
        kernel,
        out_shape=jax.ShapeDtypeStruct(arrays[0].shape, F32),
        compiler_params=room(),
        name="added",
    )(*[in_vmem(a) for a in arrays])


def weight_gradient(place, critic_in, critic_cot, c, factor):
    half = critic_cot.shape[1] // 2
    theirs = lax.dynamic_slice_in_dim(critic_in, (1 - c) * half, half, 1)
    theirs = (
        lax.dot_general(
            theirs, critic_cot, (((0,), (0,)), ((), ())), preferred_element_type=F32
        )
        * factor
    ).astype(BF)
    got = lax.ppermute(theirs, "c", SWAP)
    send_l, send_r, keep_l, keep_r = product_and_split(place, critic_in, critic_cot, got, factor)
    near = [(0, 1), (1, 0), (2, 3), (3, 2)]
    wrap = [(0, 3), (3, 0), (1, 2), (2, 1)]
    got_l = lax.ppermute(send_l, "x", near)
    got_r = lax.ppermute(send_r, "x", wrap)
    on_l, on_r = onward_of(keep_l, keep_r, got_l, got_r)
    last_l = lax.ppermute(on_l, "x", wrap)
    last_r = lax.ppermute(on_r, "x", near)
    own, *others = cut_along_y(place, keep_l, keep_r, got_l, got_r, last_l, last_r)
    others = [lax.ppermute(a, "y", turn(k)) for a, k in zip(others, (1, 2, 3))]
    cuts = cut_to_owners(place, own, others)

    def owner(far_z, far_c):
        spots = [(h, z, k) for h in range(2) for z in range(2) for k in range(2)]
        return [(h * 4 + z * 2 + k, k * 4 + (z ^ far_z) * 2 + (h ^ far_c)) for h, z, k in spots]

    ends = [lax.ppermute(a, ("zh", "zl", "c"), owner(n // 2, n % 2)) for n, a in enumerate(cuts)]
    return added(ends)


def step(
    stream,
    queries,
    new_keys,
    new_values,
    cache_keys,
    cache_values,
    cache_frames,
    group_index,
    timestep,
    gate_table,
    attn_out_weight,
    critic_in,
    critic_cot,
    critic_weight,
):
    zh, x, zl, y, c = (lax.axis_index(a) for a in ("zh", "x", "zl", "y", "c"))
    place = jnp.stack([zl, y, c, zh, x]).astype(jnp.int32)
    near_near, near_far, far_near, far_far = packed(
        place,
        group_index,
        cache_frames,
        (cache_keys[0], new_keys[0], cache_values[0], new_values[0], queries[0]),
    )
    sets = [near_near, lax.ppermute(far_near, "c", SWAP), lax.ppermute(near_far, "zl", SWAP)]
    sets.append(lax.ppermute(lax.ppermute(far_far, "c", SWAP), "zl", SWAP))
    pieces = weight_pieces(critic_weight)

    factor = float(critic_in.shape[0] * 128) ** (-0.5)
    grad_weight = weight_gradient(place, critic_in, critic_cot, c, factor)

    own = own_queries_of(sets)
    all_queries = [own] + [lax.ppermute(own, "y", turn(k)) for k in (1, 2, 3)]
    partial = attend(sets, all_queries)
    parts = [partial[0]] + [lax.ppermute(partial[k], "y", turn(-k)) for k in (1, 2, 3)]
    mixed = merged(parts)
    cross = [(0, 3), (3, 0), (1, 2), (2, 1)]
    mixed = [
        mixed[0],
        lax.ppermute(mixed[1], "c", SWAP),
        lax.ppermute(mixed[2], "zl", SWAP),
        lax.ppermute(mixed[3], ("zl", "c"), cross),
    ]
    stream_out = streamed(place, timestep, stream[0], gate_table, mixed, attn_out_weight)[None]
    grad_in = grad_of_input(place, critic_cot, pieces)
    return (stream_out, grad_in, grad_weight)


def solution(mesh):
    cut = Mesh(mesh.devices.reshape(2, 4, 2, 4, 2), ("zh", "x", "zl", "y", "c"))
    dp, seq = ("zh", "x"), ("zl", "y", "c")
    whole = dp + seq
    return jax.shard_map(
        step,
        mesh=cut,
        in_specs=(
            P(dp, seq, None),
            P(dp, seq, None),
            P(dp, seq, None),
            P(dp, seq, None),
            P(dp, seq, None),
            P(dp, seq, None),
            P(dp, seq),
            P(dp),
            P(dp),
            P(),
            P(),
            P(whole, None),
            P(whole, None),
            P(whole, None),
        ),
        out_specs=(P(dp, seq, None), P(whole, None), P(whole, None)),
        check_vma=False,
    )
```

profile of v0, /device:TPU:1, one launch (start us, length us, event | category | flops | bytes accessed | tf_op | source)
XLA Modules:
  0.0 135.2 jit_solution(13821324773717082488)
XLA Ops:
  0.7 6.6 %multiply_convert_fusion = bf16[768,1536]{1,0:T(8,128)(2,1)} fusion(bf16[1024,1536]{1,0:T(8,128)(2,1)} %cot_ref.3, bf16[1024,1536]{1,0:T(8,128)(2,1)} %in_ref.1, s32[]{:T(128)S(6)} %select_n.3), kind=kOutput, calls=%fused_computation | convolution fusion | flops 2418278400 | bytes 7077892 | tf_op jit(solution)/shard_map/dot_general | solution.py:412
  7.2 1.4 %collective-permute-start.32 = (bf16[768,1536]{1,0:T(8,128)(2,1)}, bf16[768,1536]{1,0:T(8,128)(2,1)}, u32[]{:S(2)}, u32[]{:S(2)}) collective-permute-start(bf16[768,1536]{1,0:T(8,128)(2,1)} %multiply_convert_fusion), channel_id=1, source_target_pairs={{0,1},{1,0},{2,3},{3,2},{4,5},{5,4},{6,7},{7,6},{8,9},{9,8},{10,11... | collective-permute-start | bytes 7077896 | tf_op jit(solution)/shard_map/ppermute | solution.py:417
  9.3 0.1 stack.23.place_ref
  9.4 1.3 packed.1
  10.6 0.1 collective-permute-start.2
  10.7 0.5 collective-permute-start
  11.2 1.7 %collective-permute-start.1 = (bf16[304,384]{1,0:T(8,128)(2,1)S(1)}, bf16[304,384]{1,0:T(8,128)(2,1)S(1)}, u32[]{:S(2)}, u32[]{:S(2)}) collective-permute-start(bf16[304,384]{1,0:T(8,128)(2,1)S(1)} %get-tuple-element.31), channel_id=1, source_target_pairs={{0,8},{8,0},{1,9},{9,1},{2,10},{10,2},{3,11},{11,3},{4,12},{12,4},... | collective-permute-start | bytes 700424 | tf_op jit(solution)/shard_map/ppermute | solution.py:462
  13.0 0.3 collective-permute-done.2
  13.3 1.7 %collective-permute-start.3 = (bf16[304,384]{1,0:T(8,128)(2,1)S(1)}, bf16[304,384]{1,0:T(8,128)(2,1)S(1)}, u32[]{:S(2)}, u32[]{:S(2)}) collective-permute-start(bf16[304,384]{1,0:T(8,128)(2,1)S(1)} %collective-permute-done.2), channel_id=1, source_target_pairs={{0,8},{8,0},{1,9},{9,1},{2,10},{10,2},{3,11},{11,3},{4,12},{12,4},... | collective-permute-start | bytes 700424 | tf_op jit(solution)/shard_map/ppermute | solution.py:463
  15.1 1.2 collective-permute-start.13
  16.3 2.5 %collective-permute-start.14 = (bf16[12,1536]{1,0:T(8,128)(2,1)S(1)}, bf16[12,1536]{1,0:T(8,128)(2,1)S(1)}, u32[]{:S(2)}, u32[]{:S(2)}) collective-permute-start(bf16[12,1536]{1,0:T(8,128)(2,1)S(1)} %copy-done.5), channel_id=1, source_target_pairs={{0,32},{16,48},{32,0},{48,16},{1,33},{17,49},{33,1},{49,17},{2,34}... | collective-permute-start | bytes 110600 | tf_op jit(solution)/shard_map/ppermute | solution.py:243
  18.7 5.3 %product_and_split.1 = (bf16[2,192,768]{2,1,0:T(8,128)(2,1)S(1)}, bf16[2,192,768]{2,1,0:T(8,128)(2,1)S(1)}, f32[2,192,768]{2,1,0:T(8,128)S(1)}, f32[2,192,768]{2,1,0:T(8,128)S(1)}) custom-call(s32[5]{0:T(128)S(1)} %stack.23.place_ref, bf16[1024,1536]{1,0:T(8,128)(2,1)} %in_ref.1, bf16[1024,1536]{1,0:T(8,128)(2,1)S(1)} %copy-done, ...), custom_call_target="tpu_custom_call" | custom-call | tf_op jit(solution)/shard_map/product_and_split/pallas_call | solution.py:306
  24.0 0.1 collective-permute-start.33
  24.1 1.2 collective-permute-start.15
  25.4 13.5 %collective-permute-done.15.refs_3_ = bf16[12,1536]{1,0:T(8,128)(2,1)S(1)} collective-permute-done((bf16[12,1536]{1,0:T(8,128)(2,1)S(1)}, bf16[12,1536]{1,0:T(8,128)(2,1)S(1)}, u32[]{:S(2)}, u32[]{:S(2)}) %collective-permute-start.15) | collective-permute-done | bytes 36896 | tf_op jit(solution)/shard_map/ppermute | solution.py:243
  38.8 0.8 joined.2.refs_0_
  39.7 3.4 %collective-permute-start.16 = (bf16[48,1536]{1,0:T(8,128)(2,1)S(1)}, bf16[48,1536]{1,0:T(8,128)(2,1)S(1)}, u32[]{:S(2)}, u32[]{:S(2)}) collective-permute-start(bf16[48,1536]{1,0:T(8,128)(2,1)S(1)} %joined.2.refs_0_), channel_id=1, source_target_pairs={{0,64},{64,0},{1,65},{65,1},{2,66},{66,2},{3,67},{67,3},{4,68},{68... | collective-permute-start | bytes 442376 | tf_op jit(solution)/shard_map/ppermute | solution.py:245
  43.1 1.4 %collective-permute-start.4 = (bf16[128,384]{1,0:T(8,128)(2,1)S(1)}, bf16[128,384]{1,0:T(8,128)(2,1)S(1)}, u32[]{:S(2)}, u32[]{:S(2)}) collective-permute-start(bf16[128,384]{1,0:T(8,128)(2,1)S(1)} %own_queries.1.refs_4_), channel_id=1, source_target_pairs={{0,2},{2,4},{4,6},{6,0},{1,3},{3,5},{5,7},{7,1},{8,10},{10,12},{12... | collective-permute-start | bytes 294920 | tf_op jit(solution)/shard_map/ppermute | solution.py:470
  44.4 1.2 collective-permute-done.16.refs_1_
  45.6 1.1 joined.3.refs_0_
  46.7 0.2 collective-permute-start.17
  46.9 2.7 %collective-permute-start.19 = (bf16[96,1536]{1,0:T(8,128)(2,1)S(1)}, bf16[96,1536]{1,0:T(8,128)(2,1)S(1)}, u32[]{:S(2)}, u32[]{:S(2)}) collective-permute-start(bf16[96,1536]{1,0:T(8,128)(2,1)S(1)} %joined.3.refs_0_), channel_id=1, source_target_pairs={{0,6},{2,0},{4,2},{6,4},{1,7},{3,1},{5,3},{7,5},{8,14},{10,8},{12,... | collective-permute-start | bytes 884744 | tf_op jit(solution)/shard_map/ppermute | solution.py:251
  49.6 0.3 collective-permute-start.5
  50.0 4.6 %collective-permute-done.5.refs_6_ = bf16[128,384]{1,0:T(8,128)(2,1)S(1)} collective-permute-done((bf16[128,384]{1,0:T(8,128)(2,1)S(1)}, bf16[128,384]{1,0:T(8,128)(2,1)S(1)}, u32[]{:S(2)}, u32[]{:S(2)}) %collective-permute-start.5) | collective-permute-done | bytes 98336 | tf_op jit(solution)/shard_map/ppermute | solution.py:470
  54.6 2.0 %collective-permute-start.6 = (bf16[128,384]{1,0:T(8,128)(2,1)S(1)}, bf16[128,384]{1,0:T(8,128)(2,1)S(1)}, u32[]{:S(2)}, u32[]{:S(2)}) collective-permute-start(bf16[128,384]{1,0:T(8,128)(2,1)S(1)} %own_queries.1.refs_4_), channel_id=1, source_target_pairs={{0,6},{2,0},{4,2},{6,4},{1,7},{3,1},{5,3},{7,5},{8,14},{10,8},{12,... | collective-permute-start | bytes 294920 | tf_op jit(solution)/shard_map/ppermute | solution.py:470
  56.6 2.6 %collective-permute-done.6.refs_7_ = bf16[128,384]{1,0:T(8,128)(2,1)S(1)} collective-permute-done((bf16[128,384]{1,0:T(8,128)(2,1)S(1)}, bf16[128,384]{1,0:T(8,128)(2,1)S(1)}, u32[]{:S(2)}, u32[]{:S(2)}) %collective-permute-start.6) | collective-permute-done | bytes 98336 | tf_op jit(solution)/shard_map/ppermute | solution.py:470
  59.2 3.4 %attend.1 = (bf16[128,512]{1,0:T(8,128)(2,1)S(1)}, bf16[128,512]{1,0:T(8,128)(2,1)S(1)}, bf16[128,512]{1,0:T(8,128)(2,1)S(1)}, bf16[128,512]{1,0:T(8,128)(2,1)S(1)}) custom-call(bf16[304,384]{1,0:T(8,128)(2,1)S(1)} %get-tuple-element.29.refs_0_, bf16[304,384]{1,0:T(8,128)(2,1)S(1)} %collective-permute-done.refs_1_, ...), custom_call_target="tpu_custom_call" | custom-call | tf_op jit(solution)/shard_map/attend/pallas_call | solution.py:112
  62.7 3.5 %collective-permute-start.7 = (bf16[128,512]{1,0:T(8,128)(2,1)S(1)}, bf16[128,512]{1,0:T(8,128)(2,1)S(1)}, u32[]{:S(2)}, u32[]{:S(2)}) collective-permute-start(bf16[128,512]{1,0:T(8,128)(2,1)S(1)} %get-tuple-element.34), channel_id=1, source_target_pairs={{0,6},{2,0},{4,2},{6,4},{1,7},{3,1},{5,3},{7,5},{8,14},{10,8},{12,... | collective-permute-start | bytes 393224 | tf_op jit(solution)/shard_map/ppermute | solution.py:472
  66.1 4.7 %collective-permute-start.24 = (bf16[96,1536]{1,0:T(8,128)(2,1)S(1)}, bf16[96,1536]{1,0:T(8,128)(2,1)S(1)}, u32[]{:S(2)}, u32[]{:S(2)}) collective-permute-start(bf16[96,1536]{1,0:T(8,128)(2,1)S(1)} %joined.3.refs_0_), channel_id=1, source_target_pairs={{0,1},{1,0},{2,3},{3,2},{4,5},{5,4},{6,7},{7,6},{8,9},{9,8},{10,11... | collective-permute-start | bytes 884744 | tf_op jit(solution)/shard_map/ppermute | solution.py:255
  70.8 1.5 %collective-permute-start.8 = (bf16[128,512]{1,0:T(8,128)(2,1)S(1)}, bf16[128,512]{1,0:T(8,128)(2,1)S(1)}, u32[]{:S(2)}, u32[]{:S(2)}) collective-permute-start(bf16[128,512]{1,0:T(8,128)(2,1)S(1)} %get-tuple-element.35), channel_id=1, source_target_pairs={{0,4},{2,6},{4,0},{6,2},{1,5},{3,7},{5,1},{7,3},{8,12},{10,14},{12... | collective-permute-start | bytes 393224 | tf_op jit(solution)/shard_map/ppermute | solution.py:472
  72.3 1.8 %collective-permute-start.9 = (bf16[128,512]{1,0:T(8,128)(2,1)S(1)}, bf16[128,512]{1,0:T(8,128)(2,1)S(1)}, u32[]{:S(2)}, u32[]{:S(2)}) collective-permute-start(bf16[128,512]{1,0:T(8,128)(2,1)S(1)} %get-tuple-element.36), channel_id=1, source_target_pairs={{0,2},{2,4},{4,6},{6,0},{1,3},{3,5},{5,7},{7,1},{8,10},{10,12},{12... | collective-permute-start | bytes 393224 | tf_op jit(solution)/shard_map/ppermute | solution.py:472
  74.1 0.1 collective-permute-start.20
  74.2 0.1 onward.1
  74.3 3.2 %collective-permute-done.8.refs_2_ = bf16[128,512]{1,0:T(8,128)(2,1)S(1)} collective-permute-done((bf16[128,512]{1,0:T(8,128)(2,1)S(1)}, bf16[128,512]{1,0:T(8,128)(2,1)S(1)}, u32[]{:S(2)}, u32[]{:S(2)}) %collective-permute-start.8) | collective-permute-done | bytes 131104 | tf_op jit(solution)/shard_map/ppermute | solution.py:472
  77.5 3.3 %collective-permute-start.35 = (bf16[192,768]{1,0:T(8,128)(2,1)S(1)}, bf16[192,768]{1,0:T(8,128)(2,1)S(1)}, u32[]{:S(2)}, u32[]{:S(2)}) collective-permute-start(bf16[192,768]{1,0:T(8,128)(2,1)S(1)} %get-tuple-element.45), channel_id=1, source_target_pairs={{0,48},{48,0},{16,32},{32,16},{1,49},{49,1},{17,33},{33,17},{2,50}... | collective-permute-start | bytes 884744 | tf_op jit(solution)/shard_map/ppermute | solution.py:424
  80.9 0.4 collective-permute-done.9.refs_3_
  81.3 0.8 collective-permute-start.36
  82.1 0.5 merged.1
  82.5 5.9 %collective-permute-start.10 = (bf16[32,384]{1,0:T(8,128)(2,1)S(1)}, bf16[32,384]{1,0:T(8,128)(2,1)S(1)}, u32[]{:S(2)}, u32[]{:S(2)}) collective-permute-start(bf16[32,384]{1,0:T(8,128)(2,1)S(1)} %get-tuple-element.38), channel_id=1, source_target_pairs={{0,1},{1,0},{2,3},{3,2},{4,5},{5,4},{6,7},{7,6},{8,9},{9,8},{10,11... | collective-permute-start | bytes 73736 | tf_op jit(solution)/shard_map/ppermute | solution.py:477
  88.4 1.6 %collective-permute-start.11 = (bf16[32,384]{1,0:T(8,128)(2,1)S(1)}, bf16[32,384]{1,0:T(8,128)(2,1)S(1)}, u32[]{:S(2)}, u32[]{:S(2)}) collective-permute-start(bf16[32,384]{1,0:T(8,128)(2,1)S(1)} %get-tuple-element.39), channel_id=1, source_target_pairs={{0,8},{8,0},{1,9},{9,1},{2,10},{10,2},{3,11},{11,3},{4,12},{12,4},... | collective-permute-start | bytes 73736 | tf_op jit(solution)/shard_map/ppermute | solution.py:478
  90.1 1.1 collective-permute-start.12
  91.1 0.4 collective-permute-done.11.c_ref
  91.6 1.7 %collective-permute-done.12.d_ref = bf16[32,384]{1,0:T(8,128)(2,1)S(1)} collective-permute-done((bf16[32,384]{1,0:T(8,128)(2,1)S(1)}, bf16[32,384]{1,0:T(8,128)(2,1)S(1)}, u32[]{:S(2)}, u32[]{:S(2)}) %collective-permute-start.12) | collective-permute-done | bytes 24608 | tf_op jit(solution)/shard_map/ppermute | solution.py:479
  93.3 0.4 collective-permute-start.25
  93.7 0.1 collective-permute-start.27
  93.8 1.7 %collective-permute-start.23 = (bf16[96,1536]{1,0:T(8,128)(2,1)S(1)}, bf16[96,1536]{1,0:T(8,128)(2,1)S(1)}, u32[]{:S(2)}, u32[]{:S(2)}) collective-permute-start(bf16[96,1536]{1,0:T(8,128)(2,1)S(1)} %collective-permute-done.20.refs_4_), channel_id=1, source_target_pairs={{0,2},{2,4},{4,6},{6,0},{1,3},{3,5},{5,7},{7,1},{8,10},{10,12},{12... | collective-permute-start | bytes 884744 | tf_op jit(solution)/shard_map/ppermute | solution.py:253
  95.5 0.8 cut_along_y.1
  96.4 2.9 %collective-permute-done.21.refs_5_ = bf16[96,1536]{1,0:T(8,128)(2,1)S(1)} collective-permute-done((bf16[96,1536]{1,0:T(8,128)(2,1)S(1)}, bf16[96,1536]{1,0:T(8,128)(2,1)S(1)}, u32[]{:S(2)}, u32[]{:S(2)}) %collective-permute-start.21) | collective-permute-done | bytes 294944 | tf_op jit(solution)/shard_map/ppermute | solution.py:251
  99.3 6.3 %collective-permute-done.22.refs_6_ = bf16[96,1536]{1,0:T(8,128)(2,1)S(1)} collective-permute-done((bf16[96,1536]{1,0:T(8,128)(2,1)S(1)}, bf16[96,1536]{1,0:T(8,128)(2,1)S(1)}, u32[]{:S(2)}, u32[]{:S(2)}) %collective-permute-start.22) | collective-permute-done | bytes 294944 | tf_op jit(solution)/shard_map/ppermute | solution.py:252
  105.6 1.7 %collective-permute-start.39 = (bf16[2,24,1536]{2,1,0:T(8,128)(2,1)S(1)}, bf16[2,24,1536]{2,1,0:T(8,128)(2,1)S(1)}, u32[]{:S(2)}, u32[]{:S(2)}) collective-permute-start(bf16[2,24,1536]{2,1,0:T(8,128)(2,1)S(1)} %get-tuple-element.50), channel_id=1, source_target_pairs={{0,6},{2,0},{4,2},{6,4},{1,7},{3,1},{5,3},{7,5},{8,14},{10,8},{12,... | collective-permute-start | bytes 442376 | tf_op jit(solution)/shard_map/ppermute | solution.py:427
  107.3 2.2 %collective-permute-start.26 = (bf16[96,1536]{1,0:T(8,128)(2,1)S(1)}, bf16[96,1536]{1,0:T(8,128)(2,1)S(1)}, u32[]{:S(2)}, u32[]{:S(2)}) collective-permute-start(bf16[96,1536]{1,0:T(8,128)(2,1)S(1)} %collective-permute-done.18.refs_2_), channel_id=1, source_target_pairs={{0,1},{1,0},{2,3},{3,2},{4,5},{5,4},{6,7},{7,6},{8,9},{9,8},{10,11... | collective-permute-start | bytes 884744 | tf_op jit(solution)/shard_map/ppermute | solution.py:255
  109.5 0.1 collective-permute-start.28
  109.6 0.4 collective-permute-start.29
  110.1 1.1 collective-permute-done.38.b
  111.1 2.8 %collective-permute-start.30 = (bf16[96,1536]{1,0:T(8,128)(2,1)S(1)}, bf16[96,1536]{1,0:T(8,128)(2,1)S(1)}, u32[]{:S(2)}, u32[]{:S(2)}) collective-permute-start(bf16[96,1536]{1,0:T(8,128)(2,1)S(1)} %collective-permute-done.22.refs_6_), channel_id=1, source_target_pairs={{0,1},{1,0},{2,3},{3,2},{4,5},{5,4},{6,7},{7,6},{8,9},{9,8},{10,11... | collective-permute-start | bytes 884744 | tf_op jit(solution)/shard_map/ppermute | solution.py:255
  114.0 1.8 %collective-permute-start.31 = (bf16[96,1536]{1,0:T(8,128)(2,1)S(1)}, bf16[96,1536]{1,0:T(8,128)(2,1)S(1)}, u32[]{:S(2)}, u32[]{:S(2)}) collective-permute-start(bf16[96,1536]{1,0:T(8,128)(2,1)S(1)} %collective-permute-done.23.refs_7_), channel_id=1, source_target_pairs={{0,1},{1,0},{2,3},{3,2},{4,5},{5,4},{6,7},{7,6},{8,9},{9,8},{10,11... | collective-permute-start | bytes 884744 | tf_op jit(solution)/shard_map/ppermute | solution.py:255
  115.7 0.6 cut_to_owners.1
  116.4 5.4 %collective-permute-start.40 = (f32[12,1536]{1,0:T(8,128)S(1)}, f32[12,1536]{1,0:T(8,128)S(1)}, u32[]{:S(2)}, u32[]{:S(2)}) collective-permute-start(f32[12,1536]{1,0:T(8,128)S(1)} %get-tuple-element.51), channel_id=1, source_target_pairs={{0,0},{1,64},{8,8},{9,72},{64,1},{65,65},{72,9},{73,73},{2,2},{3,6... | collective-permute-start | bytes 221192 | tf_op jit(solution)/shard_map/ppermute | solution.py:434
  121.8 0.1 collective-permute-start.41
  121.9 0.6 collective-permute-start.42
  122.5 0.1 collective-permute-start.43
  123.3 2.1 %streamed.1 = bf16[32,1536]{1,0:T(8,128)(2,1)} custom-call(s32[5]{0:T(128)S(1)} %stack.23.place_ref, s32[1]{0:T(128)S(6)} %copy.18.step_ref, bf16[32,1536]{1,0:T(8,128)(2,1)S(1)} %bitcast.15, f32[4,1536]{1,0:T(4,128)S(1)} %copy-done.3, bf16[32,384]{1,0:T(8,128)(2,1)S(1)} %get-tuple-element.37.a_ref, bf16[32,384]{1,0:T(8,128)(2,1)S(1)} %collective-permute-done.10.b_ref, ...), custom_call_target="tpu_custom_call" | custom-call | tf_op jit(solution)/shard_map/streamed/pallas_call | solution.py:163
  125.4 9.0 %grad_of_input.1 = bf16[1024,1536]{1,0:T(8,128)(2,1)} custom-call(s32[5]{0:T(128)S(1)} %stack.23.place_ref, bf16[1024,1536]{1,0:T(8,128)(2,1)S(1)} %copy-done, bf16[96,1536]{1,0:T(8,128)(2,1)S(1)} %joined.3.refs_0_, bf16[96,1536]{1,0:T(8,128)(2,1)S(1)} %collective-permute-done.17.refs_1_, bf16[96,1536]{1,0:T(8,128)(2,1)S(1)} %collective-permute-done.18.refs_2_, ...), custom_call_target="tpu_custom_call" | custom-call | tf_op jit(solution)/shard_map/grad_of_input/pallas_call | solution.py:209
  134.5 0.7 added.1
  (56 shorter events, 0.2 us)
Async XLA Ops:
  0.6 8.7 %copy-start.4 = (s32[1,96]{1,0:T(1,128)S(1)}, s32[1,96]{1,0:T(1,128)}, u32[]{:S(2)}) copy-start(s32[1,96]{1,0:T(1,128)} %frames_ref.1) | copy-start | bytes 1156
  0.6 14.4 %copy-start.5 = (bf16[12,1536]{1,0:T(8,128)(2,1)S(1)}, bf16[12,1536]{1,0:T(8,128)(2,1)}, u32[]{:S(2)}) copy-start(bf16[12,1536]{1,0:T(8,128)(2,1)} %refs_0_.1) | copy-start | bytes 110596
  0.7 18.1 %copy-start = (bf16[1024,1536]{1,0:T(8,128)(2,1)S(1)}, bf16[1024,1536]{1,0:T(8,128)(2,1)}, u32[]{:S(2)}) copy-start(bf16[1024,1536]{1,0:T(8,128)(2,1)} %cot_ref.3) | copy-start | bytes 9437188
  7.2 9.1 %collective-permute-start.32 = (bf16[768,1536]{1,0:T(8,128)(2,1)}, bf16[768,1536]{1,0:T(8,128)(2,1)}, u32[]{:S(2)}, u32[]{:S(2)}) collective-permute-start(bf16[768,1536]{1,0:T(8,128)(2,1)} %multiply_convert_fusion), channel_id=1, source_target_pairs={{0,1},{1,0},{2,3},{3,2},{4,5},{5,4},{6,7},{7,6},{8,9},{9,8},{10,11... | collective-permute-start | bytes 7077896 | tf_op jit(solution)/shard_map/ppermute | solution.py:417
  10.6 2.7 %collective-permute-start.2 = (bf16[304,384]{1,0:T(8,128)(2,1)S(1)}, bf16[304,384]{1,0:T(8,128)(2,1)S(1)}, u32[]{:S(2)}, u32[]{:S(2)}) collective-permute-start(bf16[304,384]{1,0:T(8,128)(2,1)S(1)} %get-tuple-element.32), channel_id=1, source_target_pairs={{0,1},{1,0},{2,3},{3,2},{4,5},{5,4},{6,7},{7,6},{8,9},{9,8},{10,11... | collective-permute-start | bytes 700424 | tf_op jit(solution)/shard_map/ppermute | solution.py:463
  10.7 28.9 %collective-permute-start = (bf16[304,384]{1,0:T(8,128)(2,1)S(1)}, bf16[304,384]{1,0:T(8,128)(2,1)S(1)}, u32[]{:S(2)}, u32[]{:S(2)}) collective-permute-start(bf16[304,384]{1,0:T(8,128)(2,1)S(1)} %get-tuple-element.30), channel_id=1, source_target_pairs={{0,1},{1,0},{2,3},{3,2},{4,5},{5,4},{6,7},{7,6},{8,9},{9,8},{10,11... | collective-permute-start | bytes 700424 | tf_op jit(solution)/shard_map/ppermute | solution.py:462
  11.2 31.8 %collective-permute-start.1 = (bf16[304,384]{1,0:T(8,128)(2,1)S(1)}, bf16[304,384]{1,0:T(8,128)(2,1)S(1)}, u32[]{:S(2)}, u32[]{:S(2)}) collective-permute-start(bf16[304,384]{1,0:T(8,128)(2,1)S(1)} %get-tuple-element.31), channel_id=1, source_target_pairs={{0,8},{8,0},{1,9},{9,1},{2,10},{10,2},{3,11},{11,3},{4,12},{12,4},... | collective-permute-start | bytes 700424 | tf_op jit(solution)/shard_map/ppermute | solution.py:462
  13.3 29.8 %collective-permute-start.3 = (bf16[304,384]{1,0:T(8,128)(2,1)S(1)}, bf16[304,384]{1,0:T(8,128)(2,1)S(1)}, u32[]{:S(2)}, u32[]{:S(2)}) collective-permute-start(bf16[304,384]{1,0:T(8,128)(2,1)S(1)} %collective-permute-done.2), channel_id=1, source_target_pairs={{0,8},{8,0},{1,9},{9,1},{2,10},{10,2},{3,11},{11,3},{4,12},{12,4},... | collective-permute-start | bytes 700424 | tf_op jit(solution)/shard_map/ppermute | solution.py:463
  15.1 8.9 %collective-permute-start.13 = (bf16[12,1536]{1,0:T(8,128)(2,1)S(1)}, bf16[12,1536]{1,0:T(8,128)(2,1)S(1)}, u32[]{:S(2)}, u32[]{:S(2)}) collective-permute-start(bf16[12,1536]{1,0:T(8,128)(2,1)S(1)} %copy-done.5), channel_id=1, source_target_pairs={{0,16},{16,32},{32,48},{48,0},{1,17},{17,33},{33,49},{49,1},{2,18}... | collective-permute-start | bytes 110600 | tf_op jit(solution)/shard_map/ppermute | solution.py:243
  16.3 7.8 %collective-permute-start.14 = (bf16[12,1536]{1,0:T(8,128)(2,1)S(1)}, bf16[12,1536]{1,0:T(8,128)(2,1)S(1)}, u32[]{:S(2)}, u32[]{:S(2)}) collective-permute-start(bf16[12,1536]{1,0:T(8,128)(2,1)S(1)} %copy-done.5), channel_id=1, source_target_pairs={{0,32},{16,48},{32,0},{48,16},{1,33},{17,49},{33,1},{49,17},{2,34}... | collective-permute-start | bytes 110600 | tf_op jit(solution)/shard_map/ppermute | solution.py:243
  24.0 48.3 %collective-permute-start.33 = (bf16[2,192,768]{2,1,0:T(8,128)(2,1)S(1)}, bf16[2,192,768]{2,1,0:T(8,128)(2,1)S(1)}, u32[]{:S(2)}, u32[]{:S(2)}) collective-permute-start(bf16[2,192,768]{2,1,0:T(8,128)(2,1)S(1)} %get-tuple-element.43), channel_id=1, source_target_pairs={{0,16},{16,0},{32,48},{48,32},{1,17},{17,1},{33,49},{49,33},{2,18}... | collective-permute-start | bytes 1769480 | tf_op jit(solution)/shard_map/ppermute | solution.py:421
  24.1 14.7 %collective-permute-start.15 = (bf16[12,1536]{1,0:T(8,128)(2,1)S(1)}, bf16[12,1536]{1,0:T(8,128)(2,1)S(1)}, u32[]{:S(2)}, u32[]{:S(2)}) collective-permute-start(bf16[12,1536]{1,0:T(8,128)(2,1)S(1)} %copy-done.5), channel_id=1, source_target_pairs={{0,48},{16,0},{32,16},{48,32},{1,49},{17,1},{33,17},{49,33},{2,50}... | collective-permute-start | bytes 110600 | tf_op jit(solution)/shard_map/ppermute | solution.py:243
  38.8 35.3 %collective-permute-start.34 = (bf16[2,192,768]{2,1,0:T(8,128)(2,1)S(1)}, bf16[2,192,768]{2,1,0:T(8,128)(2,1)S(1)}, u32[]{:S(2)}, u32[]{:S(2)}) collective-permute-start(bf16[2,192,768]{2,1,0:T(8,128)(2,1)S(1)} %get-tuple-element.44), channel_id=1, source_target_pairs={{0,48},{48,0},{16,32},{32,16},{1,49},{49,1},{17,33},{33,17},{2,50}... | collective-permute-start | bytes 1769480 | tf_op jit(solution)/shard_map/ppermute | solution.py:422
  39.7 6.0 %copy-start.1 = (bf16[48,1536]{1,0:T(8,128)(2,1)}, bf16[48,1536]{1,0:T(8,128)(2,1)S(1)}, u32[]{:S(2)}) copy-start(bf16[48,1536]{1,0:T(8,128)(2,1)S(1)} %joined.2.refs_0_) | copy-start | bytes 442372
  39.7 5.9 %collective-permute-start.16 = (bf16[48,1536]{1,0:T(8,128)(2,1)S(1)}, bf16[48,1536]{1,0:T(8,128)(2,1)S(1)}, u32[]{:S(2)}, u32[]{:S(2)}) collective-permute-start(bf16[48,1536]{1,0:T(8,128)(2,1)S(1)} %joined.2.refs_0_), channel_id=1, source_target_pairs={{0,64},{64,0},{1,65},{65,1},{2,66},{66,2},{3,67},{67,3},{4,68},{68... | collective-permute-start | bytes 442376 | tf_op jit(solution)/shard_map/ppermute | solution.py:245
  43.1 6.5 %collective-permute-start.4 = (bf16[128,384]{1,0:T(8,128)(2,1)S(1)}, bf16[128,384]{1,0:T(8,128)(2,1)S(1)}, u32[]{:S(2)}, u32[]{:S(2)}) collective-permute-start(bf16[128,384]{1,0:T(8,128)(2,1)S(1)} %own_queries.1.refs_4_), channel_id=1, source_target_pairs={{0,2},{2,4},{4,6},{6,0},{1,3},{3,5},{5,7},{7,1},{8,10},{10,12},{12... | collective-permute-start | bytes 294920 | tf_op jit(solution)/shard_map/ppermute | solution.py:470
  45.6 77.6 %slice-start = ((s8[4718592]{0:T(1024)(128)(4,1)}), s8[4194304]{0:T(1024)(128)(4,1)S(1)}, s32[]{:S(2)}) async-start(s8[4718592]{0:T(1024)(128)(4,1)} %bitcast.13), calls=%async_computation | async-start | bytes 8388608
  46.7 19.4 %collective-permute-start.17 = (bf16[96,1536]{1,0:T(8,128)(2,1)S(1)}, bf16[96,1536]{1,0:T(8,128)(2,1)S(1)}, u32[]{:S(2)}, u32[]{:S(2)}) collective-permute-start(bf16[96,1536]{1,0:T(8,128)(2,1)S(1)} %joined.3.refs_0_), channel_id=1, source_target_pairs={{0,8},{8,0},{1,9},{9,1},{2,10},{10,2},{3,11},{11,3},{4,12},{12,4},... | collective-permute-start | bytes 884744 | tf_op jit(solution)/shard_map/ppermute | solution.py:247
  46.9 19.2 %collective-permute-start.19 = (bf16[96,1536]{1,0:T(8,128)(2,1)S(1)}, bf16[96,1536]{1,0:T(8,128)(2,1)S(1)}, u32[]{:S(2)}, u32[]{:S(2)}) collective-permute-start(bf16[96,1536]{1,0:T(8,128)(2,1)S(1)} %joined.3.refs_0_), channel_id=1, source_target_pairs={{0,6},{2,0},{4,2},{6,4},{1,7},{3,1},{5,3},{7,5},{8,14},{10,8},{12,... | collective-permute-start | bytes 884744 | tf_op jit(solution)/shard_map/ppermute | solution.py:251
  49.6 5.0 %collective-permute-start.5 = (bf16[128,384]{1,0:T(8,128)(2,1)S(1)}, bf16[128,384]{1,0:T(8,128)(2,1)S(1)}, u32[]{:S(2)}, u32[]{:S(2)}) collective-permute-start(bf16[128,384]{1,0:T(8,128)(2,1)S(1)} %own_queries.1.refs_4_), channel_id=1, source_target_pairs={{0,4},{2,6},{4,0},{6,2},{1,5},{3,7},{5,1},{7,3},{8,12},{10,14},{12... | collective-permute-start | bytes 294920 | tf_op jit(solution)/shard_map/ppermute | solution.py:470
  54.6 4.6 %collective-permute-start.6 = (bf16[128,384]{1,0:T(8,128)(2,1)S(1)}, bf16[128,384]{1,0:T(8,128)(2,1)S(1)}, u32[]{:S(2)}, u32[]{:S(2)}) collective-permute-start(bf16[128,384]{1,0:T(8,128)(2,1)S(1)} %own_queries.1.refs_4_), channel_id=1, source_target_pairs={{0,6},{2,0},{4,2},{6,4},{1,7},{3,1},{5,3},{7,5},{8,14},{10,8},{12,... | collective-permute-start | bytes 294920 | tf_op jit(solution)/shard_map/ppermute | solution.py:470
  62.7 8.2 %collective-permute-start.7 = (bf16[128,512]{1,0:T(8,128)(2,1)S(1)}, bf16[128,512]{1,0:T(8,128)(2,1)S(1)}, u32[]{:S(2)}, u32[]{:S(2)}) collective-permute-start(bf16[128,512]{1,0:T(8,128)(2,1)S(1)} %get-tuple-element.34), channel_id=1, source_target_pairs={{0,6},{2,0},{4,2},{6,4},{1,7},{3,1},{5,3},{7,5},{8,14},{10,8},{12,... | collective-permute-start | bytes 393224 | tf_op jit(solution)/shard_map/ppermute | solution.py:472
  66.1 16.4 %collective-permute-start.18 = (bf16[96,1536]{1,0:T(8,128)(2,1)S(1)}, bf16[96,1536]{1,0:T(8,128)(2,1)S(1)}, u32[]{:S(2)}, u32[]{:S(2)}) collective-permute-start(bf16[96,1536]{1,0:T(8,128)(2,1)S(1)} %joined.3.refs_0_), channel_id=1, source_target_pairs={{0,2},{2,4},{4,6},{6,0},{1,3},{3,5},{5,7},{7,1},{8,10},{10,12},{12... | collective-permute-start | bytes 884744 | tf_op jit(solution)/shard_map/ppermute | solution.py:250
  66.1 22.3 %collective-permute-start.24 = (bf16[96,1536]{1,0:T(8,128)(2,1)S(1)}, bf16[96,1536]{1,0:T(8,128)(2,1)S(1)}, u32[]{:S(2)}, u32[]{:S(2)}) collective-permute-start(bf16[96,1536]{1,0:T(8,128)(2,1)S(1)} %joined.3.refs_0_), channel_id=1, source_target_pairs={{0,1},{1,0},{2,3},{3,2},{4,5},{5,4},{6,7},{7,6},{8,9},{9,8},{10,11... | collective-permute-start | bytes 884744 | tf_op jit(solution)/shard_map/ppermute | solution.py:255
  70.8 6.7 %collective-permute-start.8 = (bf16[128,512]{1,0:T(8,128)(2,1)S(1)}, bf16[128,512]{1,0:T(8,128)(2,1)S(1)}, u32[]{:S(2)}, u32[]{:S(2)}) collective-permute-start(bf16[128,512]{1,0:T(8,128)(2,1)S(1)} %get-tuple-element.35), channel_id=1, source_target_pairs={{0,4},{2,6},{4,0},{6,2},{1,5},{3,7},{5,1},{7,3},{8,12},{10,14},{12... | collective-permute-start | bytes 393224 | tf_op jit(solution)/shard_map/ppermute | solution.py:472
  72.3 8.9 %collective-permute-start.9 = (bf16[128,512]{1,0:T(8,128)(2,1)S(1)}, bf16[128,512]{1,0:T(8,128)(2,1)S(1)}, u32[]{:S(2)}, u32[]{:S(2)}) collective-permute-start(bf16[128,512]{1,0:T(8,128)(2,1)S(1)} %get-tuple-element.36), channel_id=1, source_target_pairs={{0,2},{2,4},{4,6},{6,0},{1,3},{3,5},{5,7},{7,1},{8,10},{10,12},{12... | collective-permute-start | bytes 393224 | tf_op jit(solution)/shard_map/ppermute | solution.py:472
  74.1 19.2 %collective-permute-start.20 = (bf16[96,1536]{1,0:T(8,128)(2,1)S(1)}, bf16[96,1536]{1,0:T(8,128)(2,1)S(1)}, u32[]{:S(2)}, u32[]{:S(2)}) collective-permute-start(bf16[96,1536]{1,0:T(8,128)(2,1)S(1)} %collective-permute-done.17.refs_1_), channel_id=1, source_target_pairs={{0,2},{2,4},{4,6},{6,0},{1,3},{3,5},{5,7},{7,1},{8,10},{10,12},{12... | collective-permute-start | bytes 884744 | tf_op jit(solution)/shard_map/ppermute | solution.py:250
  74.2 49.1 %slice-start.1 = ((s8[4718592]{0:T(1024)(128)(4,1)}), s8[524288]{0:T(1024)(128)(4,1)S(1)}, s32[]{:S(2)}) async-start(s8[4718592]{0:T(1024)(128)(4,1)} %bitcast.13), calls=%async_computation.1 | async-start | bytes 1048576
  74.3 49.0 %copy-start.2 = (bf16[1,32,1536]{2,1,0:T(8,128)(2,1)S(1)}, bf16[1,32,1536]{2,1,0:T(8,128)(2,1)}, u32[]{:S(2)}) copy-start(bf16[1,32,1536]{2,1,0:T(8,128)(2,1)} %param.14) | copy-start | bytes 294916
  74.3 49.0 %copy-start.3 = (f32[4,1536]{1,0:T(4,128)S(1)}, f32[4,1536]{1,0:T(4,128)}, u32[]{:S(2)}) copy-start(f32[4,1536]{1,0:T(4,128)} %gate_ref.1) | copy-start | bytes 73732
  77.5 16.2 %collective-permute-start.35 = (bf16[192,768]{1,0:T(8,128)(2,1)S(1)}, bf16[192,768]{1,0:T(8,128)(2,1)S(1)}, u32[]{:S(2)}, u32[]{:S(2)}) collective-permute-start(bf16[192,768]{1,0:T(8,128)(2,1)S(1)} %get-tuple-element.45), channel_id=1, source_target_pairs={{0,48},{48,0},{16,32},{32,16},{1,49},{49,1},{17,33},{33,17},{2,50}... | collective-permute-start | bytes 884744 | tf_op jit(solution)/shard_map/ppermute | solution.py:424
  81.3 12.6 %collective-permute-start.36 = (bf16[192,768]{1,0:T(8,128)(2,1)S(1)}, bf16[192,768]{1,0:T(8,128)(2,1)S(1)}, u32[]{:S(2)}, u32[]{:S(2)}) collective-permute-start(bf16[192,768]{1,0:T(8,128)(2,1)S(1)} %get-tuple-element.46), channel_id=1, source_target_pairs={{0,16},{16,0},{32,48},{48,32},{1,17},{17,1},{33,49},{49,33},{2,18}... | collective-permute-start | bytes 884744 | tf_op jit(solution)/shard_map/ppermute | solution.py:425
  82.5 7.5 %collective-permute-start.10 = (bf16[32,384]{1,0:T(8,128)(2,1)S(1)}, bf16[32,384]{1,0:T(8,128)(2,1)S(1)}, u32[]{:S(2)}, u32[]{:S(2)}) collective-permute-start(bf16[32,384]{1,0:T(8,128)(2,1)S(1)} %get-tuple-element.38), channel_id=1, source_target_pairs={{0,1},{1,0},{2,3},{3,2},{4,5},{5,4},{6,7},{7,6},{8,9},{9,8},{10,11... | collective-permute-start | bytes 73736 | tf_op jit(solution)/shard_map/ppermute | solution.py:477
  88.4 3.1 %collective-permute-start.11 = (bf16[32,384]{1,0:T(8,128)(2,1)S(1)}, bf16[32,384]{1,0:T(8,128)(2,1)S(1)}, u32[]{:S(2)}, u32[]{:S(2)}) collective-permute-start(bf16[32,384]{1,0:T(8,128)(2,1)S(1)} %get-tuple-element.39), channel_id=1, source_target_pairs={{0,8},{8,0},{1,9},{9,1},{2,10},{10,2},{3,11},{11,3},{4,12},{12,4},... | collective-permute-start | bytes 73736 | tf_op jit(solution)/shard_map/ppermute | solution.py:478
  90.1 3.3 %collective-permute-start.12 = (bf16[32,384]{1,0:T(8,128)(2,1)S(1)}, bf16[32,384]{1,0:T(8,128)(2,1)S(1)}, u32[]{:S(2)}, u32[]{:S(2)}) collective-permute-start(bf16[32,384]{1,0:T(8,128)(2,1)S(1)} %get-tuple-element.40), channel_id=1, source_target_pairs={{0,9},{9,0},{1,8},{8,1},{2,11},{11,2},{3,10},{10,3},{4,13},{13,4},... | collective-permute-start | bytes 73736 | tf_op jit(solution)/shard_map/ppermute | solution.py:479
  91.6 7.8 %collective-permute-start.21 = (bf16[96,1536]{1,0:T(8,128)(2,1)S(1)}, bf16[96,1536]{1,0:T(8,128)(2,1)S(1)}, u32[]{:S(2)}, u32[]{:S(2)}) collective-permute-start(bf16[96,1536]{1,0:T(8,128)(2,1)S(1)} %collective-permute-done.17.refs_1_), channel_id=1, source_target_pairs={{0,6},{2,0},{4,2},{6,4},{1,7},{3,1},{5,3},{7,5},{8,14},{10,8},{12,... | collective-permute-start | bytes 884744 | tf_op jit(solution)/shard_map/ppermute | solution.py:251
  93.3 12.3 %collective-permute-start.22 = (bf16[96,1536]{1,0:T(8,128)(2,1)S(1)}, bf16[96,1536]{1,0:T(8,128)(2,1)S(1)}, u32[]{:S(2)}, u32[]{:S(2)}) collective-permute-start(bf16[96,1536]{1,0:T(8,128)(2,1)S(1)} %collective-permute-done.19.refs_3_), channel_id=1, source_target_pairs={{0,6},{2,0},{4,2},{6,4},{1,7},{3,1},{5,3},{7,5},{8,14},{10,8},{12,... | collective-permute-start | bytes 884744 | tf_op jit(solution)/shard_map/ppermute | solution.py:252
  93.3 12.3 %collective-permute-start.25 = (bf16[96,1536]{1,0:T(8,128)(2,1)S(1)}, bf16[96,1536]{1,0:T(8,128)(2,1)S(1)}, u32[]{:S(2)}, u32[]{:S(2)}) collective-permute-start(bf16[96,1536]{1,0:T(8,128)(2,1)S(1)} %collective-permute-done.17.refs_1_), channel_id=1, source_target_pairs={{0,1},{1,0},{2,3},{3,2},{4,5},{5,4},{6,7},{7,6},{8,9},{9,8},{10,11... | collective-permute-start | bytes 884744 | tf_op jit(solution)/shard_map/ppermute | solution.py:255
  93.7 13.6 %collective-permute-start.27 = (bf16[96,1536]{1,0:T(8,128)(2,1)S(1)}, bf16[96,1536]{1,0:T(8,128)(2,1)S(1)}, u32[]{:S(2)}, u32[]{:S(2)}) collective-permute-start(bf16[96,1536]{1,0:T(8,128)(2,1)S(1)} %collective-permute-done.19.refs_3_), channel_id=1, source_target_pairs={{0,1},{1,0},{2,3},{3,2},{4,5},{5,4},{6,7},{7,6},{8,9},{9,8},{10,11... | collective-permute-start | bytes 884744 | tf_op jit(solution)/shard_map/ppermute | solution.py:255
  93.8 15.7 %collective-permute-start.23 = (bf16[96,1536]{1,0:T(8,128)(2,1)S(1)}, bf16[96,1536]{1,0:T(8,128)(2,1)S(1)}, u32[]{:S(2)}, u32[]{:S(2)}) collective-permute-start(bf16[96,1536]{1,0:T(8,128)(2,1)S(1)} %collective-permute-done.20.refs_4_), channel_id=1, source_target_pairs={{0,2},{2,4},{4,6},{6,0},{1,3},{3,5},{5,7},{7,1},{8,10},{10,12},{12... | collective-permute-start | bytes 884744 | tf_op jit(solution)/shard_map/ppermute | solution.py:253
  99.3 10.3 %collective-permute-start.37 = (bf16[2,24,1536]{2,1,0:T(8,128)(2,1)S(1)}, bf16[2,24,1536]{2,1,0:T(8,128)(2,1)S(1)}, u32[]{:S(2)}, u32[]{:S(2)}) collective-permute-start(bf16[2,24,1536]{2,1,0:T(8,128)(2,1)S(1)} %get-tuple-element.48), channel_id=1, source_target_pairs={{0,2},{2,4},{4,6},{6,0},{1,3},{3,5},{5,7},{7,1},{8,10},{10,12},{12... | collective-permute-start | bytes 442376 | tf_op jit(solution)/shard_map/ppermute | solution.py:427
  105.6 5.5 %collective-permute-start.38 = (bf16[2,24,1536]{2,1,0:T(8,128)(2,1)S(1)}, bf16[2,24,1536]{2,1,0:T(8,128)(2,1)S(1)}, u32[]{:S(2)}, u32[]{:S(2)}) collective-permute-start(bf16[2,24,1536]{2,1,0:T(8,128)(2,1)S(1)} %get-tuple-element.49), channel_id=1, source_target_pairs={{0,4},{2,6},{4,0},{6,2},{1,5},{3,7},{5,1},{7,3},{8,12},{10,14},{12... | collective-permute-start | bytes 442376 | tf_op jit(solution)/shard_map/ppermute | solution.py:427
  105.6 8.3 %collective-permute-start.39 = (bf16[2,24,1536]{2,1,0:T(8,128)(2,1)S(1)}, bf16[2,24,1536]{2,1,0:T(8,128)(2,1)S(1)}, u32[]{:S(2)}, u32[]{:S(2)}) collective-permute-start(bf16[2,24,1536]{2,1,0:T(8,128)(2,1)S(1)} %get-tuple-element.50), channel_id=1, source_target_pairs={{0,6},{2,0},{4,2},{6,4},{1,7},{3,1},{5,3},{7,5},{8,14},{10,8},{12,... | collective-permute-start | bytes 442376 | tf_op jit(solution)/shard_map/ppermute | solution.py:427
  107.3 9.1 %collective-permute-start.26 = (bf16[96,1536]{1,0:T(8,128)(2,1)S(1)}, bf16[96,1536]{1,0:T(8,128)(2,1)S(1)}, u32[]{:S(2)}, u32[]{:S(2)}) collective-permute-start(bf16[96,1536]{1,0:T(8,128)(2,1)S(1)} %collective-permute-done.18.refs_2_), channel_id=1, source_target_pairs={{0,1},{1,0},{2,3},{3,2},{4,5},{5,4},{6,7},{7,6},{8,9},{9,8},{10,11... | collective-permute-start | bytes 884744 | tf_op jit(solution)/shard_map/ppermute | solution.py:255
  109.5 12.2 %collective-permute-start.28 = (bf16[96,1536]{1,0:T(8,128)(2,1)S(1)}, bf16[96,1536]{1,0:T(8,128)(2,1)S(1)}, u32[]{:S(2)}, u32[]{:S(2)}) collective-permute-start(bf16[96,1536]{1,0:T(8,128)(2,1)S(1)} %collective-permute-done.20.refs_4_), channel_id=1, source_target_pairs={{0,1},{1,0},{2,3},{3,2},{4,5},{5,4},{6,7},{7,6},{8,9},{9,8},{10,11... | collective-permute-start | bytes 884744 | tf_op jit(solution)/shard_map/ppermute | solution.py:255
  109.6 12.3 %collective-permute-start.29 = (bf16[96,1536]{1,0:T(8,128)(2,1)S(1)}, bf16[96,1536]{1,0:T(8,128)(2,1)S(1)}, u32[]{:S(2)}, u32[]{:S(2)}) collective-permute-start(bf16[96,1536]{1,0:T(8,128)(2,1)S(1)} %collective-permute-done.21.refs_5_), channel_id=1, source_target_pairs={{0,1},{1,0},{2,3},{3,2},{4,5},{5,4},{6,7},{7,6},{8,9},{9,8},{10,11... | collective-permute-start | bytes 884744 | tf_op jit(solution)/shard_map/ppermute | solution.py:255
  111.1 11.4 %collective-permute-start.30 = (bf16[96,1536]{1,0:T(8,128)(2,1)S(1)}, bf16[96,1536]{1,0:T(8,128)(2,1)S(1)}, u32[]{:S(2)}, u32[]{:S(2)}) collective-permute-start(bf16[96,1536]{1,0:T(8,128)(2,1)S(1)} %collective-permute-done.22.refs_6_), channel_id=1, source_target_pairs={{0,1},{1,0},{2,3},{3,2},{4,5},{5,4},{6,7},{7,6},{8,9},{9,8},{10,11... | collective-permute-start | bytes 884744 | tf_op jit(solution)/shard_map/ppermute | solution.py:255
  114.0 11.5 %collective-permute-start.31 = (bf16[96,1536]{1,0:T(8,128)(2,1)S(1)}, bf16[96,1536]{1,0:T(8,128)(2,1)S(1)}, u32[]{:S(2)}, u32[]{:S(2)}) collective-permute-start(bf16[96,1536]{1,0:T(8,128)(2,1)S(1)} %collective-permute-done.23.refs_7_), channel_id=1, source_target_pairs={{0,1},{1,0},{2,3},{3,2},{4,5},{5,4},{6,7},{7,6},{8,9},{9,8},{10,11... | collective-permute-start | bytes 884744 | tf_op jit(solution)/shard_map/ppermute | solution.py:255
  116.4 18.1 %collective-permute-start.40 = (f32[12,1536]{1,0:T(8,128)S(1)}, f32[12,1536]{1,0:T(8,128)S(1)}, u32[]{:S(2)}, u32[]{:S(2)}) collective-permute-start(f32[12,1536]{1,0:T(8,128)S(1)} %get-tuple-element.51), channel_id=1, source_target_pairs={{0,0},{1,64},{8,8},{9,72},{64,1},{65,65},{72,9},{73,73},{2,2},{3,6... | collective-permute-start | bytes 221192 | tf_op jit(solution)/shard_map/ppermute | solution.py:434
  121.8 12.7 %collective-permute-start.41 = (f32[12,1536]{1,0:T(8,128)S(1)}, f32[12,1536]{1,0:T(8,128)S(1)}, u32[]{:S(2)}, u32[]{:S(2)}) collective-permute-start(f32[12,1536]{1,0:T(8,128)S(1)} %get-tuple-element.52), channel_id=1, source_target_pairs={{0,1},{1,65},{8,9},{9,73},{64,0},{65,64},{72,8},{73,72},{2,3},{3,6... | collective-permute-start | bytes 221192 | tf_op jit(solution)/shard_map/ppermute | solution.py:434
  121.9 12.6 %collective-permute-start.42 = (f32[12,1536]{1,0:T(8,128)S(1)}, f32[12,1536]{1,0:T(8,128)S(1)}, u32[]{:S(2)}, u32[]{:S(2)}) collective-permute-start(f32[12,1536]{1,0:T(8,128)S(1)} %get-tuple-element.53), channel_id=1, source_target_pairs={{0,8},{1,72},{8,0},{9,64},{64,9},{65,73},{72,1},{73,65},{2,10},{3,... | collective-permute-start | bytes 221192 | tf_op jit(solution)/shard_map/ppermute | solution.py:434
  122.5 12.0 %collective-permute-start.43 = (f32[12,1536]{1,0:T(8,128)S(1)}, f32[12,1536]{1,0:T(8,128)S(1)}, u32[]{:S(2)}, u32[]{:S(2)}) collective-permute-start(f32[12,1536]{1,0:T(8,128)S(1)} %get-tuple-element.54), channel_id=1, source_target_pairs={{0,9},{1,73},{8,1},{9,65},{64,8},{65,72},{72,0},{73,64},{2,11},{3,... | collective-permute-start | bytes 221192 | tf_op jit(solution)/shard_map/ppermute | solution.py:434
where the time goes:
time: 136 us; the launch traced here: 135 us
  starting transfers between devices  62.1 us (46%)
  waiting for transfers between devices  38.4 us (28%)
  Pallas kernels  25.8 us (19%)
  matrix products  6.56 us (5%)
  between operations  2.25 us (2%)
    ppermute x3, waiting for transfers between devices, weight_pieces(): on_x = [weight] + [lax.ppermute(weight, 'x', turn(k)) for k in (1, 2, 3)]  13.5 us
    ppermute x8, starting transfers between devices, weight_pieces(): lax.ppermute(p, 'c', SWAP)  12.5 us
    pallas_call x1, Pallas kernels, grad_of_input(): pl.pallas_call(kernel, grid=(rows // block,), out_shape=jax.ShapeDtypeStr...  9.03 us
    ppermute x3, waiting for transfers between devices, step(): all_queries = [own] + [lax.ppermute(own, 'y', turn(k)) for k in (1, 2, 3)]  7.24 us
    ppermute x3, starting transfers between devices, step(): lax.ppermute(partial[k], 'y', turn(-k))  6.75 us
    dot_general x1, matrix products, weight_gradient(): lax.dot_general(theirs, critic_cot, (((0,), (0,)), ((), ())), preferred_e...  6.56 us
    ppermute x1, waiting for transfers between devices, weight_pieces(): pieces[0, 2] = lax.ppermute(pieces[0, 1], 'y', turn(-1))  6.32 us
    ppermute x4, starting transfers between devices, weight_gradient(): lax.ppermute(a, ('zh', 'zl', 'c'), owner(n // 2, n % 2))  6.17 us
  transfers between devices with their start and end apart: 44, of which 12 were waited for; matrix products, arithmetic and copies ran while one was open for 0% of the time, Pallas kernels for 19%

commit v1 on v0

--- a/solution.py
+++ b/solution.py
@@ -98,7 +98,7 @@
                 ) * (HEAD ** (-0.5))
                 s = jnp.where(alive, s, -1e30)
                 top = jnp.max(s, axis=1, keepdims=True).astype(BF).astype(F32)
-                w = jnp.where(alive, jnp.exp(s - top), 0.0)
+                w = jnp.exp(s - top)
                 total = jnp.sum(w, axis=1, keepdims=True)
                 o = jnp.dot(w.astype(BF), v, preferred_element_type=F32)
                 outs[r][:, cols] = o.astype(BF)
@@ -269,6 +269,34 @@
     )(*[in_vmem(a) for a in sets])
 
 
+def product_to_send(place, critic_in, critic_cot, factor):
+    tokens, width = critic_cot.shape
+
+    def kernel(place_ref, in_ref, cot_ref, out_ref):
+        out_ref[...] = (
+            lax.dot_general(
+                in_ref[...], cot_ref[...], (((0,), (0,)), ((), ())), preferred_element_type=F32
+            )
+            * factor
+        ).astype(BF)
+
+    return pl.pallas_call(
+        kernel,
+        grid_spec=pltpu.PrefetchScalarGridSpec(
+            num_scalar_prefetch=1,
+            grid=(2,),
+            in_specs=[
+                pl.BlockSpec((tokens, width // 4), lambda p, place: (0, 2 * (1 - place[2]) + p)),
+                pl.BlockSpec((tokens, width), lambda p, place: (0, 0)),
+            ],
+            out_specs=pl.BlockSpec((width // 4, width), lambda p, place: (p, 0)),
+        ),
+        out_shape=jax.ShapeDtypeStruct((width // 2, width), BF),
+        compiler_params=room(32, dimension_semantics=("arbitrary",)),
+        name="product_to_send",
+    )(place, in_hbm(critic_in), in_vmem(critic_cot))
+
+
 def product_and_split(place, critic_in, critic_cot, got, factor):
     tokens, width = critic_cot.shape
     half = width // 2
@@ -319,7 +347,7 @@
         + [jax.ShapeDtypeStruct((2, 192, half), F32)] * 2,
         compiler_params=room(40, dimension_semantics=("arbitrary",)),
         name="product_and_split",
-    )(place, in_hbm(critic_in), critic_cot, in_vmem(got))
+    )(place, in_hbm(critic_in), in_vmem(critic_cot), in_vmem(got))
 
 
 def onward_of(keep_l, keep_r, got_l, got_r):
@@ -405,15 +433,8 @@
     )(*[in_vmem(a) for a in arrays])
 
 
-def weight_gradient(place, critic_in, critic_cot, c, factor):
-    half = critic_cot.shape[1] // 2
-    theirs = lax.dynamic_slice_in_dim(critic_in, (1 - c) * half, half, 1)
-    theirs = (
-        lax.dot_general(
-            theirs, critic_cot, (((0,), (0,)), ((), ())), preferred_element_type=F32
-        )
-        * factor
-    ).astype(BF)
+def weight_gradient(place, critic_in, critic_cot, factor):
+    theirs = product_to_send(place, critic_in, critic_cot, factor)
     got = lax.ppermute(theirs, "c", SWAP)
     send_l, send_r, keep_l, keep_r = product_and_split(place, critic_in, critic_cot, got, factor)
     near = [(0, 1), (1, 0), (2, 3), (3, 2)]
@@ -464,7 +485,7 @@
     pieces = weight_pieces(critic_weight)
 
     factor = float(critic_in.shape[0] * 128) ** (-0.5)
-    grad_weight = weight_gradient(place, critic_in, critic_cot, c, factor)
+    grad_weight = weight_gradient(place, critic_in, critic_cot, factor)
 
     own = own_queries_of(sets)
     all_queries = [own] + [lax.ppermute(own, "y", turn(k)) for k in (1, 2, 3)]

time: 136 us -> 136 us (level)
  matrix products: 6.56 us -> 0 us
  Pallas kernels: 25.8 us -> 30.4 us
  local copies, waits for them, and re-layouts: 0.13 us -> 2.01 us
    dot_general x1 -> x0, matrix products: 6.56 us -> none  [weight_gradient(): lax.dot_general(theirs, critic_cot, (((0,), (0,)), ((), ())), preferred_e...]
    pallas_call x0 -> x1, Pallas kernels: none -> 4.88 us  [product_to_send(): pl.pallas_call(kernel, grid_spec=pltpu.PrefetchScalarGridSpec(num_scalar_...]
    unnamed x16 -> x18, local copies, waits for them, and re-layouts: 0.04 us -> 1.93 us
  transfers between devices with their start and end apart: 44 -> 44, of which waited for: 12 -> 12; matrix products, arithmetic and copies ran while one was open for 0% -> 0% of each run, Pallas kernels for 19% -> 18%
where the time goes in v1:
time: 136 us; the launch traced here: 135 us
  starting transfers between devices  62.4 us (46%)
  waiting for transfers between devices  38.1 us (28%)
  Pallas kernels  30.4 us (22%)
  between operations  2.24 us (2%)
  local copies, waits for them, and re-layouts  2.01 us (1%)
    ppermute x3, waiting for transfers between devices, weight_pieces(): on_x = [weight] + [lax.ppermute(weight, 'x', turn(k)) for k in (1, 2, 3)]  13.5 us
    ppermute x8, starting transfers between devices, weight_pieces(): lax.ppermute(p, 'c', SWAP)  12.4 us
    pallas_call x1, Pallas kernels, grad_of_input(): pl.pallas_call(kernel, grid=(rows // block,), out_shape=jax.ShapeDtypeStr...  9.19 us
    ppermute x3, waiting for transfers between devices, step(): all_queries = [own] + [lax.ppermute(own, 'y', turn(k)) for k in (1, 2, 3)]  7.23 us
    ppermute x3, starting transfers between devices, step(): lax.ppermute(partial[k], 'y', turn(-k))  6.93 us
    ppermute x1, waiting for transfers between devices, weight_pieces(): pieces[0, 2] = lax.ppermute(pieces[0, 1], 'y', turn(-1))  6.32 us
    ppermute x4, starting transfers between devices, weight_gradient(): lax.ppermute(a, ('zh', 'zl', 'c'), owner(n // 2, n % 2))  6.22 us
    ppermute x1, starting transfers between devices, step(): lax.ppermute(mixed[1], 'c', SWAP)  6.18 us
  transfers between devices with their start and end apart: 44, of which 12 were waited for; matrix products, arithmetic and copies ran while one was open for 0% of the time, Pallas kernels for 18%

profile of v1, /device:TPU:1, one launch (start us, length us, event | category | flops | bytes accessed | tf_op | source)
XLA Modules:
  0.0 135.2 jit_solution(10458869636478675484)
XLA Ops:
  0.6 0.1 stack.23.place_ref
  0.7 1.9 %copy-done = bf16[1024,1536]{1,0:T(8,128)(2,1)S(1)} copy-done((bf16[1024,1536]{1,0:T(8,128)(2,1)S(1)}, bf16[1024,1536]{1,0:T(8,128)(2,1)}, u32[]{:S(2)}) %copy-start) | copy-done | bytes 3145752
  2.6 4.9 %product_to_send.1 = bf16[768,1536]{1,0:T(8,128)(2,1)S(1)} custom-call(s32[5]{0:T(128)S(1)} %stack.23.place_ref, bf16[1024,1536]{1,0:T(8,128)(2,1)} %in_ref.3, bf16[1024,1536]{1,0:T(8,128)(2,1)S(1)} %copy-done), custom_call_target="tpu_custom_call" | custom-call | tf_op jit(solution)/shard_map/product_to_send/pallas_call | solution.py:283
  7.5 1.5 %collective-permute-start.32 = (bf16[768,1536]{1,0:T(8,128)(2,1)S(1)}, bf16[768,1536]{1,0:T(8,128)(2,1)S(1)}, u32[]{:S(2)}, u32[]{:S(2)}) collective-permute-start(bf16[768,1536]{1,0:T(8,128)(2,1)S(1)} %product_to_send.1), channel_id=1, source_target_pairs={{0,1},{1,0},{2,3},{3,2},{4,5},{5,4},{6,7},{7,6},{8,9},{9,8},{10,11... | collective-permute-start | bytes 7077896 | tf_op jit(solution)/shard_map/ppermute | solution.py:438
  9.6 1.3 packed.1
  10.9 0.1 collective-permute-start.2
  11.0 0.5 collective-permute-start
  11.5 1.7 %collective-permute-start.1 = (bf16[304,384]{1,0:T(8,128)(2,1)S(1)}, bf16[304,384]{1,0:T(8,128)(2,1)S(1)}, u32[]{:S(2)}, u32[]{:S(2)}) collective-permute-start(bf16[304,384]{1,0:T(8,128)(2,1)S(1)} %get-tuple-element.31), channel_id=1, source_target_pairs={{0,8},{8,0},{1,9},{9,1},{2,10},{10,2},{3,11},{11,3},{4,12},{12,4},... | collective-permute-start | bytes 700424 | tf_op jit(solution)/shard_map/ppermute | solution.py:483
  13.3 0.2 collective-permute-done.2
  13.5 1.7 %collective-permute-start.3 = (bf16[304,384]{1,0:T(8,128)(2,1)S(1)}, bf16[304,384]{1,0:T(8,128)(2,1)S(1)}, u32[]{:S(2)}, u32[]{:S(2)}) collective-permute-start(bf16[304,384]{1,0:T(8,128)(2,1)S(1)} %collective-permute-done.2), channel_id=1, source_target_pairs={{0,8},{8,0},{1,9},{9,1},{2,10},{10,2},{3,11},{11,3},{4,12},{12,4},... | collective-permute-start | bytes 700424 | tf_op jit(solution)/shard_map/ppermute | solution.py:484
  15.2 1.2 collective-permute-start.13
  16.4 2.4 %collective-permute-start.14 = (bf16[12,1536]{1,0:T(8,128)(2,1)S(1)}, bf16[12,1536]{1,0:T(8,128)(2,1)S(1)}, u32[]{:S(2)}, u32[]{:S(2)}) collective-permute-start(bf16[12,1536]{1,0:T(8,128)(2,1)S(1)} %copy-done.6), channel_id=1, source_target_pairs={{0,32},{16,48},{32,0},{48,16},{1,33},{17,49},{33,1},{49,17},{2,34}... | collective-permute-start | bytes 110600 | tf_op jit(solution)/shard_map/ppermute | solution.py:243
  18.9 4.9 %product_and_split.1 = (bf16[2,192,768]{2,1,0:T(8,128)(2,1)S(1)}, bf16[2,192,768]{2,1,0:T(8,128)(2,1)S(1)}, f32[2,192,768]{2,1,0:T(8,128)S(1)}, f32[2,192,768]{2,1,0:T(8,128)S(1)}) custom-call(s32[5]{0:T(128)S(1)} %stack.23.place_ref, bf16[1024,1536]{1,0:T(8,128)(2,1)} %in_ref.3, bf16[1024,1536]{1,0:T(8,128)(2,1)S(1)} %copy-done.1, ...), custom_call_target="tpu_custom_call" | custom-call | tf_op jit(solution)/shard_map/product_and_split/pallas_call | solution.py:334
  23.8 0.1 collective-permute-start.33
  23.9 1.2 collective-permute-start.15
  25.2 13.5 %collective-permute-done.15.refs_3_ = bf16[12,1536]{1,0:T(8,128)(2,1)S(1)} collective-permute-done((bf16[12,1536]{1,0:T(8,128)(2,1)S(1)}, bf16[12,1536]{1,0:T(8,128)(2,1)S(1)}, u32[]{:S(2)}, u32[]{:S(2)}) %collective-permute-start.15) | collective-permute-done | bytes 36896 | tf_op jit(solution)/shard_map/ppermute | solution.py:243
  38.6 0.8 joined.2.refs_0_
  39.5 3.4 %collective-permute-start.16 = (bf16[48,1536]{1,0:T(8,128)(2,1)S(1)}, bf16[48,1536]{1,0:T(8,128)(2,1)S(1)}, u32[]{:S(2)}, u32[]{:S(2)}) collective-permute-start(bf16[48,1536]{1,0:T(8,128)(2,1)S(1)} %joined.2.refs_0_), channel_id=1, source_target_pairs={{0,64},{64,0},{1,65},{65,1},{2,66},{66,2},{3,67},{67,3},{4,68},{68... | collective-permute-start | bytes 442376 | tf_op jit(solution)/shard_map/ppermute | solution.py:245
  42.9 1.4 %collective-permute-start.4 = (bf16[128,384]{1,0:T(8,128)(2,1)S(1)}, bf16[128,384]{1,0:T(8,128)(2,1)S(1)}, u32[]{:S(2)}, u32[]{:S(2)}) collective-permute-start(bf16[128,384]{1,0:T(8,128)(2,1)S(1)} %own_queries.1.refs_4_), channel_id=1, source_target_pairs={{0,2},{2,4},{4,6},{6,0},{1,3},{3,5},{5,7},{7,1},{8,10},{10,12},{12... | collective-permute-start | bytes 294920 | tf_op jit(solution)/shard_map/ppermute | solution.py:491
  44.3 1.1 collective-permute-done.16.refs_1_
  45.4 1.1 joined.3.refs_0_
  46.5 0.2 collective-permute-start.17
  46.7 2.7 %collective-permute-start.19 = (bf16[96,1536]{1,0:T(8,128)(2,1)S(1)}, bf16[96,1536]{1,0:T(8,128)(2,1)S(1)}, u32[]{:S(2)}, u32[]{:S(2)}) collective-permute-start(bf16[96,1536]{1,0:T(8,128)(2,1)S(1)} %joined.3.refs_0_), channel_id=1, source_target_pairs={{0,6},{2,0},{4,2},{6,4},{1,7},{3,1},{5,3},{7,5},{8,14},{10,8},{12,... | collective-permute-start | bytes 884744 | tf_op jit(solution)/shard_map/ppermute | solution.py:251
  49.4 0.4 collective-permute-start.5
  49.8 4.6 %collective-permute-done.5.refs_6_ = bf16[128,384]{1,0:T(8,128)(2,1)S(1)} collective-permute-done((bf16[128,384]{1,0:T(8,128)(2,1)S(1)}, bf16[128,384]{1,0:T(8,128)(2,1)S(1)}, u32[]{:S(2)}, u32[]{:S(2)}) %collective-permute-start.5) | collective-permute-done | bytes 98336 | tf_op jit(solution)/shard_map/ppermute | solution.py:491
  54.4 2.0 %collective-permute-start.6 = (bf16[128,384]{1,0:T(8,128)(2,1)S(1)}, bf16[128,384]{1,0:T(8,128)(2,1)S(1)}, u32[]{:S(2)}, u32[]{:S(2)}) collective-permute-start(bf16[128,384]{1,0:T(8,128)(2,1)S(1)} %own_queries.1.refs_4_), channel_id=1, source_target_pairs={{0,6},{2,0},{4,2},{6,4},{1,7},{3,1},{5,3},{7,5},{8,14},{10,8},{12,... | collective-permute-start | bytes 294920 | tf_op jit(solution)/shard_map/ppermute | solution.py:491
  56.4 2.6 %collective-permute-done.6.refs_7_ = bf16[128,384]{1,0:T(8,128)(2,1)S(1)} collective-permute-done((bf16[128,384]{1,0:T(8,128)(2,1)S(1)}, bf16[128,384]{1,0:T(8,128)(2,1)S(1)}, u32[]{:S(2)}, u32[]{:S(2)}) %collective-permute-start.6) | collective-permute-done | bytes 98336 | tf_op jit(solution)/shard_map/ppermute | solution.py:491
  59.1 3.4 %attend.1 = (bf16[128,512]{1,0:T(8,128)(2,1)S(1)}, bf16[128,512]{1,0:T(8,128)(2,1)S(1)}, bf16[128,512]{1,0:T(8,128)(2,1)S(1)}, bf16[128,512]{1,0:T(8,128)(2,1)S(1)}) custom-call(bf16[304,384]{1,0:T(8,128)(2,1)S(1)} %get-tuple-element.29.refs_0_, bf16[304,384]{1,0:T(8,128)(2,1)S(1)} %collective-permute-done.refs_1_, ...), custom_call_target="tpu_custom_call" | custom-call | tf_op jit(solution)/shard_map/attend/pallas_call | solution.py:112
  62.4 3.5 %collective-permute-start.7 = (bf16[128,512]{1,0:T(8,128)(2,1)S(1)}, bf16[128,512]{1,0:T(8,128)(2,1)S(1)}, u32[]{:S(2)}, u32[]{:S(2)}) collective-permute-start(bf16[128,512]{1,0:T(8,128)(2,1)S(1)} %get-tuple-element.34), channel_id=1, source_target_pairs={{0,6},{2,0},{4,2},{6,4},{1,7},{3,1},{5,3},{7,5},{8,14},{10,8},{12,... | collective-permute-start | bytes 393224 | tf_op jit(solution)/shard_map/ppermute | solution.py:493
  65.9 4.5 %collective-permute-start.24 = (bf16[96,1536]{1,0:T(8,128)(2,1)S(1)}, bf16[96,1536]{1,0:T(8,128)(2,1)S(1)}, u32[]{:S(2)}, u32[]{:S(2)}) collective-permute-start(bf16[96,1536]{1,0:T(8,128)(2,1)S(1)} %joined.3.refs_0_), channel_id=1, source_target_pairs={{0,1},{1,0},{2,3},{3,2},{4,5},{5,4},{6,7},{7,6},{8,9},{9,8},{10,11... | collective-permute-start | bytes 884744 | tf_op jit(solution)/shard_map/ppermute | solution.py:255
  70.4 1.5 %collective-permute-start.8 = (bf16[128,512]{1,0:T(8,128)(2,1)S(1)}, bf16[128,512]{1,0:T(8,128)(2,1)S(1)}, u32[]{:S(2)}, u32[]{:S(2)}) collective-permute-start(bf16[128,512]{1,0:T(8,128)(2,1)S(1)} %get-tuple-element.35), channel_id=1, source_target_pairs={{0,4},{2,6},{4,0},{6,2},{1,5},{3,7},{5,1},{7,3},{8,12},{10,14},{12... | collective-permute-start | bytes 393224 | tf_op jit(solution)/shard_map/ppermute | solution.py:493
  71.9 1.9 %collective-permute-start.9 = (bf16[128,512]{1,0:T(8,128)(2,1)S(1)}, bf16[128,512]{1,0:T(8,128)(2,1)S(1)}, u32[]{:S(2)}, u32[]{:S(2)}) collective-permute-start(bf16[128,512]{1,0:T(8,128)(2,1)S(1)} %get-tuple-element.36), channel_id=1, source_target_pairs={{0,2},{2,4},{4,6},{6,0},{1,3},{3,5},{5,7},{7,1},{8,10},{10,12},{12... | collective-permute-start | bytes 393224 | tf_op jit(solution)/shard_map/ppermute | solution.py:493
  74.0 0.1 onward.1
  74.1 3.1 %collective-permute-done.8.refs_2_ = bf16[128,512]{1,0:T(8,128)(2,1)S(1)} collective-permute-done((bf16[128,512]{1,0:T(8,128)(2,1)S(1)}, bf16[128,512]{1,0:T(8,128)(2,1)S(1)}, u32[]{:S(2)}, u32[]{:S(2)}) %collective-permute-start.8) | collective-permute-done | bytes 131104 | tf_op jit(solution)/shard_map/ppermute | solution.py:493
  77.1 3.0 %collective-permute-start.35 = (bf16[192,768]{1,0:T(8,128)(2,1)S(1)}, bf16[192,768]{1,0:T(8,128)(2,1)S(1)}, u32[]{:S(2)}, u32[]{:S(2)}) collective-permute-start(bf16[192,768]{1,0:T(8,128)(2,1)S(1)} %get-tuple-element.45), channel_id=1, source_target_pairs={{0,48},{48,0},{16,32},{32,16},{1,49},{49,1},{17,33},{33,17},{2,50}... | collective-permute-start | bytes 884744 | tf_op jit(solution)/shard_map/ppermute | solution.py:445
  80.2 0.5 collective-permute-done.9.refs_3_
  80.7 1.0 collective-permute-start.36
  81.7 0.5 merged.1
  82.2 6.2 %collective-permute-start.10 = (bf16[32,384]{1,0:T(8,128)(2,1)S(1)}, bf16[32,384]{1,0:T(8,128)(2,1)S(1)}, u32[]{:S(2)}, u32[]{:S(2)}) collective-permute-start(bf16[32,384]{1,0:T(8,128)(2,1)S(1)} %get-tuple-element.38), channel_id=1, source_target_pairs={{0,1},{1,0},{2,3},{3,2},{4,5},{5,4},{6,7},{7,6},{8,9},{9,8},{10,11... | collective-permute-start | bytes 73736 | tf_op jit(solution)/shard_map/ppermute | solution.py:498
  88.3 1.6 %collective-permute-start.11 = (bf16[32,384]{1,0:T(8,128)(2,1)S(1)}, bf16[32,384]{1,0:T(8,128)(2,1)S(1)}, u32[]{:S(2)}, u32[]{:S(2)}) collective-permute-start(bf16[32,384]{1,0:T(8,128)(2,1)S(1)} %get-tuple-element.39), channel_id=1, source_target_pairs={{0,8},{8,0},{1,9},{9,1},{2,10},{10,2},{3,11},{11,3},{4,12},{12,4},... | collective-permute-start | bytes 73736 | tf_op jit(solution)/shard_map/ppermute | solution.py:499
  89.9 1.1 collective-permute-start.12
  91.0 0.4 collective-permute-done.11.c_ref
  91.4 1.7 %collective-permute-done.12.d_ref = bf16[32,384]{1,0:T(8,128)(2,1)S(1)} collective-permute-done((bf16[32,384]{1,0:T(8,128)(2,1)S(1)}, bf16[32,384]{1,0:T(8,128)(2,1)S(1)}, u32[]{:S(2)}, u32[]{:S(2)}) %collective-permute-start.12) | collective-permute-done | bytes 24608 | tf_op jit(solution)/shard_map/ppermute | solution.py:500
  93.2 0.4 collective-permute-start.25
  93.5 0.1 collective-permute-start.27
  93.7 1.7 %collective-permute-start.23 = (bf16[96,1536]{1,0:T(8,128)(2,1)S(1)}, bf16[96,1536]{1,0:T(8,128)(2,1)S(1)}, u32[]{:S(2)}, u32[]{:S(2)}) collective-permute-start(bf16[96,1536]{1,0:T(8,128)(2,1)S(1)} %collective-permute-done.20.refs_4_), channel_id=1, source_target_pairs={{0,2},{2,4},{4,6},{6,0},{1,3},{3,5},{5,7},{7,1},{8,10},{10,12},{12... | collective-permute-start | bytes 884744 | tf_op jit(solution)/shard_map/ppermute | solution.py:253
  95.4 0.8 cut_along_y.1
  96.2 2.9 %collective-permute-done.21.refs_5_ = bf16[96,1536]{1,0:T(8,128)(2,1)S(1)} collective-permute-done((bf16[96,1536]{1,0:T(8,128)(2,1)S(1)}, bf16[96,1536]{1,0:T(8,128)(2,1)S(1)}, u32[]{:S(2)}, u32[]{:S(2)}) %collective-permute-start.21) | collective-permute-done | bytes 294944 | tf_op jit(solution)/shard_map/ppermute | solution.py:251
  99.1 6.3 %collective-permute-done.22.refs_6_ = bf16[96,1536]{1,0:T(8,128)(2,1)S(1)} collective-permute-done((bf16[96,1536]{1,0:T(8,128)(2,1)S(1)}, bf16[96,1536]{1,0:T(8,128)(2,1)S(1)}, u32[]{:S(2)}, u32[]{:S(2)}) %collective-permute-start.22) | collective-permute-done | bytes 294944 | tf_op jit(solution)/shard_map/ppermute | solution.py:252
  105.4 1.7 %collective-permute-start.39 = (bf16[2,24,1536]{2,1,0:T(8,128)(2,1)S(1)}, bf16[2,24,1536]{2,1,0:T(8,128)(2,1)S(1)}, u32[]{:S(2)}, u32[]{:S(2)}) collective-permute-start(bf16[2,24,1536]{2,1,0:T(8,128)(2,1)S(1)} %get-tuple-element.50), channel_id=1, source_target_pairs={{0,6},{2,0},{4,2},{6,4},{1,7},{3,1},{5,3},{7,5},{8,14},{10,8},{12,... | collective-permute-start | bytes 442376 | tf_op jit(solution)/shard_map/ppermute | solution.py:448
  107.1 2.3 %collective-permute-start.26 = (bf16[96,1536]{1,0:T(8,128)(2,1)S(1)}, bf16[96,1536]{1,0:T(8,128)(2,1)S(1)}, u32[]{:S(2)}, u32[]{:S(2)}) collective-permute-start(bf16[96,1536]{1,0:T(8,128)(2,1)S(1)} %collective-permute-done.18.refs_2_), channel_id=1, source_target_pairs={{0,1},{1,0},{2,3},{3,2},{4,5},{5,4},{6,7},{7,6},{8,9},{9,8},{10,11... | collective-permute-start | bytes 884744 | tf_op jit(solution)/shard_map/ppermute | solution.py:255
  109.4 0.1 collective-permute-start.28
  109.5 0.4 collective-permute-start.29
  109.9 1.0 collective-permute-done.38.b
  110.9 2.9 %collective-permute-start.30 = (bf16[96,1536]{1,0:T(8,128)(2,1)S(1)}, bf16[96,1536]{1,0:T(8,128)(2,1)S(1)}, u32[]{:S(2)}, u32[]{:S(2)}) collective-permute-start(bf16[96,1536]{1,0:T(8,128)(2,1)S(1)} %collective-permute-done.22.refs_6_), channel_id=1, source_target_pairs={{0,1},{1,0},{2,3},{3,2},{4,5},{5,4},{6,7},{7,6},{8,9},{9,8},{10,11... | collective-permute-start | bytes 884744 | tf_op jit(solution)/shard_map/ppermute | solution.py:255
  113.8 1.7 %collective-permute-start.31 = (bf16[96,1536]{1,0:T(8,128)(2,1)S(1)}, bf16[96,1536]{1,0:T(8,128)(2,1)S(1)}, u32[]{:S(2)}, u32[]{:S(2)}) collective-permute-start(bf16[96,1536]{1,0:T(8,128)(2,1)S(1)} %collective-permute-done.23.refs_7_), channel_id=1, source_target_pairs={{0,1},{1,0},{2,3},{3,2},{4,5},{5,4},{6,7},{7,6},{8,9},{9,8},{10,11... | collective-permute-start | bytes 884744 | tf_op jit(solution)/shard_map/ppermute | solution.py:255
  115.5 0.6 cut_to_owners.1
  116.2 5.4 %collective-permute-start.40 = (f32[12,1536]{1,0:T(8,128)S(1)}, f32[12,1536]{1,0:T(8,128)S(1)}, u32[]{:S(2)}, u32[]{:S(2)}) collective-permute-start(f32[12,1536]{1,0:T(8,128)S(1)} %get-tuple-element.51), channel_id=1, source_target_pairs={{0,0},{1,64},{8,8},{9,72},{64,1},{65,65},{72,9},{73,73},{2,2},{3,6... | collective-permute-start | bytes 221192 | tf_op jit(solution)/shard_map/ppermute | solution.py:455
  121.6 0.1 collective-permute-start.41
  121.7 0.6 collective-permute-start.42
  122.3 0.1 collective-permute-start.43
  123.1 2.1 %streamed.1 = bf16[32,1536]{1,0:T(8,128)(2,1)} custom-call(s32[5]{0:T(128)S(1)} %stack.23.place_ref, s32[1]{0:T(128)S(6)} %copy.18.step_ref, bf16[32,1536]{1,0:T(8,128)(2,1)S(1)} %bitcast.14, f32[4,1536]{1,0:T(4,128)S(1)} %copy-done.4, bf16[32,384]{1,0:T(8,128)(2,1)S(1)} %get-tuple-element.37.a_ref, bf16[32,384]{1,0:T(8,128)(2,1)S(1)} %collective-permute-done.10.b_ref, ...), custom_call_target="tpu_custom_call" | custom-call | tf_op jit(solution)/shard_map/streamed/pallas_call | solution.py:163
  125.3 9.2 %grad_of_input.1 = bf16[1024,1536]{1,0:T(8,128)(2,1)} custom-call(s32[5]{0:T(128)S(1)} %stack.23.place_ref, bf16[1024,1536]{1,0:T(8,128)(2,1)S(1)} %copy-done.1, bf16[96,1536]{1,0:T(8,128)(2,1)S(1)} %joined.3.refs_0_, bf16[96,1536]{1,0:T(8,128)(2,1)S(1)} %collective-permute-done.17.refs_1_, bf16[96,1536]{1,0:T(8,128)(2,1)S(1)} %collective-permute-done.18.refs_2_, ...), custom_call_target="tpu_custom_call" | custom-call | tf_op jit(solution)/shard_map/grad_of_input/pallas_call | solution.py:209
  134.5 0.7 added.1
  (58 shorter events, 0.2 us)
Async XLA Ops:
  0.7 1.9 %copy-start = (bf16[1024,1536]{1,0:T(8,128)(2,1)S(1)}, bf16[1024,1536]{1,0:T(8,128)(2,1)}, u32[]{:S(2)}) copy-start(bf16[1024,1536]{1,0:T(8,128)(2,1)} %cot_ref.5) | copy-start | bytes 9437188
  2.6 7.0 %copy-start.5 = (s32[1,96]{1,0:T(1,128)S(1)}, s32[1,96]{1,0:T(1,128)}, u32[]{:S(2)}) copy-start(s32[1,96]{1,0:T(1,128)} %frames_ref.1) | copy-start | bytes 1156
  2.6 12.6 %copy-start.6 = (bf16[12,1536]{1,0:T(8,128)(2,1)S(1)}, bf16[12,1536]{1,0:T(8,128)(2,1)}, u32[]{:S(2)}) copy-start(bf16[12,1536]{1,0:T(8,128)(2,1)} %refs_0_.1) | copy-start | bytes 110596
  2.6 16.3 %copy-start.1 = (bf16[1024,1536]{1,0:T(8,128)(2,1)S(1)}, bf16[1024,1536]{1,0:T(8,128)(2,1)}, u32[]{:S(2)}) copy-start(bf16[1024,1536]{1,0:T(8,128)(2,1)} %cot_ref.5) | copy-start | bytes 9437188
  7.5 8.9 %collective-permute-start.32 = (bf16[768,1536]{1,0:T(8,128)(2,1)S(1)}, bf16[768,1536]{1,0:T(8,128)(2,1)S(1)}, u32[]{:S(2)}, u32[]{:S(2)}) collective-permute-start(bf16[768,1536]{1,0:T(8,128)(2,1)S(1)} %product_to_send.1), channel_id=1, source_target_pairs={{0,1},{1,0},{2,3},{3,2},{4,5},{5,4},{6,7},{7,6},{8,9},{9,8},{10,11... | collective-permute-start | bytes 7077896 | tf_op jit(solution)/shard_map/ppermute | solution.py:438
  10.9 2.5 %collective-permute-start.2 = (bf16[304,384]{1,0:T(8,128)(2,1)S(1)}, bf16[304,384]{1,0:T(8,128)(2,1)S(1)}, u32[]{:S(2)}, u32[]{:S(2)}) collective-permute-start(bf16[304,384]{1,0:T(8,128)(2,1)S(1)} %get-tuple-element.32), channel_id=1, source_target_pairs={{0,1},{1,0},{2,3},{3,2},{4,5},{5,4},{6,7},{7,6},{8,9},{9,8},{10,11... | collective-permute-start | bytes 700424 | tf_op jit(solution)/shard_map/ppermute | solution.py:484
  11.0 28.5 %collective-permute-start = (bf16[304,384]{1,0:T(8,128)(2,1)S(1)}, bf16[304,384]{1,0:T(8,128)(2,1)S(1)}, u32[]{:S(2)}, u32[]{:S(2)}) collective-permute-start(bf16[304,384]{1,0:T(8,128)(2,1)S(1)} %get-tuple-element.30), channel_id=1, source_target_pairs={{0,1},{1,0},{2,3},{3,2},{4,5},{5,4},{6,7},{7,6},{8,9},{9,8},{10,11... | collective-permute-start | bytes 700424 | tf_op jit(solution)/shard_map/ppermute | solution.py:483
  11.5 31.4 %collective-permute-start.1 = (bf16[304,384]{1,0:T(8,128)(2,1)S(1)}, bf16[304,384]{1,0:T(8,128)(2,1)S(1)}, u32[]{:S(2)}, u32[]{:S(2)}) collective-permute-start(bf16[304,384]{1,0:T(8,128)(2,1)S(1)} %get-tuple-element.31), channel_id=1, source_target_pairs={{0,8},{8,0},{1,9},{9,1},{2,10},{10,2},{3,11},{11,3},{4,12},{12,4},... | collective-permute-start | bytes 700424 | tf_op jit(solution)/shard_map/ppermute | solution.py:483
  13.5 29.4 %collective-permute-start.3 = (bf16[304,384]{1,0:T(8,128)(2,1)S(1)}, bf16[304,384]{1,0:T(8,128)(2,1)S(1)}, u32[]{:S(2)}, u32[]{:S(2)}) collective-permute-start(bf16[304,384]{1,0:T(8,128)(2,1)S(1)} %collective-permute-done.2), channel_id=1, source_target_pairs={{0,8},{8,0},{1,9},{9,1},{2,10},{10,2},{3,11},{11,3},{4,12},{12,4},... | collective-permute-start | bytes 700424 | tf_op jit(solution)/shard_map/ppermute | solution.py:484
  15.2 8.6 %collective-permute-start.13 = (bf16[12,1536]{1,0:T(8,128)(2,1)S(1)}, bf16[12,1536]{1,0:T(8,128)(2,1)S(1)}, u32[]{:S(2)}, u32[]{:S(2)}) collective-permute-start(bf16[12,1536]{1,0:T(8,128)(2,1)S(1)} %copy-done.6), channel_id=1, source_target_pairs={{0,16},{16,32},{32,48},{48,0},{1,17},{17,33},{33,49},{49,1},{2,18}... | collective-permute-start | bytes 110600 | tf_op jit(solution)/shard_map/ppermute | solution.py:243
  16.4 7.5 %collective-permute-start.14 = (bf16[12,1536]{1,0:T(8,128)(2,1)S(1)}, bf16[12,1536]{1,0:T(8,128)(2,1)S(1)}, u32[]{:S(2)}, u32[]{:S(2)}) collective-permute-start(bf16[12,1536]{1,0:T(8,128)(2,1)S(1)} %copy-done.6), channel_id=1, source_target_pairs={{0,32},{16,48},{32,0},{48,16},{1,33},{17,49},{33,1},{49,17},{2,34}... | collective-permute-start | bytes 110600 | tf_op jit(solution)/shard_map/ppermute | solution.py:243
  23.8 48.1 %collective-permute-start.33 = (bf16[2,192,768]{2,1,0:T(8,128)(2,1)S(1)}, bf16[2,192,768]{2,1,0:T(8,128)(2,1)S(1)}, u32[]{:S(2)}, u32[]{:S(2)}) collective-permute-start(bf16[2,192,768]{2,1,0:T(8,128)(2,1)S(1)} %get-tuple-element.43), channel_id=1, source_target_pairs={{0,16},{16,0},{32,48},{48,32},{1,17},{17,1},{33,49},{49,33},{2,18}... | collective-permute-start | bytes 1769480 | tf_op jit(solution)/shard_map/ppermute | solution.py:442
  23.9 14.7 %collective-permute-start.15 = (bf16[12,1536]{1,0:T(8,128)(2,1)S(1)}, bf16[12,1536]{1,0:T(8,128)(2,1)S(1)}, u32[]{:S(2)}, u32[]{:S(2)}) collective-permute-start(bf16[12,1536]{1,0:T(8,128)(2,1)S(1)} %copy-done.6), channel_id=1, source_target_pairs={{0,48},{16,0},{32,16},{48,32},{1,49},{17,1},{33,17},{49,33},{2,50}... | collective-permute-start | bytes 110600 | tf_op jit(solution)/shard_map/ppermute | solution.py:243
  38.6 35.2 %collective-permute-start.34 = (bf16[2,192,768]{2,1,0:T(8,128)(2,1)S(1)}, bf16[2,192,768]{2,1,0:T(8,128)(2,1)S(1)}, u32[]{:S(2)}, u32[]{:S(2)}) collective-permute-start(bf16[2,192,768]{2,1,0:T(8,128)(2,1)S(1)} %get-tuple-element.44), channel_id=1, source_target_pairs={{0,48},{48,0},{16,32},{32,16},{1,49},{49,1},{17,33},{33,17},{2,50}... | collective-permute-start | bytes 1769480 | tf_op jit(solution)/shard_map/ppermute | solution.py:443
  39.5 5.9 %copy-start.2 = (bf16[48,1536]{1,0:T(8,128)(2,1)}, bf16[48,1536]{1,0:T(8,128)(2,1)S(1)}, u32[]{:S(2)}) copy-start(bf16[48,1536]{1,0:T(8,128)(2,1)S(1)} %joined.2.refs_0_) | copy-start | bytes 442372
  39.5 5.9 %collective-permute-start.16 = (bf16[48,1536]{1,0:T(8,128)(2,1)S(1)}, bf16[48,1536]{1,0:T(8,128)(2,1)S(1)}, u32[]{:S(2)}, u32[]{:S(2)}) collective-permute-start(bf16[48,1536]{1,0:T(8,128)(2,1)S(1)} %joined.2.refs_0_), channel_id=1, source_target_pairs={{0,64},{64,0},{1,65},{65,1},{2,66},{66,2},{3,67},{67,3},{4,68},{68... | collective-permute-start | bytes 442376 | tf_op jit(solution)/shard_map/ppermute | solution.py:245
  42.9 6.6 %collective-permute-start.4 = (bf16[128,384]{1,0:T(8,128)(2,1)S(1)}, bf16[128,384]{1,0:T(8,128)(2,1)S(1)}, u32[]{:S(2)}, u32[]{:S(2)}) collective-permute-start(bf16[128,384]{1,0:T(8,128)(2,1)S(1)} %own_queries.1.refs_4_), channel_id=1, source_target_pairs={{0,2},{2,4},{4,6},{6,0},{1,3},{3,5},{5,7},{7,1},{8,10},{10,12},{12... | collective-permute-start | bytes 294920 | tf_op jit(solution)/shard_map/ppermute | solution.py:491
  45.4 77.7 %slice-start = ((s8[4718592]{0:T(1024)(128)(4,1)}), s8[4194304]{0:T(1024)(128)(4,1)S(1)}, s32[]{:S(2)}) async-start(s8[4718592]{0:T(1024)(128)(4,1)} %bitcast.12), calls=%async_computation | async-start | bytes 8388608
  46.5 19.4 %collective-permute-start.17 = (bf16[96,1536]{1,0:T(8,128)(2,1)S(1)}, bf16[96,1536]{1,0:T(8,128)(2,1)S(1)}, u32[]{:S(2)}, u32[]{:S(2)}) collective-permute-start(bf16[96,1536]{1,0:T(8,128)(2,1)S(1)} %joined.3.refs_0_), channel_id=1, source_target_pairs={{0,8},{8,0},{1,9},{9,1},{2,10},{10,2},{3,11},{11,3},{4,12},{12,4},... | collective-permute-start | bytes 884744 | tf_op jit(solution)/shard_map/ppermute | solution.py:247
  46.7 19.2 %collective-permute-start.19 = (bf16[96,1536]{1,0:T(8,128)(2,1)S(1)}, bf16[96,1536]{1,0:T(8,128)(2,1)S(1)}, u32[]{:S(2)}, u32[]{:S(2)}) collective-permute-start(bf16[96,1536]{1,0:T(8,128)(2,1)S(1)} %joined.3.refs_0_), channel_id=1, source_target_pairs={{0,6},{2,0},{4,2},{6,4},{1,7},{3,1},{5,3},{7,5},{8,14},{10,8},{12,... | collective-permute-start | bytes 884744 | tf_op jit(solution)/shard_map/ppermute | solution.py:251
  49.4 5.0 %collective-permute-start.5 = (bf16[128,384]{1,0:T(8,128)(2,1)S(1)}, bf16[128,384]{1,0:T(8,128)(2,1)S(1)}, u32[]{:S(2)}, u32[]{:S(2)}) collective-permute-start(bf16[128,384]{1,0:T(8,128)(2,1)S(1)} %own_queries.1.refs_4_), channel_id=1, source_target_pairs={{0,4},{2,6},{4,0},{6,2},{1,5},{3,7},{5,1},{7,3},{8,12},{10,14},{12... | collective-permute-start | bytes 294920 | tf_op jit(solution)/shard_map/ppermute | solution.py:491
  54.4 4.6 %collective-permute-start.6 = (bf16[128,384]{1,0:T(8,128)(2,1)S(1)}, bf16[128,384]{1,0:T(8,128)(2,1)S(1)}, u32[]{:S(2)}, u32[]{:S(2)}) collective-permute-start(bf16[128,384]{1,0:T(8,128)(2,1)S(1)} %own_queries.1.refs_4_), channel_id=1, source_target_pairs={{0,6},{2,0},{4,2},{6,4},{1,7},{3,1},{5,3},{7,5},{8,14},{10,8},{12,... | collective-permute-start | bytes 294920 | tf_op jit(solution)/shard_map/ppermute | solution.py:491
  62.4 8.0 %collective-permute-start.7 = (bf16[128,512]{1,0:T(8,128)(2,1)S(1)}, bf16[128,512]{1,0:T(8,128)(2,1)S(1)}, u32[]{:S(2)}, u32[]{:S(2)}) collective-permute-start(bf16[128,512]{1,0:T(8,128)(2,1)S(1)} %get-tuple-element.34), channel_id=1, source_target_pairs={{0,6},{2,0},{4,2},{6,4},{1,7},{3,1},{5,3},{7,5},{8,14},{10,8},{12,... | collective-permute-start | bytes 393224 | tf_op jit(solution)/shard_map/ppermute | solution.py:493
  65.9 16.2 %collective-permute-start.18 = (bf16[96,1536]{1,0:T(8,128)(2,1)S(1)}, bf16[96,1536]{1,0:T(8,128)(2,1)S(1)}, u32[]{:S(2)}, u32[]{:S(2)}) collective-permute-start(bf16[96,1536]{1,0:T(8,128)(2,1)S(1)} %joined.3.refs_0_), channel_id=1, source_target_pairs={{0,2},{2,4},{4,6},{6,0},{1,3},{3,5},{5,7},{7,1},{8,10},{10,12},{12... | collective-permute-start | bytes 884744 | tf_op jit(solution)/shard_map/ppermute | solution.py:250
  65.9 22.4 %collective-permute-start.24 = (bf16[96,1536]{1,0:T(8,128)(2,1)S(1)}, bf16[96,1536]{1,0:T(8,128)(2,1)S(1)}, u32[]{:S(2)}, u32[]{:S(2)}) collective-permute-start(bf16[96,1536]{1,0:T(8,128)(2,1)S(1)} %joined.3.refs_0_), channel_id=1, source_target_pairs={{0,1},{1,0},{2,3},{3,2},{4,5},{5,4},{6,7},{7,6},{8,9},{9,8},{10,11... | collective-permute-start | bytes 884744 | tf_op jit(solution)/shard_map/ppermute | solution.py:255
  70.4 6.7 %collective-permute-start.8 = (bf16[128,512]{1,0:T(8,128)(2,1)S(1)}, bf16[128,512]{1,0:T(8,128)(2,1)S(1)}, u32[]{:S(2)}, u32[]{:S(2)}) collective-permute-start(bf16[128,512]{1,0:T(8,128)(2,1)S(1)} %get-tuple-element.35), channel_id=1, source_target_pairs={{0,4},{2,6},{4,0},{6,2},{1,5},{3,7},{5,1},{7,3},{8,12},{10,14},{12... | collective-permute-start | bytes 393224 | tf_op jit(solution)/shard_map/ppermute | solution.py:493
  71.9 8.7 %collective-permute-start.9 = (bf16[128,512]{1,0:T(8,128)(2,1)S(1)}, bf16[128,512]{1,0:T(8,128)(2,1)S(1)}, u32[]{:S(2)}, u32[]{:S(2)}) collective-permute-start(bf16[128,512]{1,0:T(8,128)(2,1)S(1)} %get-tuple-element.36), channel_id=1, source_target_pairs={{0,2},{2,4},{4,6},{6,0},{1,3},{3,5},{5,7},{7,1},{8,10},{10,12},{12... | collective-permute-start | bytes 393224 | tf_op jit(solution)/shard_map/ppermute | solution.py:493
  73.9 19.3 %collective-permute-start.20 = (bf16[96,1536]{1,0:T(8,128)(2,1)S(1)}, bf16[96,1536]{1,0:T(8,128)(2,1)S(1)}, u32[]{:S(2)}, u32[]{:S(2)}) collective-permute-start(bf16[96,1536]{1,0:T(8,128)(2,1)S(1)} %collective-permute-done.17.refs_1_), channel_id=1, source_target_pairs={{0,2},{2,4},{4,6},{6,0},{1,3},{3,5},{5,7},{7,1},{8,10},{10,12},{12... | collective-permute-start | bytes 884744 | tf_op jit(solution)/shard_map/ppermute | solution.py:250
  74.0 49.1 %slice-start.1 = ((s8[4718592]{0:T(1024)(128)(4,1)}), s8[524288]{0:T(1024)(128)(4,1)S(1)}, s32[]{:S(2)}) async-start(s8[4718592]{0:T(1024)(128)(4,1)} %bitcast.12), calls=%async_computation.1 | async-start | bytes 1048576
  74.1 49.0 %copy-start.3 = (bf16[1,32,1536]{2,1,0:T(8,128)(2,1)S(1)}, bf16[1,32,1536]{2,1,0:T(8,128)(2,1)}, u32[]{:S(2)}) copy-start(bf16[1,32,1536]{2,1,0:T(8,128)(2,1)} %param.14) | copy-start | bytes 294916
  74.1 49.0 %copy-start.4 = (f32[4,1536]{1,0:T(4,128)S(1)}, f32[4,1536]{1,0:T(4,128)}, u32[]{:S(2)}) copy-start(f32[4,1536]{1,0:T(4,128)} %gate_ref.1) | copy-start | bytes 73732
  77.1 16.4 %collective-permute-start.35 = (bf16[192,768]{1,0:T(8,128)(2,1)S(1)}, bf16[192,768]{1,0:T(8,128)(2,1)S(1)}, u32[]{:S(2)}, u32[]{:S(2)}) collective-permute-start(bf16[192,768]{1,0:T(8,128)(2,1)S(1)} %get-tuple-element.45), channel_id=1, source_target_pairs={{0,48},{48,0},{16,32},{32,16},{1,49},{49,1},{17,33},{33,17},{2,50}... | collective-permute-start | bytes 884744 | tf_op jit(solution)/shard_map/ppermute | solution.py:445
  80.7 13.0 %collective-permute-start.36 = (bf16[192,768]{1,0:T(8,128)(2,1)S(1)}, bf16[192,768]{1,0:T(8,128)(2,1)S(1)}, u32[]{:S(2)}, u32[]{:S(2)}) collective-permute-start(bf16[192,768]{1,0:T(8,128)(2,1)S(1)} %get-tuple-element.46), channel_id=1, source_target_pairs={{0,16},{16,0},{32,48},{48,32},{1,17},{17,1},{33,49},{49,33},{2,18}... | collective-permute-start | bytes 884744 | tf_op jit(solution)/shard_map/ppermute | solution.py:446
  82.2 7.7 %collective-permute-start.10 = (bf16[32,384]{1,0:T(8,128)(2,1)S(1)}, bf16[32,384]{1,0:T(8,128)(2,1)S(1)}, u32[]{:S(2)}, u32[]{:S(2)}) collective-permute-start(bf16[32,384]{1,0:T(8,128)(2,1)S(1)} %get-tuple-element.38), channel_id=1, source_target_pairs={{0,1},{1,0},{2,3},{3,2},{4,5},{5,4},{6,7},{7,6},{8,9},{9,8},{10,11... | collective-permute-start | bytes 73736 | tf_op jit(solution)/shard_map/ppermute | solution.py:498
  88.3 3.1 %collective-permute-start.11 = (bf16[32,384]{1,0:T(8,128)(2,1)S(1)}, bf16[32,384]{1,0:T(8,128)(2,1)S(1)}, u32[]{:S(2)}, u32[]{:S(2)}) collective-permute-start(bf16[32,384]{1,0:T(8,128)(2,1)S(1)} %get-tuple-element.39), channel_id=1, source_target_pairs={{0,8},{8,0},{1,9},{9,1},{2,10},{10,2},{3,11},{11,3},{4,12},{12,4},... | collective-permute-start | bytes 73736 | tf_op jit(solution)/shard_map/ppermute | solution.py:499
  89.9 3.3 %collective-permute-start.12 = (bf16[32,384]{1,0:T(8,128)(2,1)S(1)}, bf16[32,384]{1,0:T(8,128)(2,1)S(1)}, u32[]{:S(2)}, u32[]{:S(2)}) collective-permute-start(bf16[32,384]{1,0:T(8,128)(2,1)S(1)} %get-tuple-element.40), channel_id=1, source_target_pairs={{0,9},{9,0},{1,8},{8,1},{2,11},{11,2},{3,10},{10,3},{4,13},{13,4},... | collective-permute-start | bytes 73736 | tf_op jit(solution)/shard_map/ppermute | solution.py:500
  91.4 7.7 %collective-permute-start.21 = (bf16[96,1536]{1,0:T(8,128)(2,1)S(1)}, bf16[96,1536]{1,0:T(8,128)(2,1)S(1)}, u32[]{:S(2)}, u32[]{:S(2)}) collective-permute-start(bf16[96,1536]{1,0:T(8,128)(2,1)S(1)} %collective-permute-done.17.refs_1_), channel_id=1, source_target_pairs={{0,6},{2,0},{4,2},{6,4},{1,7},{3,1},{5,3},{7,5},{8,14},{10,8},{12,... | collective-permute-start | bytes 884744 | tf_op jit(solution)/shard_map/ppermute | solution.py:251
  93.2 12.3 %collective-permute-start.22 = (bf16[96,1536]{1,0:T(8,128)(2,1)S(1)}, bf16[96,1536]{1,0:T(8,128)(2,1)S(1)}, u32[]{:S(2)}, u32[]{:S(2)}) collective-permute-start(bf16[96,1536]{1,0:T(8,128)(2,1)S(1)} %collective-permute-done.19.refs_3_), channel_id=1, source_target_pairs={{0,6},{2,0},{4,2},{6,4},{1,7},{3,1},{5,3},{7,5},{8,14},{10,8},{12,... | collective-permute-start | bytes 884744 | tf_op jit(solution)/shard_map/ppermute | solution.py:252
  93.2 12.3 %collective-permute-start.25 = (bf16[96,1536]{1,0:T(8,128)(2,1)S(1)}, bf16[96,1536]{1,0:T(8,128)(2,1)S(1)}, u32[]{:S(2)}, u32[]{:S(2)}) collective-permute-start(bf16[96,1536]{1,0:T(8,128)(2,1)S(1)} %collective-permute-done.17.refs_1_), channel_id=1, source_target_pairs={{0,1},{1,0},{2,3},{3,2},{4,5},{5,4},{6,7},{7,6},{8,9},{9,8},{10,11... | collective-permute-start | bytes 884744 | tf_op jit(solution)/shard_map/ppermute | solution.py:255
  93.5 13.5 %collective-permute-start.27 = (bf16[96,1536]{1,0:T(8,128)(2,1)S(1)}, bf16[96,1536]{1,0:T(8,128)(2,1)S(1)}, u32[]{:S(2)}, u32[]{:S(2)}) collective-permute-start(bf16[96,1536]{1,0:T(8,128)(2,1)S(1)} %collective-permute-done.19.refs_3_), channel_id=1, source_target_pairs={{0,1},{1,0},{2,3},{3,2},{4,5},{5,4},{6,7},{7,6},{8,9},{9,8},{10,11... | collective-permute-start | bytes 884744 | tf_op jit(solution)/shard_map/ppermute | solution.py:255
  93.7 15.7 %collective-permute-start.23 = (bf16[96,1536]{1,0:T(8,128)(2,1)S(1)}, bf16[96,1536]{1,0:T(8,128)(2,1)S(1)}, u32[]{:S(2)}, u32[]{:S(2)}) collective-permute-start(bf16[96,1536]{1,0:T(8,128)(2,1)S(1)} %collective-permute-done.20.refs_4_), channel_id=1, source_target_pairs={{0,2},{2,4},{4,6},{6,0},{1,3},{3,5},{5,7},{7,1},{8,10},{10,12},{12... | collective-permute-start | bytes 884744 | tf_op jit(solution)/shard_map/ppermute | solution.py:253
  99.1 10.4 %collective-permute-start.37 = (bf16[2,24,1536]{2,1,0:T(8,128)(2,1)S(1)}, bf16[2,24,1536]{2,1,0:T(8,128)(2,1)S(1)}, u32[]{:S(2)}, u32[]{:S(2)}) collective-permute-start(bf16[2,24,1536]{2,1,0:T(8,128)(2,1)S(1)} %get-tuple-element.48), channel_id=1, source_target_pairs={{0,2},{2,4},{4,6},{6,0},{1,3},{3,5},{5,7},{7,1},{8,10},{10,12},{12... | collective-permute-start | bytes 442376 | tf_op jit(solution)/shard_map/ppermute | solution.py:448
  105.4 5.5 %collective-permute-start.38 = (bf16[2,24,1536]{2,1,0:T(8,128)(2,1)S(1)}, bf16[2,24,1536]{2,1,0:T(8,128)(2,1)S(1)}, u32[]{:S(2)}, u32[]{:S(2)}) collective-permute-start(bf16[2,24,1536]{2,1,0:T(8,128)(2,1)S(1)} %get-tuple-element.49), channel_id=1, source_target_pairs={{0,4},{2,6},{4,0},{6,2},{1,5},{3,7},{5,1},{7,3},{8,12},{10,14},{12... | collective-permute-start | bytes 442376 | tf_op jit(solution)/shard_map/ppermute | solution.py:448
  105.4 8.4 %collective-permute-start.39 = (bf16[2,24,1536]{2,1,0:T(8,128)(2,1)S(1)}, bf16[2,24,1536]{2,1,0:T(8,128)(2,1)S(1)}, u32[]{:S(2)}, u32[]{:S(2)}) collective-permute-start(bf16[2,24,1536]{2,1,0:T(8,128)(2,1)S(1)} %get-tuple-element.50), channel_id=1, source_target_pairs={{0,6},{2,0},{4,2},{6,4},{1,7},{3,1},{5,3},{7,5},{8,14},{10,8},{12,... | collective-permute-start | bytes 442376 | tf_op jit(solution)/shard_map/ppermute | solution.py:448
  107.1 9.1 %collective-permute-start.26 = (bf16[96,1536]{1,0:T(8,128)(2,1)S(1)}, bf16[96,1536]{1,0:T(8,128)(2,1)S(1)}, u32[]{:S(2)}, u32[]{:S(2)}) collective-permute-start(bf16[96,1536]{1,0:T(8,128)(2,1)S(1)} %collective-permute-done.18.refs_2_), channel_id=1, source_target_pairs={{0,1},{1,0},{2,3},{3,2},{4,5},{5,4},{6,7},{7,6},{8,9},{9,8},{10,11... | collective-permute-start | bytes 884744 | tf_op jit(solution)/shard_map/ppermute | solution.py:255
  109.4 12.2 %collective-permute-start.28 = (bf16[96,1536]{1,0:T(8,128)(2,1)S(1)}, bf16[96,1536]{1,0:T(8,128)(2,1)S(1)}, u32[]{:S(2)}, u32[]{:S(2)}) collective-permute-start(bf16[96,1536]{1,0:T(8,128)(2,1)S(1)} %collective-permute-done.20.refs_4_), channel_id=1, source_target_pairs={{0,1},{1,0},{2,3},{3,2},{4,5},{5,4},{6,7},{7,6},{8,9},{9,8},{10,11... | collective-permute-start | bytes 884744 | tf_op jit(solution)/shard_map/ppermute | solution.py:255
  109.5 12.2 %collective-permute-start.29 = (bf16[96,1536]{1,0:T(8,128)(2,1)S(1)}, bf16[96,1536]{1,0:T(8,128)(2,1)S(1)}, u32[]{:S(2)}, u32[]{:S(2)}) collective-permute-start(bf16[96,1536]{1,0:T(8,128)(2,1)S(1)} %collective-permute-done.21.refs_5_), channel_id=1, source_target_pairs={{0,1},{1,0},{2,3},{3,2},{4,5},{5,4},{6,7},{7,6},{8,9},{9,8},{10,11... | collective-permute-start | bytes 884744 | tf_op jit(solution)/shard_map/ppermute | solution.py:255
  110.9 11.4 %collective-permute-start.30 = (bf16[96,1536]{1,0:T(8,128)(2,1)S(1)}, bf16[96,1536]{1,0:T(8,128)(2,1)S(1)}, u32[]{:S(2)}, u32[]{:S(2)}) collective-permute-start(bf16[96,1536]{1,0:T(8,128)(2,1)S(1)} %collective-permute-done.22.refs_6_), channel_id=1, source_target_pairs={{0,1},{1,0},{2,3},{3,2},{4,5},{5,4},{6,7},{7,6},{8,9},{9,8},{10,11... | collective-permute-start | bytes 884744 | tf_op jit(solution)/shard_map/ppermute | solution.py:255
  113.8 11.5 %collective-permute-start.31 = (bf16[96,1536]{1,0:T(8,128)(2,1)S(1)}, bf16[96,1536]{1,0:T(8,128)(2,1)S(1)}, u32[]{:S(2)}, u32[]{:S(2)}) collective-permute-start(bf16[96,1536]{1,0:T(8,128)(2,1)S(1)} %collective-permute-done.23.refs_7_), channel_id=1, source_target_pairs={{0,1},{1,0},{2,3},{3,2},{4,5},{5,4},{6,7},{7,6},{8,9},{9,8},{10,11... | collective-permute-start | bytes 884744 | tf_op jit(solution)/shard_map/ppermute | solution.py:255
  116.2 18.3 %collective-permute-start.40 = (f32[12,1536]{1,0:T(8,128)S(1)}, f32[12,1536]{1,0:T(8,128)S(1)}, u32[]{:S(2)}, u32[]{:S(2)}) collective-permute-start(f32[12,1536]{1,0:T(8,128)S(1)} %get-tuple-element.51), channel_id=1, source_target_pairs={{0,0},{1,64},{8,8},{9,72},{64,1},{65,65},{72,9},{73,73},{2,2},{3,6... | collective-permute-start | bytes 221192 | tf_op jit(solution)/shard_map/ppermute | solution.py:455
  121.6 12.9 %collective-permute-start.41 = (f32[12,1536]{1,0:T(8,128)S(1)}, f32[12,1536]{1,0:T(8,128)S(1)}, u32[]{:S(2)}, u32[]{:S(2)}) collective-permute-start(f32[12,1536]{1,0:T(8,128)S(1)} %get-tuple-element.52), channel_id=1, source_target_pairs={{0,1},{1,65},{8,9},{9,73},{64,0},{65,64},{72,8},{73,72},{2,3},{3,6... | collective-permute-start | bytes 221192 | tf_op jit(solution)/shard_map/ppermute | solution.py:455
  121.7 12.8 %collective-permute-start.42 = (f32[12,1536]{1,0:T(8,128)S(1)}, f32[12,1536]{1,0:T(8,128)S(1)}, u32[]{:S(2)}, u32[]{:S(2)}) collective-permute-start(f32[12,1536]{1,0:T(8,128)S(1)} %get-tuple-element.53), channel_id=1, source_target_pairs={{0,8},{1,72},{8,0},{9,64},{64,9},{65,73},{72,1},{73,65},{2,10},{3,... | collective-permute-start | bytes 221192 | tf_op jit(solution)/shard_map/ppermute | solution.py:455
  122.3 12.2 %collective-permute-start.43 = (f32[12,1536]{1,0:T(8,128)S(1)}, f32[12,1536]{1,0:T(8,128)S(1)}, u32[]{:S(2)}, u32[]{:S(2)}) collective-permute-start(f32[12,1536]{1,0:T(8,128)S(1)} %get-tuple-element.54), channel_id=1, source_target_pairs={{0,9},{1,73},{8,1},{9,65},{64,8},{65,72},{72,0},{73,64},{2,11},{3,... | collective-permute-start | bytes 221192 | tf_op jit(solution)/shard_map/ppermute | solution.py:455

commit v2 on v1

--- a/solution.py
+++ b/solution.py
@@ -222,7 +222,7 @@
     )(place, cot, *[in_vmem(p) for _, p in pieces])
 
 
-def joined(arrays):
+def joined(arrays, first_in_vmem=False):
     rows = [a.shape[0] for a in arrays]
 
     def kernel(*refs):
@@ -231,19 +231,20 @@
             out_ref[at : at + n, :] = ref[...]
             at += n
 
-    return pl.pallas_call(
-        kernel,
-        out_shape=jax.ShapeDtypeStruct((sum(rows), arrays[0].shape[1]), arrays[0].dtype),
+    place_first = in_vmem if first_in_vmem else in_hbm
+    return pl.pallas_call(
+        kernel,
+        out_shape=pltpu.VMEM((sum(rows), arrays[0].shape[1]), arrays[0].dtype),
         compiler_params=room(),
         name="joined",
-    )(in_hbm(arrays[0]), *[in_vmem(a) for a in arrays[1:]])
+    )(place_first(arrays[0]), *[in_vmem(a) for a in arrays[1:]])
 
 
 def weight_pieces(weight):
     on_x = [weight] + [lax.ppermute(weight, "x", turn(k)) for k in (1, 2, 3)]
     on_x = joined(on_x)
     far = lax.ppermute(on_x, "zh", SWAP)
-    near = joined([on_x, far])
+    near = joined([on_x, far], True)
     far = lax.ppermute(near, "zl", SWAP)
     pieces = {(0, 0): near, (1, 0): far}
     for f in range(2):
@@ -263,7 +264,7 @@
 
     return pl.pallas_call(
         kernel,
-        out_shape=jax.ShapeDtypeStruct((128, 3 * HEAD), BF),
+        out_shape=pltpu.VMEM((128, 3 * HEAD), BF),
         compiler_params=room(),
         name="own_queries",
     )(*[in_vmem(a) for a in sets])
@@ -284,12 +285,12 @@
         kernel,
         grid_spec=pltpu.PrefetchScalarGridSpec(
             num_scalar_prefetch=1,
-            grid=(2,),
+            grid=(4,),
             in_specs=[
-                pl.BlockSpec((tokens, width // 4), lambda p, place: (0, 2 * (1 - place[2]) + p)),
-                pl.BlockSpec((tokens, width), lambda p, place: (0, 0)),
+                pl.BlockSpec((tokens, width // 2), lambda p, place: (0, 1 - place[2])),
+                pl.BlockSpec((tokens, width // 4), lambda p, place: (0, p)),
             ],
-            out_specs=pl.BlockSpec((width // 4, width), lambda p, place: (p, 0)),
+            out_specs=pl.BlockSpec((width // 2, width // 4), lambda p, place: (0, p)),
         ),
         out_shape=jax.ShapeDtypeStruct((width // 2, width), BF),
         compiler_params=room(32, dimension_semantics=("arbitrary",)),

time: 136 us -> 138 us (1.015)
  starting transfers between devices: 62.4 us -> 64 us
    pallas_call x1, Pallas kernels: 4.88 us -> 6.83 us  [product_to_send(): pl.pallas_call(kernel, grid_spec=pltpu.PrefetchScalarGridSpec(num_scalar_...]
  transfers between devices with their start and end apart: 44 -> 44, of which waited for: 12 -> 11; matrix products, arithmetic and copies ran while one was open for 0% -> 0% of each run, Pallas kernels for 18% -> 17%
where the time goes in v2:
time: 138 us; the launch traced here: 137 us
  starting transfers between devices  64 us (46%)
  waiting for transfers between devices  37.7 us (27%)
  Pallas kernels  31.3 us (23%)
  between operations  2.23 us (2%)
  local copies, waits for them, and re-layouts  2.01 us (1%)
    ppermute x3, waiting for transfers between devices, weight_pieces(): on_x = [weight] + [lax.ppermute(weight, 'x', turn(k)) for k in (1, 2, 3)]  13.5 us
    ppermute x8, starting transfers between devices, weight_pieces(): lax.ppermute(p, 'c', SWAP)  12.8 us
    pallas_call x1, Pallas kernels, grad_of_input(): pl.pallas_call(kernel, grid=(rows // block,), out_shape=jax.ShapeDtypeStr...  9.19 us
    ppermute x3, waiting for transfers between devices, step(): all_queries = [own] + [lax.ppermute(own, 'y', turn(k)) for k in (1, 2, 3)]  6.96 us
    ppermute x3, starting transfers between devices, step(): lax.ppermute(partial[k], 'y', turn(-k))  6.93 us
    pallas_call x1, Pallas kernels, product_to_send(): pl.pallas_call(kernel, grid_spec=pltpu.PrefetchScalarGridSpec(num_scalar_...  6.83 us
    ppermute x1, waiting for transfers between devices, weight_pieces(): pieces[0, 2] = lax.ppermute(pieces[0, 1], 'y', turn(-1))  6.32 us
    ppermute x1, starting transfers between devices, step(): lax.ppermute(mixed[1], 'c', SWAP)  6.25 us
  transfers between devices with their start and end apart: 44, of which 11 were waited for; matrix products, arithmetic and copies ran while one was open for 0% of the time, Pallas kernels for 17%

profile of v2, /device:TPU:1, one launch (start us, length us, event | category | flops | bytes accessed | tf_op | source)
XLA Modules:
  0.0 137.2 jit_solution(5092008374920426980)
XLA Ops:
  0.6 0.1 stack.23.place_ref
  0.7 1.9 %copy-done = bf16[1024,1536]{1,0:T(8,128)(2,1)S(1)} copy-done((bf16[1024,1536]{1,0:T(8,128)(2,1)S(1)}, bf16[1024,1536]{1,0:T(8,128)(2,1)}, u32[]{:S(2)}) %copy-start) | copy-done | bytes 3145752
  2.6 6.8 %product_to_send.1 = bf16[768,1536]{1,0:T(8,128)(2,1)S(1)} custom-call(s32[5]{0:T(128)S(1)} %stack.23.place_ref, bf16[1024,1536]{1,0:T(8,128)(2,1)} %in_ref.3, bf16[1024,1536]{1,0:T(8,128)(2,1)S(1)} %copy-done), custom_call_target="tpu_custom_call" | custom-call | tf_op jit(solution)/shard_map/product_to_send/pallas_call | solution.py:284
  9.5 1.5 %collective-permute-start.32 = (bf16[768,1536]{1,0:T(8,128)(2,1)S(1)}, bf16[768,1536]{1,0:T(8,128)(2,1)S(1)}, u32[]{:S(2)}, u32[]{:S(2)}) collective-permute-start(bf16[768,1536]{1,0:T(8,128)(2,1)S(1)} %product_to_send.1), channel_id=1, source_target_pairs={{0,1},{1,0},{2,3},{3,2},{4,5},{5,4},{6,7},{7,6},{8,9},{9,8},{10,11... | collective-permute-start | bytes 7077896 | tf_op jit(solution)/shard_map/ppermute | solution.py:439
  11.6 1.3 packed.1
  12.9 0.1 collective-permute-start.2
  13.0 0.5 collective-permute-start
  13.5 1.7 %collective-permute-start.1 = (bf16[304,384]{1,0:T(8,128)(2,1)S(1)}, bf16[304,384]{1,0:T(8,128)(2,1)S(1)}, u32[]{:S(2)}, u32[]{:S(2)}) collective-permute-start(bf16[304,384]{1,0:T(8,128)(2,1)S(1)} %get-tuple-element.31), channel_id=1, source_target_pairs={{0,8},{8,0},{1,9},{9,1},{2,10},{10,2},{3,11},{11,3},{4,12},{12,4},... | collective-permute-start | bytes 700424 | tf_op jit(solution)/shard_map/ppermute | solution.py:484
  15.2 0.2 collective-permute-done.2
  15.4 1.7 %collective-permute-start.3 = (bf16[304,384]{1,0:T(8,128)(2,1)S(1)}, bf16[304,384]{1,0:T(8,128)(2,1)S(1)}, u32[]{:S(2)}, u32[]{:S(2)}) collective-permute-start(bf16[304,384]{1,0:T(8,128)(2,1)S(1)} %collective-permute-done.2), channel_id=1, source_target_pairs={{0,8},{8,0},{1,9},{9,1},{2,10},{10,2},{3,11},{11,3},{4,12},{12,4},... | collective-permute-start | bytes 700424 | tf_op jit(solution)/shard_map/ppermute | solution.py:485
  17.2 1.2 collective-permute-start.13
  18.4 2.4 %collective-permute-start.14 = (bf16[12,1536]{1,0:T(8,128)(2,1)S(1)}, bf16[12,1536]{1,0:T(8,128)(2,1)S(1)}, u32[]{:S(2)}, u32[]{:S(2)}) collective-permute-start(bf16[12,1536]{1,0:T(8,128)(2,1)S(1)} %copy-done.5), channel_id=1, source_target_pairs={{0,32},{16,48},{32,0},{48,16},{1,33},{17,49},{33,1},{49,17},{2,34}... | collective-permute-start | bytes 110600 | tf_op jit(solution)/shard_map/ppermute | solution.py:244
  20.8 4.9 %product_and_split.1 = (bf16[2,192,768]{2,1,0:T(8,128)(2,1)S(1)}, bf16[2,192,768]{2,1,0:T(8,128)(2,1)S(1)}, f32[2,192,768]{2,1,0:T(8,128)S(1)}, f32[2,192,768]{2,1,0:T(8,128)S(1)}) custom-call(s32[5]{0:T(128)S(1)} %stack.23.place_ref, bf16[1024,1536]{1,0:T(8,128)(2,1)} %in_ref.3, bf16[1024,1536]{1,0:T(8,128)(2,1)S(1)} %copy-done.1, ...), custom_call_target="tpu_custom_call" | custom-call | tf_op jit(solution)/shard_map/product_and_split/pallas_call | solution.py:335
  25.8 0.1 collective-permute-start.33
  25.9 1.2 collective-permute-start.15
  27.1 13.5 %collective-permute-done.15.refs_3_ = bf16[12,1536]{1,0:T(8,128)(2,1)S(1)} collective-permute-done((bf16[12,1536]{1,0:T(8,128)(2,1)S(1)}, bf16[12,1536]{1,0:T(8,128)(2,1)S(1)}, u32[]{:S(2)}, u32[]{:S(2)}) %collective-permute-start.15) | collective-permute-done | bytes 36896 | tf_op jit(solution)/shard_map/ppermute | solution.py:244
  40.6 0.8 joined.2.refs_0_
  41.4 3.4 %collective-permute-start.16 = (bf16[48,1536]{1,0:T(8,128)(2,1)S(1)}, bf16[48,1536]{1,0:T(8,128)(2,1)S(1)}, u32[]{:S(2)}, u32[]{:S(2)}) collective-permute-start(bf16[48,1536]{1,0:T(8,128)(2,1)S(1)} %joined.2.refs_0_), channel_id=1, source_target_pairs={{0,64},{64,0},{1,65},{65,1},{2,66},{66,2},{3,67},{67,3},{4,68},{68... | collective-permute-start | bytes 442376 | tf_op jit(solution)/shard_map/ppermute | solution.py:246
  44.8 1.4 collective-permute-start.4
  46.2 1.1 collective-permute-done.16.refs_1_
  47.4 0.2 collective-permute-start.17
  47.6 2.7 %collective-permute-start.19 = (bf16[96,1536]{1,0:T(8,128)(2,1)S(1)}, bf16[96,1536]{1,0:T(8,128)(2,1)S(1)}, u32[]{:S(2)}, u32[]{:S(2)}) collective-permute-start(bf16[96,1536]{1,0:T(8,128)(2,1)S(1)} %joined.3.refs_0_), channel_id=1, source_target_pairs={{0,6},{2,0},{4,2},{6,4},{1,7},{3,1},{5,3},{7,5},{8,14},{10,8},{12,... | collective-permute-start | bytes 884744 | tf_op jit(solution)/shard_map/ppermute | solution.py:252
  50.3 1.3 collective-permute-start.5
  51.6 3.7 %collective-permute-done.5.refs_6_ = bf16[128,384]{1,0:T(8,128)(2,1)S(1)} collective-permute-done((bf16[128,384]{1,0:T(8,128)(2,1)S(1)}, bf16[128,384]{1,0:T(8,128)(2,1)S(1)}, u32[]{:S(2)}, u32[]{:S(2)}) %collective-permute-start.5) | collective-permute-done | bytes 98336 | tf_op jit(solution)/shard_map/ppermute | solution.py:492
  55.3 1.4 %collective-permute-start.6 = (bf16[128,384]{1,0:T(8,128)(2,1)S(1)}, bf16[128,384]{1,0:T(8,128)(2,1)S(1)}, u32[]{:S(2)}, u32[]{:S(2)}) collective-permute-start(bf16[128,384]{1,0:T(8,128)(2,1)S(1)} %own_queries.1.refs_4_), channel_id=1, source_target_pairs={{0,6},{2,0},{4,2},{6,4},{1,7},{3,1},{5,3},{7,5},{8,14},{10,8},{12,... | collective-permute-start | bytes 294920 | tf_op jit(solution)/shard_map/ppermute | solution.py:492
  56.7 3.2 %collective-permute-done.6.refs_7_ = bf16[128,384]{1,0:T(8,128)(2,1)S(1)} collective-permute-done((bf16[128,384]{1,0:T(8,128)(2,1)S(1)}, bf16[128,384]{1,0:T(8,128)(2,1)S(1)}, u32[]{:S(2)}, u32[]{:S(2)}) %collective-permute-start.6) | collective-permute-done | bytes 98336 | tf_op jit(solution)/shard_map/ppermute | solution.py:492
  60.0 3.4 %attend.1 = (bf16[128,512]{1,0:T(8,128)(2,1)S(1)}, bf16[128,512]{1,0:T(8,128)(2,1)S(1)}, bf16[128,512]{1,0:T(8,128)(2,1)S(1)}, bf16[128,512]{1,0:T(8,128)(2,1)S(1)}) custom-call(bf16[304,384]{1,0:T(8,128)(2,1)S(1)} %get-tuple-element.29.refs_0_, bf16[304,384]{1,0:T(8,128)(2,1)S(1)} %collective-permute-done.refs_1_, ...), custom_call_target="tpu_custom_call" | custom-call | tf_op jit(solution)/shard_map/attend/pallas_call | solution.py:112
  63.3 3.5 %collective-permute-start.7 = (bf16[128,512]{1,0:T(8,128)(2,1)S(1)}, bf16[128,512]{1,0:T(8,128)(2,1)S(1)}, u32[]{:S(2)}, u32[]{:S(2)}) collective-permute-start(bf16[128,512]{1,0:T(8,128)(2,1)S(1)} %get-tuple-element.34), channel_id=1, source_target_pairs={{0,6},{2,0},{4,2},{6,4},{1,7},{3,1},{5,3},{7,5},{8,14},{10,8},{12,... | collective-permute-start | bytes 393224 | tf_op jit(solution)/shard_map/ppermute | solution.py:494
  66.8 5.1 %collective-permute-start.24 = (bf16[96,1536]{1,0:T(8,128)(2,1)S(1)}, bf16[96,1536]{1,0:T(8,128)(2,1)S(1)}, u32[]{:S(2)}, u32[]{:S(2)}) collective-permute-start(bf16[96,1536]{1,0:T(8,128)(2,1)S(1)} %joined.3.refs_0_), channel_id=1, source_target_pairs={{0,1},{1,0},{2,3},{3,2},{4,5},{5,4},{6,7},{7,6},{8,9},{9,8},{10,11... | collective-permute-start | bytes 884744 | tf_op jit(solution)/shard_map/ppermute | solution.py:256
  71.9 1.2 collective-permute-start.8
  73.1 2.3 %collective-permute-start.9 = (bf16[128,512]{1,0:T(8,128)(2,1)S(1)}, bf16[128,512]{1,0:T(8,128)(2,1)S(1)}, u32[]{:S(2)}, u32[]{:S(2)}) collective-permute-start(bf16[128,512]{1,0:T(8,128)(2,1)S(1)} %get-tuple-element.36), channel_id=1, source_target_pairs={{0,2},{2,4},{4,6},{6,0},{1,3},{3,5},{5,7},{7,1},{8,10},{10,12},{12... | collective-permute-start | bytes 393224 | tf_op jit(solution)/shard_map/ppermute | solution.py:494
  75.4 0.1 collective-permute-start.20
  75.5 0.1 onward.1
  75.6 0.0 copy-start.3
  75.6 3.1 %collective-permute-done.8.refs_2_ = bf16[128,512]{1,0:T(8,128)(2,1)S(1)} collective-permute-done((bf16[128,512]{1,0:T(8,128)(2,1)S(1)}, bf16[128,512]{1,0:T(8,128)(2,1)S(1)}, u32[]{:S(2)}, u32[]{:S(2)}) %collective-permute-start.8) | collective-permute-done | bytes 131104 | tf_op jit(solution)/shard_map/ppermute | solution.py:494
  78.7 3.6 %collective-permute-start.35 = (bf16[192,768]{1,0:T(8,128)(2,1)S(1)}, bf16[192,768]{1,0:T(8,128)(2,1)S(1)}, u32[]{:S(2)}, u32[]{:S(2)}) collective-permute-start(bf16[192,768]{1,0:T(8,128)(2,1)S(1)} %get-tuple-element.45), channel_id=1, source_target_pairs={{0,48},{48,0},{16,32},{32,16},{1,49},{49,1},{17,33},{33,17},{2,50}... | collective-permute-start | bytes 884744 | tf_op jit(solution)/shard_map/ppermute | solution.py:446
  82.3 1.1 collective-permute-start.36
  83.3 0.5 merged.1
  83.8 6.2 %collective-permute-start.10 = (bf16[32,384]{1,0:T(8,128)(2,1)S(1)}, bf16[32,384]{1,0:T(8,128)(2,1)S(1)}, u32[]{:S(2)}, u32[]{:S(2)}) collective-permute-start(bf16[32,384]{1,0:T(8,128)(2,1)S(1)} %get-tuple-element.38), channel_id=1, source_target_pairs={{0,1},{1,0},{2,3},{3,2},{4,5},{5,4},{6,7},{7,6},{8,9},{9,8},{10,11... | collective-permute-start | bytes 73736 | tf_op jit(solution)/shard_map/ppermute | solution.py:499
  90.1 1.9 %collective-permute-start.11 = (bf16[32,384]{1,0:T(8,128)(2,1)S(1)}, bf16[32,384]{1,0:T(8,128)(2,1)S(1)}, u32[]{:S(2)}, u32[]{:S(2)}) collective-permute-start(bf16[32,384]{1,0:T(8,128)(2,1)S(1)} %get-tuple-element.39), channel_id=1, source_target_pairs={{0,8},{8,0},{1,9},{9,1},{2,10},{10,2},{3,11},{11,3},{4,12},{12,4},... | collective-permute-start | bytes 73736 | tf_op jit(solution)/shard_map/ppermute | solution.py:500
  92.0 1.1 collective-permute-start.12
  93.0 0.4 collective-permute-done.11.c_ref
  93.5 1.7 %collective-permute-done.12.d_ref = bf16[32,384]{1,0:T(8,128)(2,1)S(1)} collective-permute-done((bf16[32,384]{1,0:T(8,128)(2,1)S(1)}, bf16[32,384]{1,0:T(8,128)(2,1)S(1)}, u32[]{:S(2)}, u32[]{:S(2)}) %collective-permute-start.12) | collective-permute-done | bytes 24608 | tf_op jit(solution)/shard_map/ppermute | solution.py:501
  95.2 0.4 collective-permute-start.25
  95.6 0.1 collective-permute-start.27
  95.8 1.7 %collective-permute-start.23 = (bf16[96,1536]{1,0:T(8,128)(2,1)S(1)}, bf16[96,1536]{1,0:T(8,128)(2,1)S(1)}, u32[]{:S(2)}, u32[]{:S(2)}) collective-permute-start(bf16[96,1536]{1,0:T(8,128)(2,1)S(1)} %collective-permute-done.20.refs_4_), channel_id=1, source_target_pairs={{0,2},{2,4},{4,6},{6,0},{1,3},{3,5},{5,7},{7,1},{8,10},{10,12},{12... | collective-permute-start | bytes 884744 | tf_op jit(solution)/shard_map/ppermute | solution.py:254
  97.5 0.8 cut_along_y.1
  98.3 3.1 %collective-permute-done.21.refs_5_ = bf16[96,1536]{1,0:T(8,128)(2,1)S(1)} collective-permute-done((bf16[96,1536]{1,0:T(8,128)(2,1)S(1)}, bf16[96,1536]{1,0:T(8,128)(2,1)S(1)}, u32[]{:S(2)}, u32[]{:S(2)}) %collective-permute-start.21) | collective-permute-done | bytes 294944 | tf_op jit(solution)/shard_map/ppermute | solution.py:252
  101.4 6.3 %collective-permute-done.22.refs_6_ = bf16[96,1536]{1,0:T(8,128)(2,1)S(1)} collective-permute-done((bf16[96,1536]{1,0:T(8,128)(2,1)S(1)}, bf16[96,1536]{1,0:T(8,128)(2,1)S(1)}, u32[]{:S(2)}, u32[]{:S(2)}) %collective-permute-start.22) | collective-permute-done | bytes 294944 | tf_op jit(solution)/shard_map/ppermute | solution.py:253
  107.7 1.7 %collective-permute-start.39 = (bf16[2,24,1536]{2,1,0:T(8,128)(2,1)S(1)}, bf16[2,24,1536]{2,1,0:T(8,128)(2,1)S(1)}, u32[]{:S(2)}, u32[]{:S(2)}) collective-permute-start(bf16[2,24,1536]{2,1,0:T(8,128)(2,1)S(1)} %get-tuple-element.50), channel_id=1, source_target_pairs={{0,6},{2,0},{4,2},{6,4},{1,7},{3,1},{5,3},{7,5},{8,14},{10,8},{12,... | collective-permute-start | bytes 442376 | tf_op jit(solution)/shard_map/ppermute | solution.py:449
  109.4 2.1 %collective-permute-start.26 = (bf16[96,1536]{1,0:T(8,128)(2,1)S(1)}, bf16[96,1536]{1,0:T(8,128)(2,1)S(1)}, u32[]{:S(2)}, u32[]{:S(2)}) collective-permute-start(bf16[96,1536]{1,0:T(8,128)(2,1)S(1)} %collective-permute-done.18.refs_2_), channel_id=1, source_target_pairs={{0,1},{1,0},{2,3},{3,2},{4,5},{5,4},{6,7},{7,6},{8,9},{9,8},{10,11... | collective-permute-start | bytes 884744 | tf_op jit(solution)/shard_map/ppermute | solution.py:256
  111.5 0.1 collective-permute-start.28
  111.5 0.4 collective-permute-start.29
  112.0 1.2 collective-permute-done.38.b
  113.2 2.7 %collective-permute-start.30 = (bf16[96,1536]{1,0:T(8,128)(2,1)S(1)}, bf16[96,1536]{1,0:T(8,128)(2,1)S(1)}, u32[]{:S(2)}, u32[]{:S(2)}) collective-permute-start(bf16[96,1536]{1,0:T(8,128)(2,1)S(1)} %collective-permute-done.22.refs_6_), channel_id=1, source_target_pairs={{0,1},{1,0},{2,3},{3,2},{4,5},{5,4},{6,7},{7,6},{8,9},{9,8},{10,11... | collective-permute-start | bytes 884744 | tf_op jit(solution)/shard_map/ppermute | solution.py:256
  115.9 1.9 %collective-permute-start.31 = (bf16[96,1536]{1,0:T(8,128)(2,1)S(1)}, bf16[96,1536]{1,0:T(8,128)(2,1)S(1)}, u32[]{:S(2)}, u32[]{:S(2)}) collective-permute-start(bf16[96,1536]{1,0:T(8,128)(2,1)S(1)} %collective-permute-done.23.refs_7_), channel_id=1, source_target_pairs={{0,1},{1,0},{2,3},{3,2},{4,5},{5,4},{6,7},{7,6},{8,9},{9,8},{10,11... | collective-permute-start | bytes 884744 | tf_op jit(solution)/shard_map/ppermute | solution.py:256
  117.8 0.6 cut_to_owners.1
  118.4 5.4 %collective-permute-start.40 = (f32[12,1536]{1,0:T(8,128)S(1)}, f32[12,1536]{1,0:T(8,128)S(1)}, u32[]{:S(2)}, u32[]{:S(2)}) collective-permute-start(f32[12,1536]{1,0:T(8,128)S(1)} %get-tuple-element.51), channel_id=1, source_target_pairs={{0,0},{1,64},{8,8},{9,72},{64,1},{65,65},{72,9},{73,73},{2,2},{3,6... | collective-permute-start | bytes 221192 | tf_op jit(solution)/shard_map/ppermute | solution.py:456
  123.9 0.1 collective-permute-start.41
  124.0 0.4 collective-permute-start.42
  124.4 0.1 collective-permute-start.43
  125.2 2.1 %streamed.1 = bf16[32,1536]{1,0:T(8,128)(2,1)} custom-call(s32[5]{0:T(128)S(1)} %stack.23.place_ref, s32[1]{0:T(128)S(6)} %copy.18.step_ref, bf16[32,1536]{1,0:T(8,128)(2,1)S(1)} %bitcast.14, f32[4,1536]{1,0:T(4,128)S(1)} %copy-done.3, bf16[32,384]{1,0:T(8,128)(2,1)S(1)} %get-tuple-element.37.a_ref, bf16[32,384]{1,0:T(8,128)(2,1)S(1)} %collective-permute-done.10.b_ref, ...), custom_call_target="tpu_custom_call" | custom-call | tf_op jit(solution)/shard_map/streamed/pallas_call | solution.py:163
  127.3 9.2 %grad_of_input.1 = bf16[1024,1536]{1,0:T(8,128)(2,1)} custom-call(s32[5]{0:T(128)S(1)} %stack.23.place_ref, bf16[1024,1536]{1,0:T(8,128)(2,1)S(1)} %copy-done.1, bf16[96,1536]{1,0:T(8,128)(2,1)S(1)} %joined.3.refs_0_, bf16[96,1536]{1,0:T(8,128)(2,1)S(1)} %collective-permute-done.17.refs_1_, bf16[96,1536]{1,0:T(8,128)(2,1)S(1)} %collective-permute-done.18.refs_2_, ...), custom_call_target="tpu_custom_call" | custom-call | tf_op jit(solution)/shard_map/grad_of_input/pallas_call | solution.py:209
  136.6 0.7 added.1
  (56 shorter events, 0.2 us)
Async XLA Ops:
  0.7 1.9 %copy-start = (bf16[1024,1536]{1,0:T(8,128)(2,1)S(1)}, bf16[1024,1536]{1,0:T(8,128)(2,1)}, u32[]{:S(2)}) copy-start(bf16[1024,1536]{1,0:T(8,128)(2,1)} %cot_ref.5) | copy-start | bytes 9437188
  2.6 9.0 %copy-start.4 = (s32[1,96]{1,0:T(1,128)S(1)}, s32[1,96]{1,0:T(1,128)}, u32[]{:S(2)}) copy-start(s32[1,96]{1,0:T(1,128)} %frames_ref.1) | copy-start | bytes 1156
  2.6 14.6 %copy-start.5 = (bf16[12,1536]{1,0:T(8,128)(2,1)S(1)}, bf16[12,1536]{1,0:T(8,128)(2,1)}, u32[]{:S(2)}) copy-start(bf16[12,1536]{1,0:T(8,128)(2,1)} %refs_0_.1) | copy-start | bytes 110596
  2.6 18.2 %copy-start.1 = (bf16[1024,1536]{1,0:T(8,128)(2,1)S(1)}, bf16[1024,1536]{1,0:T(8,128)(2,1)}, u32[]{:S(2)}) copy-start(bf16[1024,1536]{1,0:T(8,128)(2,1)} %cot_ref.5) | copy-start | bytes 9437188
  9.5 8.9 %collective-permute-start.32 = (bf16[768,1536]{1,0:T(8,128)(2,1)S(1)}, bf16[768,1536]{1,0:T(8,128)(2,1)S(1)}, u32[]{:S(2)}, u32[]{:S(2)}) collective-permute-start(bf16[768,1536]{1,0:T(8,128)(2,1)S(1)} %product_to_send.1), channel_id=1, source_target_pairs={{0,1},{1,0},{2,3},{3,2},{4,5},{5,4},{6,7},{7,6},{8,9},{9,8},{10,11... | collective-permute-start | bytes 7077896 | tf_op jit(solution)/shard_map/ppermute | solution.py:439
  12.9 2.5 %collective-permute-start.2 = (bf16[304,384]{1,0:T(8,128)(2,1)S(1)}, bf16[304,384]{1,0:T(8,128)(2,1)S(1)}, u32[]{:S(2)}, u32[]{:S(2)}) collective-permute-start(bf16[304,384]{1,0:T(8,128)(2,1)S(1)} %get-tuple-element.32), channel_id=1, source_target_pairs={{0,1},{1,0},{2,3},{3,2},{4,5},{5,4},{6,7},{7,6},{8,9},{9,8},{10,11... | collective-permute-start | bytes 700424 | tf_op jit(solution)/shard_map/ppermute | solution.py:485
  13.0 28.5 %collective-permute-start = (bf16[304,384]{1,0:T(8,128)(2,1)S(1)}, bf16[304,384]{1,0:T(8,128)(2,1)S(1)}, u32[]{:S(2)}, u32[]{:S(2)}) collective-permute-start(bf16[304,384]{1,0:T(8,128)(2,1)S(1)} %get-tuple-element.30), channel_id=1, source_target_pairs={{0,1},{1,0},{2,3},{3,2},{4,5},{5,4},{6,7},{7,6},{8,9},{9,8},{10,11... | collective-permute-start | bytes 700424 | tf_op jit(solution)/shard_map/ppermute | solution.py:484
  13.5 31.4 %collective-permute-start.1 = (bf16[304,384]{1,0:T(8,128)(2,1)S(1)}, bf16[304,384]{1,0:T(8,128)(2,1)S(1)}, u32[]{:S(2)}, u32[]{:S(2)}) collective-permute-start(bf16[304,384]{1,0:T(8,128)(2,1)S(1)} %get-tuple-element.31), channel_id=1, source_target_pairs={{0,8},{8,0},{1,9},{9,1},{2,10},{10,2},{3,11},{11,3},{4,12},{12,4},... | collective-permute-start | bytes 700424 | tf_op jit(solution)/shard_map/ppermute | solution.py:484
  15.4 29.4 %collective-permute-start.3 = (bf16[304,384]{1,0:T(8,128)(2,1)S(1)}, bf16[304,384]{1,0:T(8,128)(2,1)S(1)}, u32[]{:S(2)}, u32[]{:S(2)}) collective-permute-start(bf16[304,384]{1,0:T(8,128)(2,1)S(1)} %collective-permute-done.2), channel_id=1, source_target_pairs={{0,8},{8,0},{1,9},{9,1},{2,10},{10,2},{3,11},{11,3},{4,12},{12,4},... | collective-permute-start | bytes 700424 | tf_op jit(solution)/shard_map/ppermute | solution.py:485
  17.2 8.6 %collective-permute-start.13 = (bf16[12,1536]{1,0:T(8,128)(2,1)S(1)}, bf16[12,1536]{1,0:T(8,128)(2,1)S(1)}, u32[]{:S(2)}, u32[]{:S(2)}) collective-permute-start(bf16[12,1536]{1,0:T(8,128)(2,1)S(1)} %copy-done.5), channel_id=1, source_target_pairs={{0,16},{16,32},{32,48},{48,0},{1,17},{17,33},{33,49},{49,1},{2,18}... | collective-permute-start | bytes 110600 | tf_op jit(solution)/shard_map/ppermute | solution.py:244
  18.4 7.5 %collective-permute-start.14 = (bf16[12,1536]{1,0:T(8,128)(2,1)S(1)}, bf16[12,1536]{1,0:T(8,128)(2,1)S(1)}, u32[]{:S(2)}, u32[]{:S(2)}) collective-permute-start(bf16[12,1536]{1,0:T(8,128)(2,1)S(1)} %copy-done.5), channel_id=1, source_target_pairs={{0,32},{16,48},{32,0},{48,16},{1,33},{17,49},{33,1},{49,17},{2,34}... | collective-permute-start | bytes 110600 | tf_op jit(solution)/shard_map/ppermute | solution.py:244
  25.8 47.3 %collective-permute-start.33 = (bf16[2,192,768]{2,1,0:T(8,128)(2,1)S(1)}, bf16[2,192,768]{2,1,0:T(8,128)(2,1)S(1)}, u32[]{:S(2)}, u32[]{:S(2)}) collective-permute-start(bf16[2,192,768]{2,1,0:T(8,128)(2,1)S(1)} %get-tuple-element.43), channel_id=1, source_target_pairs={{0,16},{16,0},{32,48},{48,32},{1,17},{17,1},{33,49},{49,33},{2,18}... | collective-permute-start | bytes 1769480 | tf_op jit(solution)/shard_map/ppermute | solution.py:443
  25.9 14.7 %collective-permute-start.15 = (bf16[12,1536]{1,0:T(8,128)(2,1)S(1)}, bf16[12,1536]{1,0:T(8,128)(2,1)S(1)}, u32[]{:S(2)}, u32[]{:S(2)}) collective-permute-start(bf16[12,1536]{1,0:T(8,128)(2,1)S(1)} %copy-done.5), channel_id=1, source_target_pairs={{0,48},{16,0},{32,16},{48,32},{1,49},{17,1},{33,17},{49,33},{2,50}... | collective-permute-start | bytes 110600 | tf_op jit(solution)/shard_map/ppermute | solution.py:244
  40.6 34.8 %collective-permute-start.34 = (bf16[2,192,768]{2,1,0:T(8,128)(2,1)S(1)}, bf16[2,192,768]{2,1,0:T(8,128)(2,1)S(1)}, u32[]{:S(2)}, u32[]{:S(2)}) collective-permute-start(bf16[2,192,768]{2,1,0:T(8,128)(2,1)S(1)} %get-tuple-element.44), channel_id=1, source_target_pairs={{0,48},{48,0},{16,32},{32,16},{1,49},{49,1},{17,33},{33,17},{2,50}... | collective-permute-start | bytes 1769480 | tf_op jit(solution)/shard_map/ppermute | solution.py:444
  41.4 5.9 %collective-permute-start.16 = (bf16[48,1536]{1,0:T(8,128)(2,1)S(1)}, bf16[48,1536]{1,0:T(8,128)(2,1)S(1)}, u32[]{:S(2)}, u32[]{:S(2)}) collective-permute-start(bf16[48,1536]{1,0:T(8,128)(2,1)S(1)} %joined.2.refs_0_), channel_id=1, source_target_pairs={{0,64},{64,0},{1,65},{65,1},{2,66},{66,2},{3,67},{67,3},{4,68},{68... | collective-permute-start | bytes 442376 | tf_op jit(solution)/shard_map/ppermute | solution.py:246
  44.8 5.5 %collective-permute-start.4 = (bf16[128,384]{1,0:T(8,128)(2,1)S(1)}, bf16[128,384]{1,0:T(8,128)(2,1)S(1)}, u32[]{:S(2)}, u32[]{:S(2)}) collective-permute-start(bf16[128,384]{1,0:T(8,128)(2,1)S(1)} %own_queries.1.refs_4_), channel_id=1, source_target_pairs={{0,2},{2,4},{4,6},{6,0},{1,3},{3,5},{5,7},{7,1},{8,10},{10,12},{12... | collective-permute-start | bytes 294920 | tf_op jit(solution)/shard_map/ppermute | solution.py:492
  47.3 77.8 %slice-start = ((s8[4718592]{0:T(1024)(128)(4,1)}), s8[4194304]{0:T(1024)(128)(4,1)S(1)}, s32[]{:S(2)}) async-start(s8[4718592]{0:T(1024)(128)(4,1)} %bitcast.12), calls=%async_computation | async-start | bytes 8388608
  47.4 19.5 %collective-permute-start.17 = (bf16[96,1536]{1,0:T(8,128)(2,1)S(1)}, bf16[96,1536]{1,0:T(8,128)(2,1)S(1)}, u32[]{:S(2)}, u32[]{:S(2)}) collective-permute-start(bf16[96,1536]{1,0:T(8,128)(2,1)S(1)} %joined.3.refs_0_), channel_id=1, source_target_pairs={{0,8},{8,0},{1,9},{9,1},{2,10},{10,2},{3,11},{11,3},{4,12},{12,4},... | collective-permute-start | bytes 884744 | tf_op jit(solution)/shard_map/ppermute | solution.py:248
  47.6 19.2 %collective-permute-start.19 = (bf16[96,1536]{1,0:T(8,128)(2,1)S(1)}, bf16[96,1536]{1,0:T(8,128)(2,1)S(1)}, u32[]{:S(2)}, u32[]{:S(2)}) collective-permute-start(bf16[96,1536]{1,0:T(8,128)(2,1)S(1)} %joined.3.refs_0_), channel_id=1, source_target_pairs={{0,6},{2,0},{4,2},{6,4},{1,7},{3,1},{5,3},{7,5},{8,14},{10,8},{12,... | collective-permute-start | bytes 884744 | tf_op jit(solution)/shard_map/ppermute | solution.py:252
  50.3 5.0 %collective-permute-start.5 = (bf16[128,384]{1,0:T(8,128)(2,1)S(1)}, bf16[128,384]{1,0:T(8,128)(2,1)S(1)}, u32[]{:S(2)}, u32[]{:S(2)}) collective-permute-start(bf16[128,384]{1,0:T(8,128)(2,1)S(1)} %own_queries.1.refs_4_), channel_id=1, source_target_pairs={{0,4},{2,6},{4,0},{6,2},{1,5},{3,7},{5,1},{7,3},{8,12},{10,14},{12... | collective-permute-start | bytes 294920 | tf_op jit(solution)/shard_map/ppermute | solution.py:492
  55.3 4.7 %collective-permute-start.6 = (bf16[128,384]{1,0:T(8,128)(2,1)S(1)}, bf16[128,384]{1,0:T(8,128)(2,1)S(1)}, u32[]{:S(2)}, u32[]{:S(2)}) collective-permute-start(bf16[128,384]{1,0:T(8,128)(2,1)S(1)} %own_queries.1.refs_4_), channel_id=1, source_target_pairs={{0,6},{2,0},{4,2},{6,4},{1,7},{3,1},{5,3},{7,5},{8,14},{10,8},{12,... | collective-permute-start | bytes 294920 | tf_op jit(solution)/shard_map/ppermute | solution.py:492
  63.3 8.6 %collective-permute-start.7 = (bf16[128,512]{1,0:T(8,128)(2,1)S(1)}, bf16[128,512]{1,0:T(8,128)(2,1)S(1)}, u32[]{:S(2)}, u32[]{:S(2)}) collective-permute-start(bf16[128,512]{1,0:T(8,128)(2,1)S(1)} %get-tuple-element.34), channel_id=1, source_target_pairs={{0,6},{2,0},{4,2},{6,4},{1,7},{3,1},{5,3},{7,5},{8,14},{10,8},{12,... | collective-permute-start | bytes 393224 | tf_op jit(solution)/shard_map/ppermute | solution.py:494
  66.8 17.0 %collective-permute-start.18 = (bf16[96,1536]{1,0:T(8,128)(2,1)S(1)}, bf16[96,1536]{1,0:T(8,128)(2,1)S(1)}, u32[]{:S(2)}, u32[]{:S(2)}) collective-permute-start(bf16[96,1536]{1,0:T(8,128)(2,1)S(1)} %joined.3.refs_0_), channel_id=1, source_target_pairs={{0,2},{2,4},{4,6},{6,0},{1,3},{3,5},{5,7},{7,1},{8,10},{10,12},{12... | collective-permute-start | bytes 884744 | tf_op jit(solution)/shard_map/ppermute | solution.py:251
  66.8 23.2 %collective-permute-start.24 = (bf16[96,1536]{1,0:T(8,128)(2,1)S(1)}, bf16[96,1536]{1,0:T(8,128)(2,1)S(1)}, u32[]{:S(2)}, u32[]{:S(2)}) collective-permute-start(bf16[96,1536]{1,0:T(8,128)(2,1)S(1)} %joined.3.refs_0_), channel_id=1, source_target_pairs={{0,1},{1,0},{2,3},{3,2},{4,5},{5,4},{6,7},{7,6},{8,9},{9,8},{10,11... | collective-permute-start | bytes 884744 | tf_op jit(solution)/shard_map/ppermute | solution.py:256
  71.9 6.7 %collective-permute-start.8 = (bf16[128,512]{1,0:T(8,128)(2,1)S(1)}, bf16[128,512]{1,0:T(8,128)(2,1)S(1)}, u32[]{:S(2)}, u32[]{:S(2)}) collective-permute-start(bf16[128,512]{1,0:T(8,128)(2,1)S(1)} %get-tuple-element.35), channel_id=1, source_target_pairs={{0,4},{2,6},{4,0},{6,2},{1,5},{3,7},{5,1},{7,3},{8,12},{10,14},{12... | collective-permute-start | bytes 393224 | tf_op jit(solution)/shard_map/ppermute | solution.py:494
  73.1 9.1 %collective-permute-start.9 = (bf16[128,512]{1,0:T(8,128)(2,1)S(1)}, bf16[128,512]{1,0:T(8,128)(2,1)S(1)}, u32[]{:S(2)}, u32[]{:S(2)}) collective-permute-start(bf16[128,512]{1,0:T(8,128)(2,1)S(1)} %get-tuple-element.36), channel_id=1, source_target_pairs={{0,2},{2,4},{4,6},{6,0},{1,3},{3,5},{5,7},{7,1},{8,10},{10,12},{12... | collective-permute-start | bytes 393224 | tf_op jit(solution)/shard_map/ppermute | solution.py:494
  75.4 19.8 %collective-permute-start.20 = (bf16[96,1536]{1,0:T(8,128)(2,1)S(1)}, bf16[96,1536]{1,0:T(8,128)(2,1)S(1)}, u32[]{:S(2)}, u32[]{:S(2)}) collective-permute-start(bf16[96,1536]{1,0:T(8,128)(2,1)S(1)} %collective-permute-done.17.refs_1_), channel_id=1, source_target_pairs={{0,2},{2,4},{4,6},{6,0},{1,3},{3,5},{5,7},{7,1},{8,10},{10,12},{12... | collective-permute-start | bytes 884744 | tf_op jit(solution)/shard_map/ppermute | solution.py:251
  75.5 49.7 %slice-start.1 = ((s8[4718592]{0:T(1024)(128)(4,1)}), s8[524288]{0:T(1024)(128)(4,1)S(1)}, s32[]{:S(2)}) async-start(s8[4718592]{0:T(1024)(128)(4,1)} %bitcast.12), calls=%async_computation.1 | async-start | bytes 1048576
  75.6 49.6 %copy-start.2 = (bf16[1,32,1536]{2,1,0:T(8,128)(2,1)S(1)}, bf16[1,32,1536]{2,1,0:T(8,128)(2,1)}, u32[]{:S(2)}) copy-start(bf16[1,32,1536]{2,1,0:T(8,128)(2,1)} %param.14) | copy-start | bytes 294916
  75.6 49.6 %copy-start.3 = (f32[4,1536]{1,0:T(4,128)S(1)}, f32[4,1536]{1,0:T(4,128)}, u32[]{:S(2)}) copy-start(f32[4,1536]{1,0:T(4,128)} %gate_ref.1) | copy-start | bytes 73732
  78.7 17.0 %collective-permute-start.35 = (bf16[192,768]{1,0:T(8,128)(2,1)S(1)}, bf16[192,768]{1,0:T(8,128)(2,1)S(1)}, u32[]{:S(2)}, u32[]{:S(2)}) collective-permute-start(bf16[192,768]{1,0:T(8,128)(2,1)S(1)} %get-tuple-element.45), channel_id=1, source_target_pairs={{0,48},{48,0},{16,32},{32,16},{1,49},{49,1},{17,33},{33,17},{2,50}... | collective-permute-start | bytes 884744 | tf_op jit(solution)/shard_map/ppermute | solution.py:446
  82.3 13.5 %collective-permute-start.36 = (bf16[192,768]{1,0:T(8,128)(2,1)S(1)}, bf16[192,768]{1,0:T(8,128)(2,1)S(1)}, u32[]{:S(2)}, u32[]{:S(2)}) collective-permute-start(bf16[192,768]{1,0:T(8,128)(2,1)S(1)} %get-tuple-element.46), channel_id=1, source_target_pairs={{0,16},{16,0},{32,48},{48,32},{1,17},{17,1},{33,49},{49,33},{2,18}... | collective-permute-start | bytes 884744 | tf_op jit(solution)/shard_map/ppermute | solution.py:447
  83.8 8.2 %collective-permute-start.10 = (bf16[32,384]{1,0:T(8,128)(2,1)S(1)}, bf16[32,384]{1,0:T(8,128)(2,1)S(1)}, u32[]{:S(2)}, u32[]{:S(2)}) collective-permute-start(bf16[32,384]{1,0:T(8,128)(2,1)S(1)} %get-tuple-element.38), channel_id=1, source_target_pairs={{0,1},{1,0},{2,3},{3,2},{4,5},{5,4},{6,7},{7,6},{8,9},{9,8},{10,11... | collective-permute-start | bytes 73736 | tf_op jit(solution)/shard_map/ppermute | solution.py:499
  90.1 3.4 %collective-permute-start.11 = (bf16[32,384]{1,0:T(8,128)(2,1)S(1)}, bf16[32,384]{1,0:T(8,128)(2,1)S(1)}, u32[]{:S(2)}, u32[]{:S(2)}) collective-permute-start(bf16[32,384]{1,0:T(8,128)(2,1)S(1)} %get-tuple-element.39), channel_id=1, source_target_pairs={{0,8},{8,0},{1,9},{9,1},{2,10},{10,2},{3,11},{11,3},{4,12},{12,4},... | collective-permute-start | bytes 73736 | tf_op jit(solution)/shard_map/ppermute | solution.py:500
  92.0 3.3 %collective-permute-start.12 = (bf16[32,384]{1,0:T(8,128)(2,1)S(1)}, bf16[32,384]{1,0:T(8,128)(2,1)S(1)}, u32[]{:S(2)}, u32[]{:S(2)}) collective-permute-start(bf16[32,384]{1,0:T(8,128)(2,1)S(1)} %get-tuple-element.40), channel_id=1, source_target_pairs={{0,9},{9,0},{1,8},{8,1},{2,11},{11,2},{3,10},{10,3},{4,13},{13,4},... | collective-permute-start | bytes 73736 | tf_op jit(solution)/shard_map/ppermute | solution.py:501
  93.5 7.9 %collective-permute-start.21 = (bf16[96,1536]{1,0:T(8,128)(2,1)S(1)}, bf16[96,1536]{1,0:T(8,128)(2,1)S(1)}, u32[]{:S(2)}, u32[]{:S(2)}) collective-permute-start(bf16[96,1536]{1,0:T(8,128)(2,1)S(1)} %collective-permute-done.17.refs_1_), channel_id=1, source_target_pairs={{0,6},{2,0},{4,2},{6,4},{1,7},{3,1},{5,3},{7,5},{8,14},{10,8},{12,... | collective-permute-start | bytes 884744 | tf_op jit(solution)/shard_map/ppermute | solution.py:252
  95.2 12.5 %collective-permute-start.22 = (bf16[96,1536]{1,0:T(8,128)(2,1)S(1)}, bf16[96,1536]{1,0:T(8,128)(2,1)S(1)}, u32[]{:S(2)}, u32[]{:S(2)}) collective-permute-start(bf16[96,1536]{1,0:T(8,128)(2,1)S(1)} %collective-permute-done.19.refs_3_), channel_id=1, source_target_pairs={{0,6},{2,0},{4,2},{6,4},{1,7},{3,1},{5,3},{7,5},{8,14},{10,8},{12,... | collective-permute-start | bytes 884744 | tf_op jit(solution)/shard_map/ppermute | solution.py:253
  95.2 12.5 %collective-permute-start.25 = (bf16[96,1536]{1,0:T(8,128)(2,1)S(1)}, bf16[96,1536]{1,0:T(8,128)(2,1)S(1)}, u32[]{:S(2)}, u32[]{:S(2)}) collective-permute-start(bf16[96,1536]{1,0:T(8,128)(2,1)S(1)} %collective-permute-done.17.refs_1_), channel_id=1, source_target_pairs={{0,1},{1,0},{2,3},{3,2},{4,5},{5,4},{6,7},{7,6},{8,9},{9,8},{10,11... | collective-permute-start | bytes 884744 | tf_op jit(solution)/shard_map/ppermute | solution.py:256
  95.6 13.7 %collective-permute-start.27 = (bf16[96,1536]{1,0:T(8,128)(2,1)S(1)}, bf16[96,1536]{1,0:T(8,128)(2,1)S(1)}, u32[]{:S(2)}, u32[]{:S(2)}) collective-permute-start(bf16[96,1536]{1,0:T(8,128)(2,1)S(1)} %collective-permute-done.19.refs_3_), channel_id=1, source_target_pairs={{0,1},{1,0},{2,3},{3,2},{4,5},{5,4},{6,7},{7,6},{8,9},{9,8},{10,11... | collective-permute-start | bytes 884744 | tf_op jit(solution)/shard_map/ppermute | solution.py:256
  95.8 15.7 %collective-permute-start.23 = (bf16[96,1536]{1,0:T(8,128)(2,1)S(1)}, bf16[96,1536]{1,0:T(8,128)(2,1)S(1)}, u32[]{:S(2)}, u32[]{:S(2)}) collective-permute-start(bf16[96,1536]{1,0:T(8,128)(2,1)S(1)} %collective-permute-done.20.refs_4_), channel_id=1, source_target_pairs={{0,2},{2,4},{4,6},{6,0},{1,3},{3,5},{5,7},{7,1},{8,10},{10,12},{12... | collective-permute-start | bytes 884744 | tf_op jit(solution)/shard_map/ppermute | solution.py:254
  101.4 10.2 %collective-permute-start.37 = (bf16[2,24,1536]{2,1,0:T(8,128)(2,1)S(1)}, bf16[2,24,1536]{2,1,0:T(8,128)(2,1)S(1)}, u32[]{:S(2)}, u32[]{:S(2)}) collective-permute-start(bf16[2,24,1536]{2,1,0:T(8,128)(2,1)S(1)} %get-tuple-element.48), channel_id=1, source_target_pairs={{0,2},{2,4},{4,6},{6,0},{1,3},{3,5},{5,7},{7,1},{8,10},{10,12},{12... | collective-permute-start | bytes 442376 | tf_op jit(solution)/shard_map/ppermute | solution.py:449
  107.7 5.5 %collective-permute-start.38 = (bf16[2,24,1536]{2,1,0:T(8,128)(2,1)S(1)}, bf16[2,24,1536]{2,1,0:T(8,128)(2,1)S(1)}, u32[]{:S(2)}, u32[]{:S(2)}) collective-permute-start(bf16[2,24,1536]{2,1,0:T(8,128)(2,1)S(1)} %get-tuple-element.49), channel_id=1, source_target_pairs={{0,4},{2,6},{4,0},{6,2},{1,5},{3,7},{5,1},{7,3},{8,12},{10,14},{12... | collective-permute-start | bytes 442376 | tf_op jit(solution)/shard_map/ppermute | solution.py:449
  107.7 8.2 %collective-permute-start.39 = (bf16[2,24,1536]{2,1,0:T(8,128)(2,1)S(1)}, bf16[2,24,1536]{2,1,0:T(8,128)(2,1)S(1)}, u32[]{:S(2)}, u32[]{:S(2)}) collective-permute-start(bf16[2,24,1536]{2,1,0:T(8,128)(2,1)S(1)} %get-tuple-element.50), channel_id=1, source_target_pairs={{0,6},{2,0},{4,2},{6,4},{1,7},{3,1},{5,3},{7,5},{8,14},{10,8},{12,... | collective-permute-start | bytes 442376 | tf_op jit(solution)/shard_map/ppermute | solution.py:449
  109.4 9.1 %collective-permute-start.26 = (bf16[96,1536]{1,0:T(8,128)(2,1)S(1)}, bf16[96,1536]{1,0:T(8,128)(2,1)S(1)}, u32[]{:S(2)}, u32[]{:S(2)}) collective-permute-start(bf16[96,1536]{1,0:T(8,128)(2,1)S(1)} %collective-permute-done.18.refs_2_), channel_id=1, source_target_pairs={{0,1},{1,0},{2,3},{3,2},{4,5},{5,4},{6,7},{7,6},{8,9},{9,8},{10,11... | collective-permute-start | bytes 884744 | tf_op jit(solution)/shard_map/ppermute | solution.py:256
  111.5 12.4 %collective-permute-start.28 = (bf16[96,1536]{1,0:T(8,128)(2,1)S(1)}, bf16[96,1536]{1,0:T(8,128)(2,1)S(1)}, u32[]{:S(2)}, u32[]{:S(2)}) collective-permute-start(bf16[96,1536]{1,0:T(8,128)(2,1)S(1)} %collective-permute-done.20.refs_4_), channel_id=1, source_target_pairs={{0,1},{1,0},{2,3},{3,2},{4,5},{5,4},{6,7},{7,6},{8,9},{9,8},{10,11... | collective-permute-start | bytes 884744 | tf_op jit(solution)/shard_map/ppermute | solution.py:256
  111.5 12.4 %collective-permute-start.29 = (bf16[96,1536]{1,0:T(8,128)(2,1)S(1)}, bf16[96,1536]{1,0:T(8,128)(2,1)S(1)}, u32[]{:S(2)}, u32[]{:S(2)}) collective-permute-start(bf16[96,1536]{1,0:T(8,128)(2,1)S(1)} %collective-permute-done.21.refs_5_), channel_id=1, source_target_pairs={{0,1},{1,0},{2,3},{3,2},{4,5},{5,4},{6,7},{7,6},{8,9},{9,8},{10,11... | collective-permute-start | bytes 884744 | tf_op jit(solution)/shard_map/ppermute | solution.py:256
  113.2 11.2 %collective-permute-start.30 = (bf16[96,1536]{1,0:T(8,128)(2,1)S(1)}, bf16[96,1536]{1,0:T(8,128)(2,1)S(1)}, u32[]{:S(2)}, u32[]{:S(2)}) collective-permute-start(bf16[96,1536]{1,0:T(8,128)(2,1)S(1)} %collective-permute-done.22.refs_6_), channel_id=1, source_target_pairs={{0,1},{1,0},{2,3},{3,2},{4,5},{5,4},{6,7},{7,6},{8,9},{9,8},{10,11... | collective-permute-start | bytes 884744 | tf_op jit(solution)/shard_map/ppermute | solution.py:256
  115.9 11.5 %collective-permute-start.31 = (bf16[96,1536]{1,0:T(8,128)(2,1)S(1)}, bf16[96,1536]{1,0:T(8,128)(2,1)S(1)}, u32[]{:S(2)}, u32[]{:S(2)}) collective-permute-start(bf16[96,1536]{1,0:T(8,128)(2,1)S(1)} %collective-permute-done.23.refs_7_), channel_id=1, source_target_pairs={{0,1},{1,0},{2,3},{3,2},{4,5},{5,4},{6,7},{7,6},{8,9},{9,8},{10,11... | collective-permute-start | bytes 884744 | tf_op jit(solution)/shard_map/ppermute | solution.py:256
  118.4 18.1 %collective-permute-start.40 = (f32[12,1536]{1,0:T(8,128)S(1)}, f32[12,1536]{1,0:T(8,128)S(1)}, u32[]{:S(2)}, u32[]{:S(2)}) collective-permute-start(f32[12,1536]{1,0:T(8,128)S(1)} %get-tuple-element.51), channel_id=1, source_target_pairs={{0,0},{1,64},{8,8},{9,72},{64,1},{65,65},{72,9},{73,73},{2,2},{3,6... | collective-permute-start | bytes 221192 | tf_op jit(solution)/shard_map/ppermute | solution.py:456
  123.9 12.7 %collective-permute-start.41 = (f32[12,1536]{1,0:T(8,128)S(1)}, f32[12,1536]{1,0:T(8,128)S(1)}, u32[]{:S(2)}, u32[]{:S(2)}) collective-permute-start(f32[12,1536]{1,0:T(8,128)S(1)} %get-tuple-element.52), channel_id=1, source_target_pairs={{0,1},{1,65},{8,9},{9,73},{64,0},{65,64},{72,8},{73,72},{2,3},{3,6... | collective-permute-start | bytes 221192 | tf_op jit(solution)/shard_map/ppermute | solution.py:456
  124.0 12.6 %collective-permute-start.42 = (f32[12,1536]{1,0:T(8,128)S(1)}, f32[12,1536]{1,0:T(8,128)S(1)}, u32[]{:S(2)}, u32[]{:S(2)}) collective-permute-start(f32[12,1536]{1,0:T(8,128)S(1)} %get-tuple-element.53), channel_id=1, source_target_pairs={{0,8},{1,72},{8,0},{9,64},{64,9},{65,73},{72,1},{73,65},{2,10},{3,... | collective-permute-start | bytes 221192 | tf_op jit(solution)/shard_map/ppermute | solution.py:456
  124.4 12.2 %collective-permute-start.43 = (f32[12,1536]{1,0:T(8,128)S(1)}, f32[12,1536]{1,0:T(8,128)S(1)}, u32[]{:S(2)}, u32[]{:S(2)}) collective-permute-start(f32[12,1536]{1,0:T(8,128)S(1)} %get-tuple-element.54), channel_id=1, source_target_pairs={{0,9},{1,73},{8,1},{9,65},{64,8},{65,72},{72,0},{73,64},{2,11},{3,... | collective-permute-start | bytes 221192 | tf_op jit(solution)/shard_map/ppermute | solution.py:456

commit v3 on v2

--- a/solution.py
+++ b/solution.py
@@ -285,12 +285,12 @@
         kernel,
         grid_spec=pltpu.PrefetchScalarGridSpec(
             num_scalar_prefetch=1,
-            grid=(4,),
+            grid=(2,),
             in_specs=[
-                pl.BlockSpec((tokens, width // 2), lambda p, place: (0, 1 - place[2])),
-                pl.BlockSpec((tokens, width // 4), lambda p, place: (0, p)),
+                pl.BlockSpec((tokens, width // 4), lambda p, place: (0, 2 * (1 - place[2]) + p)),
+                pl.BlockSpec((tokens, width), lambda p, place: (0, 0)),
             ],
-            out_specs=pl.BlockSpec((width // 2, width // 4), lambda p, place: (0, p)),
+            out_specs=pl.BlockSpec((width // 4, width), lambda p, place: (p, 0)),
         ),
         out_shape=jax.ShapeDtypeStruct((width // 2, width), BF),
         compiler_params=room(32, dimension_semantics=("arbitrary",)),

time: 138 us -> 136 us (0.986)
  Pallas kernels: 31.3 us -> 29.4 us
    pallas_call x1, Pallas kernels: 6.83 us -> 4.88 us  [product_to_send(): pl.pallas_call(kernel, grid_spec=pltpu.PrefetchScalarGridSpec(num_scalar_...]
  transfers between devices with their start and end apart: 44 -> 44, of which waited for: 11 -> 11; matrix products, arithmetic and copies ran while one was open for 0% -> 0% of each run, Pallas kernels for 17% -> 18%
where the time goes in v3:
time: 136 us; the launch traced here: 135 us
  starting transfers between devices  64 us (47%)
  waiting for transfers between devices  37.7 us (28%)
  Pallas kernels  29.4 us (22%)
  between operations  2.23 us (2%)
  local copies, waits for them, and re-layouts  2.01 us (1%)
    ppermute x3, waiting for transfers between devices, weight_pieces(): on_x = [weight] + [lax.ppermute(weight, 'x', turn(k)) for k in (1, 2, 3)]  13.5 us
    ppermute x8, starting transfers between devices, weight_pieces(): lax.ppermute(p, 'c', SWAP)  12.8 us
    pallas_call x1, Pallas kernels, grad_of_input(): pl.pallas_call(kernel, grid=(rows // block,), out_shape=jax.ShapeDtypeStr...  9.19 us
    ppermute x3, waiting for transfers between devices, step(): all_queries = [own] + [lax.ppermute(own, 'y', turn(k)) for k in (1, 2, 3)]  6.97 us
    ppermute x3, starting transfers between devices, step(): lax.ppermute(partial[k], 'y', turn(-k))  6.93 us
    ppermute x1, waiting for transfers between devices, weight_pieces(): pieces[0, 2] = lax.ppermute(pieces[0, 1], 'y', turn(-1))  6.32 us
    ppermute x1, starting transfers between devices, step(): lax.ppermute(mixed[1], 'c', SWAP)  6.25 us
    ppermute x4, starting transfers between devices, weight_gradient(): lax.ppermute(a, ('zh', 'zl', 'c'), owner(n // 2, n % 2))  6.04 us
  transfers between devices with their start and end apart: 44, of which 11 were waited for; matrix products, arithmetic and copies ran while one was open for 0% of the time, Pallas kernels for 18%

profile of v3, /device:TPU:1, one launch (start us, length us, event | category | flops | bytes accessed | tf_op | source)
XLA Modules:
  0.0 135.3 jit_solution(13842445251551931671)
XLA Ops:
  0.6 0.1 stack.23.place_ref
  0.7 1.9 %copy-done = bf16[1024,1536]{1,0:T(8,128)(2,1)S(1)} copy-done((bf16[1024,1536]{1,0:T(8,128)(2,1)S(1)}, bf16[1024,1536]{1,0:T(8,128)(2,1)}, u32[]{:S(2)}) %copy-start) | copy-done | bytes 3145752
  2.6 4.9 %product_to_send.1 = bf16[768,1536]{1,0:T(8,128)(2,1)S(1)} custom-call(s32[5]{0:T(128)S(1)} %stack.23.place_ref, bf16[1024,1536]{1,0:T(8,128)(2,1)} %in_ref.3, bf16[1024,1536]{1,0:T(8,128)(2,1)S(1)} %copy-done), custom_call_target="tpu_custom_call" | custom-call | tf_op jit(solution)/shard_map/product_to_send/pallas_call | solution.py:284
  7.5 1.5 %collective-permute-start.32 = (bf16[768,1536]{1,0:T(8,128)(2,1)S(1)}, bf16[768,1536]{1,0:T(8,128)(2,1)S(1)}, u32[]{:S(2)}, u32[]{:S(2)}) collective-permute-start(bf16[768,1536]{1,0:T(8,128)(2,1)S(1)} %product_to_send.1), channel_id=1, source_target_pairs={{0,1},{1,0},{2,3},{3,2},{4,5},{5,4},{6,7},{7,6},{8,9},{9,8},{10,11... | collective-permute-start | bytes 7077896 | tf_op jit(solution)/shard_map/ppermute | solution.py:439
  9.6 1.3 packed.1
  10.9 0.1 collective-permute-start.2
  11.0 0.5 collective-permute-start
  11.5 1.7 %collective-permute-start.1 = (bf16[304,384]{1,0:T(8,128)(2,1)S(1)}, bf16[304,384]{1,0:T(8,128)(2,1)S(1)}, u32[]{:S(2)}, u32[]{:S(2)}) collective-permute-start(bf16[304,384]{1,0:T(8,128)(2,1)S(1)} %get-tuple-element.31), channel_id=1, source_target_pairs={{0,8},{8,0},{1,9},{9,1},{2,10},{10,2},{3,11},{11,3},{4,12},{12,4},... | collective-permute-start | bytes 700424 | tf_op jit(solution)/shard_map/ppermute | solution.py:484
  13.3 0.2 collective-permute-done.2
  13.5 1.7 %collective-permute-start.3 = (bf16[304,384]{1,0:T(8,128)(2,1)S(1)}, bf16[304,384]{1,0:T(8,128)(2,1)S(1)}, u32[]{:S(2)}, u32[]{:S(2)}) collective-permute-start(bf16[304,384]{1,0:T(8,128)(2,1)S(1)} %collective-permute-done.2), channel_id=1, source_target_pairs={{0,8},{8,0},{1,9},{9,1},{2,10},{10,2},{3,11},{11,3},{4,12},{12,4},... | collective-permute-start | bytes 700424 | tf_op jit(solution)/shard_map/ppermute | solution.py:485
  15.2 1.2 collective-permute-start.13
  16.4 2.4 %collective-permute-start.14 = (bf16[12,1536]{1,0:T(8,128)(2,1)S(1)}, bf16[12,1536]{1,0:T(8,128)(2,1)S(1)}, u32[]{:S(2)}, u32[]{:S(2)}) collective-permute-start(bf16[12,1536]{1,0:T(8,128)(2,1)S(1)} %copy-done.5), channel_id=1, source_target_pairs={{0,32},{16,48},{32,0},{48,16},{1,33},{17,49},{33,1},{49,17},{2,34}... | collective-permute-start | bytes 110600 | tf_op jit(solution)/shard_map/ppermute | solution.py:244
  18.9 4.9 %product_and_split.1 = (bf16[2,192,768]{2,1,0:T(8,128)(2,1)S(1)}, bf16[2,192,768]{2,1,0:T(8,128)(2,1)S(1)}, f32[2,192,768]{2,1,0:T(8,128)S(1)}, f32[2,192,768]{2,1,0:T(8,128)S(1)}) custom-call(s32[5]{0:T(128)S(1)} %stack.23.place_ref, bf16[1024,1536]{1,0:T(8,128)(2,1)} %in_ref.3, bf16[1024,1536]{1,0:T(8,128)(2,1)S(1)} %copy-done.1, ...), custom_call_target="tpu_custom_call" | custom-call | tf_op jit(solution)/shard_map/product_and_split/pallas_call | solution.py:335
  23.8 0.1 collective-permute-start.33
  23.9 1.2 collective-permute-start.15
  25.2 13.5 %collective-permute-done.15.refs_3_ = bf16[12,1536]{1,0:T(8,128)(2,1)S(1)} collective-permute-done((bf16[12,1536]{1,0:T(8,128)(2,1)S(1)}, bf16[12,1536]{1,0:T(8,128)(2,1)S(1)}, u32[]{:S(2)}, u32[]{:S(2)}) %collective-permute-start.15) | collective-permute-done | bytes 36896 | tf_op jit(solution)/shard_map/ppermute | solution.py:244
  38.6 0.8 joined.2.refs_0_
  39.5 3.4 %collective-permute-start.16 = (bf16[48,1536]{1,0:T(8,128)(2,1)S(1)}, bf16[48,1536]{1,0:T(8,128)(2,1)S(1)}, u32[]{:S(2)}, u32[]{:S(2)}) collective-permute-start(bf16[48,1536]{1,0:T(8,128)(2,1)S(1)} %joined.2.refs_0_), channel_id=1, source_target_pairs={{0,64},{64,0},{1,65},{65,1},{2,66},{66,2},{3,67},{67,3},{4,68},{68... | collective-permute-start | bytes 442376 | tf_op jit(solution)/shard_map/ppermute | solution.py:246
  42.9 1.4 %collective-permute-start.4 = (bf16[128,384]{1,0:T(8,128)(2,1)S(1)}, bf16[128,384]{1,0:T(8,128)(2,1)S(1)}, u32[]{:S(2)}, u32[]{:S(2)}) collective-permute-start(bf16[128,384]{1,0:T(8,128)(2,1)S(1)} %own_queries.1.refs_4_), channel_id=1, source_target_pairs={{0,2},{2,4},{4,6},{6,0},{1,3},{3,5},{5,7},{7,1},{8,10},{10,12},{12... | collective-permute-start | bytes 294920 | tf_op jit(solution)/shard_map/ppermute | solution.py:492
  44.2 1.1 collective-permute-done.16.refs_1_
  45.4 0.2 collective-permute-start.17
  45.6 2.7 %collective-permute-start.19 = (bf16[96,1536]{1,0:T(8,128)(2,1)S(1)}, bf16[96,1536]{1,0:T(8,128)(2,1)S(1)}, u32[]{:S(2)}, u32[]{:S(2)}) collective-permute-start(bf16[96,1536]{1,0:T(8,128)(2,1)S(1)} %joined.3.refs_0_), channel_id=1, source_target_pairs={{0,6},{2,0},{4,2},{6,4},{1,7},{3,1},{5,3},{7,5},{8,14},{10,8},{12,... | collective-permute-start | bytes 884744 | tf_op jit(solution)/shard_map/ppermute | solution.py:252
  48.4 1.2 collective-permute-start.5
  49.6 3.7 %collective-permute-done.5.refs_6_ = bf16[128,384]{1,0:T(8,128)(2,1)S(1)} collective-permute-done((bf16[128,384]{1,0:T(8,128)(2,1)S(1)}, bf16[128,384]{1,0:T(8,128)(2,1)S(1)}, u32[]{:S(2)}, u32[]{:S(2)}) %collective-permute-start.5) | collective-permute-done | bytes 98336 | tf_op jit(solution)/shard_map/ppermute | solution.py:492
  53.3 1.4 %collective-permute-start.6 = (bf16[128,384]{1,0:T(8,128)(2,1)S(1)}, bf16[128,384]{1,0:T(8,128)(2,1)S(1)}, u32[]{:S(2)}, u32[]{:S(2)}) collective-permute-start(bf16[128,384]{1,0:T(8,128)(2,1)S(1)} %own_queries.1.refs_4_), channel_id=1, source_target_pairs={{0,6},{2,0},{4,2},{6,4},{1,7},{3,1},{5,3},{7,5},{8,14},{10,8},{12,... | collective-permute-start | bytes 294920 | tf_op jit(solution)/shard_map/ppermute | solution.py:492
  54.8 3.2 %collective-permute-done.6.refs_7_ = bf16[128,384]{1,0:T(8,128)(2,1)S(1)} collective-permute-done((bf16[128,384]{1,0:T(8,128)(2,1)S(1)}, bf16[128,384]{1,0:T(8,128)(2,1)S(1)}, u32[]{:S(2)}, u32[]{:S(2)}) %collective-permute-start.6) | collective-permute-done | bytes 98336 | tf_op jit(solution)/shard_map/ppermute | solution.py:492
  58.0 3.4 %attend.1 = (bf16[128,512]{1,0:T(8,128)(2,1)S(1)}, bf16[128,512]{1,0:T(8,128)(2,1)S(1)}, bf16[128,512]{1,0:T(8,128)(2,1)S(1)}, bf16[128,512]{1,0:T(8,128)(2,1)S(1)}) custom-call(bf16[304,384]{1,0:T(8,128)(2,1)S(1)} %get-tuple-element.29.refs_0_, bf16[304,384]{1,0:T(8,128)(2,1)S(1)} %collective-permute-done.refs_1_, ...), custom_call_target="tpu_custom_call" | custom-call | tf_op jit(solution)/shard_map/attend/pallas_call | solution.py:112
  61.4 3.5 %collective-permute-start.7 = (bf16[128,512]{1,0:T(8,128)(2,1)S(1)}, bf16[128,512]{1,0:T(8,128)(2,1)S(1)}, u32[]{:S(2)}, u32[]{:S(2)}) collective-permute-start(bf16[128,512]{1,0:T(8,128)(2,1)S(1)} %get-tuple-element.34), channel_id=1, source_target_pairs={{0,6},{2,0},{4,2},{6,4},{1,7},{3,1},{5,3},{7,5},{8,14},{10,8},{12,... | collective-permute-start | bytes 393224 | tf_op jit(solution)/shard_map/ppermute | solution.py:494
  64.9 5.1 %collective-permute-start.24 = (bf16[96,1536]{1,0:T(8,128)(2,1)S(1)}, bf16[96,1536]{1,0:T(8,128)(2,1)S(1)}, u32[]{:S(2)}, u32[]{:S(2)}) collective-permute-start(bf16[96,1536]{1,0:T(8,128)(2,1)S(1)} %joined.3.refs_0_), channel_id=1, source_target_pairs={{0,1},{1,0},{2,3},{3,2},{4,5},{5,4},{6,7},{7,6},{8,9},{9,8},{10,11... | collective-permute-start | bytes 884744 | tf_op jit(solution)/shard_map/ppermute | solution.py:256
  70.0 1.2 collective-permute-start.8
  71.1 2.3 %collective-permute-start.9 = (bf16[128,512]{1,0:T(8,128)(2,1)S(1)}, bf16[128,512]{1,0:T(8,128)(2,1)S(1)}, u32[]{:S(2)}, u32[]{:S(2)}) collective-permute-start(bf16[128,512]{1,0:T(8,128)(2,1)S(1)} %get-tuple-element.36), channel_id=1, source_target_pairs={{0,2},{2,4},{4,6},{6,0},{1,3},{3,5},{5,7},{7,1},{8,10},{10,12},{12... | collective-permute-start | bytes 393224 | tf_op jit(solution)/shard_map/ppermute | solution.py:494
  73.4 0.1 collective-permute-start.20
  73.5 0.1 onward.1
  73.6 0.0 copy-start.2
  73.6 3.1 %collective-permute-done.8.refs_2_ = bf16[128,512]{1,0:T(8,128)(2,1)S(1)} collective-permute-done((bf16[128,512]{1,0:T(8,128)(2,1)S(1)}, bf16[128,512]{1,0:T(8,128)(2,1)S(1)}, u32[]{:S(2)}, u32[]{:S(2)}) %collective-permute-start.8) | collective-permute-done | bytes 131104 | tf_op jit(solution)/shard_map/ppermute | solution.py:494
  76.7 3.6 %collective-permute-start.35 = (bf16[192,768]{1,0:T(8,128)(2,1)S(1)}, bf16[192,768]{1,0:T(8,128)(2,1)S(1)}, u32[]{:S(2)}, u32[]{:S(2)}) collective-permute-start(bf16[192,768]{1,0:T(8,128)(2,1)S(1)} %get-tuple-element.45), channel_id=1, source_target_pairs={{0,48},{48,0},{16,32},{32,16},{1,49},{49,1},{17,33},{33,17},{2,50}... | collective-permute-start | bytes 884744 | tf_op jit(solution)/shard_map/ppermute | solution.py:446
  80.3 1.1 collective-permute-start.36
  81.4 0.5 merged.1
  81.8 6.2 %collective-permute-start.10 = (bf16[32,384]{1,0:T(8,128)(2,1)S(1)}, bf16[32,384]{1,0:T(8,128)(2,1)S(1)}, u32[]{:S(2)}, u32[]{:S(2)}) collective-permute-start(bf16[32,384]{1,0:T(8,128)(2,1)S(1)} %get-tuple-element.38), channel_id=1, source_target_pairs={{0,1},{1,0},{2,3},{3,2},{4,5},{5,4},{6,7},{7,6},{8,9},{9,8},{10,11... | collective-permute-start | bytes 73736 | tf_op jit(solution)/shard_map/ppermute | solution.py:499
  88.1 1.9 %collective-permute-start.11 = (bf16[32,384]{1,0:T(8,128)(2,1)S(1)}, bf16[32,384]{1,0:T(8,128)(2,1)S(1)}, u32[]{:S(2)}, u32[]{:S(2)}) collective-permute-start(bf16[32,384]{1,0:T(8,128)(2,1)S(1)} %get-tuple-element.39), channel_id=1, source_target_pairs={{0,8},{8,0},{1,9},{9,1},{2,10},{10,2},{3,11},{11,3},{4,12},{12,4},... | collective-permute-start | bytes 73736 | tf_op jit(solution)/shard_map/ppermute | solution.py:500
  90.0 1.1 collective-permute-start.12
  91.1 0.4 collective-permute-done.11.c_ref
  91.5 1.7 %collective-permute-done.12.d_ref = bf16[32,384]{1,0:T(8,128)(2,1)S(1)} collective-permute-done((bf16[32,384]{1,0:T(8,128)(2,1)S(1)}, bf16[32,384]{1,0:T(8,128)(2,1)S(1)}, u32[]{:S(2)}, u32[]{:S(2)}) %collective-permute-start.12) | collective-permute-done | bytes 24608 | tf_op jit(solution)/shard_map/ppermute | solution.py:501
  93.3 0.4 collective-permute-start.25
  93.7 0.1 collective-permute-start.27
  93.8 1.7 %collective-permute-start.23 = (bf16[96,1536]{1,0:T(8,128)(2,1)S(1)}, bf16[96,1536]{1,0:T(8,128)(2,1)S(1)}, u32[]{:S(2)}, u32[]{:S(2)}) collective-permute-start(bf16[96,1536]{1,0:T(8,128)(2,1)S(1)} %collective-permute-done.20.refs_4_), channel_id=1, source_target_pairs={{0,2},{2,4},{4,6},{6,0},{1,3},{3,5},{5,7},{7,1},{8,10},{10,12},{12... | collective-permute-start | bytes 884744 | tf_op jit(solution)/shard_map/ppermute | solution.py:254
  95.5 0.8 cut_along_y.1
  96.3 3.1 %collective-permute-done.21.refs_5_ = bf16[96,1536]{1,0:T(8,128)(2,1)S(1)} collective-permute-done((bf16[96,1536]{1,0:T(8,128)(2,1)S(1)}, bf16[96,1536]{1,0:T(8,128)(2,1)S(1)}, u32[]{:S(2)}, u32[]{:S(2)}) %collective-permute-start.21) | collective-permute-done | bytes 294944 | tf_op jit(solution)/shard_map/ppermute | solution.py:252
  99.4 6.3 %collective-permute-done.22.refs_6_ = bf16[96,1536]{1,0:T(8,128)(2,1)S(1)} collective-permute-done((bf16[96,1536]{1,0:T(8,128)(2,1)S(1)}, bf16[96,1536]{1,0:T(8,128)(2,1)S(1)}, u32[]{:S(2)}, u32[]{:S(2)}) %collective-permute-start.22) | collective-permute-done | bytes 294944 | tf_op jit(solution)/shard_map/ppermute | solution.py:253
  105.7 1.7 %collective-permute-start.39 = (bf16[2,24,1536]{2,1,0:T(8,128)(2,1)S(1)}, bf16[2,24,1536]{2,1,0:T(8,128)(2,1)S(1)}, u32[]{:S(2)}, u32[]{:S(2)}) collective-permute-start(bf16[2,24,1536]{2,1,0:T(8,128)(2,1)S(1)} %get-tuple-element.50), channel_id=1, source_target_pairs={{0,6},{2,0},{4,2},{6,4},{1,7},{3,1},{5,3},{7,5},{8,14},{10,8},{12,... | collective-permute-start | bytes 442376 | tf_op jit(solution)/shard_map/ppermute | solution.py:449
  107.4 2.1 %collective-permute-start.26 = (bf16[96,1536]{1,0:T(8,128)(2,1)S(1)}, bf16[96,1536]{1,0:T(8,128)(2,1)S(1)}, u32[]{:S(2)}, u32[]{:S(2)}) collective-permute-start(bf16[96,1536]{1,0:T(8,128)(2,1)S(1)} %collective-permute-done.18.refs_2_), channel_id=1, source_target_pairs={{0,1},{1,0},{2,3},{3,2},{4,5},{5,4},{6,7},{7,6},{8,9},{9,8},{10,11... | collective-permute-start | bytes 884744 | tf_op jit(solution)/shard_map/ppermute | solution.py:256
  109.5 0.1 collective-permute-start.28
  109.6 0.4 collective-permute-start.29
  110.0 1.2 collective-permute-done.38.b
  111.2 2.7 %collective-permute-start.30 = (bf16[96,1536]{1,0:T(8,128)(2,1)S(1)}, bf16[96,1536]{1,0:T(8,128)(2,1)S(1)}, u32[]{:S(2)}, u32[]{:S(2)}) collective-permute-start(bf16[96,1536]{1,0:T(8,128)(2,1)S(1)} %collective-permute-done.22.refs_6_), channel_id=1, source_target_pairs={{0,1},{1,0},{2,3},{3,2},{4,5},{5,4},{6,7},{7,6},{8,9},{9,8},{10,11... | collective-permute-start | bytes 884744 | tf_op jit(solution)/shard_map/ppermute | solution.py:256
  113.9 1.9 %collective-permute-start.31 = (bf16[96,1536]{1,0:T(8,128)(2,1)S(1)}, bf16[96,1536]{1,0:T(8,128)(2,1)S(1)}, u32[]{:S(2)}, u32[]{:S(2)}) collective-permute-start(bf16[96,1536]{1,0:T(8,128)(2,1)S(1)} %collective-permute-done.23.refs_7_), channel_id=1, source_target_pairs={{0,1},{1,0},{2,3},{3,2},{4,5},{5,4},{6,7},{7,6},{8,9},{9,8},{10,11... | collective-permute-start | bytes 884744 | tf_op jit(solution)/shard_map/ppermute | solution.py:256
  115.8 0.6 cut_to_owners.1
  116.5 5.4 %collective-permute-start.40 = (f32[12,1536]{1,0:T(8,128)S(1)}, f32[12,1536]{1,0:T(8,128)S(1)}, u32[]{:S(2)}, u32[]{:S(2)}) collective-permute-start(f32[12,1536]{1,0:T(8,128)S(1)} %get-tuple-element.51), channel_id=1, source_target_pairs={{0,0},{1,64},{8,8},{9,72},{64,1},{65,65},{72,9},{73,73},{2,2},{3,6... | collective-permute-start | bytes 221192 | tf_op jit(solution)/shard_map/ppermute | solution.py:456
  121.9 0.1 collective-permute-start.41
  122.0 0.4 collective-permute-start.42
  122.5 0.1 collective-permute-start.43
  123.2 2.1 %streamed.1 = bf16[32,1536]{1,0:T(8,128)(2,1)} custom-call(s32[5]{0:T(128)S(1)} %stack.23.place_ref, s32[1]{0:T(128)S(6)} %copy.18.step_ref, bf16[32,1536]{1,0:T(8,128)(2,1)S(1)} %bitcast.14, f32[4,1536]{1,0:T(4,128)S(1)} %copy-done.3, bf16[32,384]{1,0:T(8,128)(2,1)S(1)} %get-tuple-element.37.a_ref, bf16[32,384]{1,0:T(8,128)(2,1)S(1)} %collective-permute-done.10.b_ref, ...), custom_call_target="tpu_custom_call" | custom-call | tf_op jit(solution)/shard_map/streamed/pallas_call | solution.py:163
  125.4 9.2 %grad_of_input.1 = bf16[1024,1536]{1,0:T(8,128)(2,1)} custom-call(s32[5]{0:T(128)S(1)} %stack.23.place_ref, bf16[1024,1536]{1,0:T(8,128)(2,1)S(1)} %copy-done.1, bf16[96,1536]{1,0:T(8,128)(2,1)S(1)} %joined.3.refs_0_, bf16[96,1536]{1,0:T(8,128)(2,1)S(1)} %collective-permute-done.17.refs_1_, bf16[96,1536]{1,0:T(8,128)(2,1)S(1)} %collective-permute-done.18.refs_2_, ...), custom_call_target="tpu_custom_call" | custom-call | tf_op jit(solution)/shard_map/grad_of_input/pallas_call | solution.py:209
  134.6 0.7 added.1
  (56 shorter events, 0.2 us)
Async XLA Ops:
  0.7 1.9 %copy-start = (bf16[1024,1536]{1,0:T(8,128)(2,1)S(1)}, bf16[1024,1536]{1,0:T(8,128)(2,1)}, u32[]{:S(2)}) copy-start(bf16[1024,1536]{1,0:T(8,128)(2,1)} %cot_ref.5) | copy-start | bytes 9437188
  2.6 7.0 %copy-start.4 = (s32[1,96]{1,0:T(1,128)S(1)}, s32[1,96]{1,0:T(1,128)}, u32[]{:S(2)}) copy-start(s32[1,96]{1,0:T(1,128)} %frames_ref.1) | copy-start | bytes 1156
  2.6 12.6 %copy-start.5 = (bf16[12,1536]{1,0:T(8,128)(2,1)S(1)}, bf16[12,1536]{1,0:T(8,128)(2,1)}, u32[]{:S(2)}) copy-start(bf16[12,1536]{1,0:T(8,128)(2,1)} %refs_0_.1) | copy-start | bytes 110596
  2.6 16.3 %copy-start.1 = (bf16[1024,1536]{1,0:T(8,128)(2,1)S(1)}, bf16[1024,1536]{1,0:T(8,128)(2,1)}, u32[]{:S(2)}) copy-start(bf16[1024,1536]{1,0:T(8,128)(2,1)} %cot_ref.5) | copy-start | bytes 9437188
  7.5 8.9 %collective-permute-start.32 = (bf16[768,1536]{1,0:T(8,128)(2,1)S(1)}, bf16[768,1536]{1,0:T(8,128)(2,1)S(1)}, u32[]{:S(2)}, u32[]{:S(2)}) collective-permute-start(bf16[768,1536]{1,0:T(8,128)(2,1)S(1)} %product_to_send.1), channel_id=1, source_target_pairs={{0,1},{1,0},{2,3},{3,2},{4,5},{5,4},{6,7},{7,6},{8,9},{9,8},{10,11... | collective-permute-start | bytes 7077896 | tf_op jit(solution)/shard_map/ppermute | solution.py:439
  10.9 2.5 %collective-permute-start.2 = (bf16[304,384]{1,0:T(8,128)(2,1)S(1)}, bf16[304,384]{1,0:T(8,128)(2,1)S(1)}, u32[]{:S(2)}, u32[]{:S(2)}) collective-permute-start(bf16[304,384]{1,0:T(8,128)(2,1)S(1)} %get-tuple-element.32), channel_id=1, source_target_pairs={{0,1},{1,0},{2,3},{3,2},{4,5},{5,4},{6,7},{7,6},{8,9},{9,8},{10,11... | collective-permute-start | bytes 700424 | tf_op jit(solution)/shard_map/ppermute | solution.py:485
  11.0 28.5 %collective-permute-start = (bf16[304,384]{1,0:T(8,128)(2,1)S(1)}, bf16[304,384]{1,0:T(8,128)(2,1)S(1)}, u32[]{:S(2)}, u32[]{:S(2)}) collective-permute-start(bf16[304,384]{1,0:T(8,128)(2,1)S(1)} %get-tuple-element.30), channel_id=1, source_target_pairs={{0,1},{1,0},{2,3},{3,2},{4,5},{5,4},{6,7},{7,6},{8,9},{9,8},{10,11... | collective-permute-start | bytes 700424 | tf_op jit(solution)/shard_map/ppermute | solution.py:484
  11.5 31.3 %collective-permute-start.1 = (bf16[304,384]{1,0:T(8,128)(2,1)S(1)}, bf16[304,384]{1,0:T(8,128)(2,1)S(1)}, u32[]{:S(2)}, u32[]{:S(2)}) collective-permute-start(bf16[304,384]{1,0:T(8,128)(2,1)S(1)} %get-tuple-element.31), channel_id=1, source_target_pairs={{0,8},{8,0},{1,9},{9,1},{2,10},{10,2},{3,11},{11,3},{4,12},{12,4},... | collective-permute-start | bytes 700424 | tf_op jit(solution)/shard_map/ppermute | solution.py:484
  13.5 29.4 %collective-permute-start.3 = (bf16[304,384]{1,0:T(8,128)(2,1)S(1)}, bf16[304,384]{1,0:T(8,128)(2,1)S(1)}, u32[]{:S(2)}, u32[]{:S(2)}) collective-permute-start(bf16[304,384]{1,0:T(8,128)(2,1)S(1)} %collective-permute-done.2), channel_id=1, source_target_pairs={{0,8},{8,0},{1,9},{9,1},{2,10},{10,2},{3,11},{11,3},{4,12},{12,4},... | collective-permute-start | bytes 700424 | tf_op jit(solution)/shard_map/ppermute | solution.py:485
  15.2 8.6 %collective-permute-start.13 = (bf16[12,1536]{1,0:T(8,128)(2,1)S(1)}, bf16[12,1536]{1,0:T(8,128)(2,1)S(1)}, u32[]{:S(2)}, u32[]{:S(2)}) collective-permute-start(bf16[12,1536]{1,0:T(8,128)(2,1)S(1)} %copy-done.5), channel_id=1, source_target_pairs={{0,16},{16,32},{32,48},{48,0},{1,17},{17,33},{33,49},{49,1},{2,18}... | collective-permute-start | bytes 110600 | tf_op jit(solution)/shard_map/ppermute | solution.py:244
  16.4 7.5 %collective-permute-start.14 = (bf16[12,1536]{1,0:T(8,128)(2,1)S(1)}, bf16[12,1536]{1,0:T(8,128)(2,1)S(1)}, u32[]{:S(2)}, u32[]{:S(2)}) collective-permute-start(bf16[12,1536]{1,0:T(8,128)(2,1)S(1)} %copy-done.5), channel_id=1, source_target_pairs={{0,32},{16,48},{32,0},{48,16},{1,33},{17,49},{33,1},{49,17},{2,34}... | collective-permute-start | bytes 110600 | tf_op jit(solution)/shard_map/ppermute | solution.py:244
  23.8 47.3 %collective-permute-start.33 = (bf16[2,192,768]{2,1,0:T(8,128)(2,1)S(1)}, bf16[2,192,768]{2,1,0:T(8,128)(2,1)S(1)}, u32[]{:S(2)}, u32[]{:S(2)}) collective-permute-start(bf16[2,192,768]{2,1,0:T(8,128)(2,1)S(1)} %get-tuple-element.43), channel_id=1, source_target_pairs={{0,16},{16,0},{32,48},{48,32},{1,17},{17,1},{33,49},{49,33},{2,18}... | collective-permute-start | bytes 1769480 | tf_op jit(solution)/shard_map/ppermute | solution.py:443
  23.9 14.7 %collective-permute-start.15 = (bf16[12,1536]{1,0:T(8,128)(2,1)S(1)}, bf16[12,1536]{1,0:T(8,128)(2,1)S(1)}, u32[]{:S(2)}, u32[]{:S(2)}) collective-permute-start(bf16[12,1536]{1,0:T(8,128)(2,1)S(1)} %copy-done.5), channel_id=1, source_target_pairs={{0,48},{16,0},{32,16},{48,32},{1,49},{17,1},{33,17},{49,33},{2,50}... | collective-permute-start | bytes 110600 | tf_op jit(solution)/shard_map/ppermute | solution.py:244
  38.6 34.8 %collective-permute-start.34 = (bf16[2,192,768]{2,1,0:T(8,128)(2,1)S(1)}, bf16[2,192,768]{2,1,0:T(8,128)(2,1)S(1)}, u32[]{:S(2)}, u32[]{:S(2)}) collective-permute-start(bf16[2,192,768]{2,1,0:T(8,128)(2,1)S(1)} %get-tuple-element.44), channel_id=1, source_target_pairs={{0,48},{48,0},{16,32},{32,16},{1,49},{49,1},{17,33},{33,17},{2,50}... | collective-permute-start | bytes 1769480 | tf_op jit(solution)/shard_map/ppermute | solution.py:444
  39.5 5.9 %collective-permute-start.16 = (bf16[48,1536]{1,0:T(8,128)(2,1)S(1)}, bf16[48,1536]{1,0:T(8,128)(2,1)S(1)}, u32[]{:S(2)}, u32[]{:S(2)}) collective-permute-start(bf16[48,1536]{1,0:T(8,128)(2,1)S(1)} %joined.2.refs_0_), channel_id=1, source_target_pairs={{0,64},{64,0},{1,65},{65,1},{2,66},{66,2},{3,67},{67,3},{4,68},{68... | collective-permute-start | bytes 442376 | tf_op jit(solution)/shard_map/ppermute | solution.py:246
  42.9 5.5 %collective-permute-start.4 = (bf16[128,384]{1,0:T(8,128)(2,1)S(1)}, bf16[128,384]{1,0:T(8,128)(2,1)S(1)}, u32[]{:S(2)}, u32[]{:S(2)}) collective-permute-start(bf16[128,384]{1,0:T(8,128)(2,1)S(1)} %own_queries.1.refs_4_), channel_id=1, source_target_pairs={{0,2},{2,4},{4,6},{6,0},{1,3},{3,5},{5,7},{7,1},{8,10},{10,12},{12... | collective-permute-start | bytes 294920 | tf_op jit(solution)/shard_map/ppermute | solution.py:492
  45.4 77.8 %slice-start = ((s8[4718592]{0:T(1024)(128)(4,1)}), s8[4194304]{0:T(1024)(128)(4,1)S(1)}, s32[]{:S(2)}) async-start(s8[4718592]{0:T(1024)(128)(4,1)} %bitcast.12), calls=%async_computation | async-start | bytes 8388608
  45.4 19.4 %collective-permute-start.17 = (bf16[96,1536]{1,0:T(8,128)(2,1)S(1)}, bf16[96,1536]{1,0:T(8,128)(2,1)S(1)}, u32[]{:S(2)}, u32[]{:S(2)}) collective-permute-start(bf16[96,1536]{1,0:T(8,128)(2,1)S(1)} %joined.3.refs_0_), channel_id=1, source_target_pairs={{0,8},{8,0},{1,9},{9,1},{2,10},{10,2},{3,11},{11,3},{4,12},{12,4},... | collective-permute-start | bytes 884744 | tf_op jit(solution)/shard_map/ppermute | solution.py:248
  45.6 19.2 %collective-permute-start.19 = (bf16[96,1536]{1,0:T(8,128)(2,1)S(1)}, bf16[96,1536]{1,0:T(8,128)(2,1)S(1)}, u32[]{:S(2)}, u32[]{:S(2)}) collective-permute-start(bf16[96,1536]{1,0:T(8,128)(2,1)S(1)} %joined.3.refs_0_), channel_id=1, source_target_pairs={{0,6},{2,0},{4,2},{6,4},{1,7},{3,1},{5,3},{7,5},{8,14},{10,8},{12,... | collective-permute-start | bytes 884744 | tf_op jit(solution)/shard_map/ppermute | solution.py:252
  48.4 5.0 %collective-permute-start.5 = (bf16[128,384]{1,0:T(8,128)(2,1)S(1)}, bf16[128,384]{1,0:T(8,128)(2,1)S(1)}, u32[]{:S(2)}, u32[]{:S(2)}) collective-permute-start(bf16[128,384]{1,0:T(8,128)(2,1)S(1)} %own_queries.1.refs_4_), channel_id=1, source_target_pairs={{0,4},{2,6},{4,0},{6,2},{1,5},{3,7},{5,1},{7,3},{8,12},{10,14},{12... | collective-permute-start | bytes 294920 | tf_op jit(solution)/shard_map/ppermute | solution.py:492
  53.3 4.6 %collective-permute-start.6 = (bf16[128,384]{1,0:T(8,128)(2,1)S(1)}, bf16[128,384]{1,0:T(8,128)(2,1)S(1)}, u32[]{:S(2)}, u32[]{:S(2)}) collective-permute-start(bf16[128,384]{1,0:T(8,128)(2,1)S(1)} %own_queries.1.refs_4_), channel_id=1, source_target_pairs={{0,6},{2,0},{4,2},{6,4},{1,7},{3,1},{5,3},{7,5},{8,14},{10,8},{12,... | collective-permute-start | bytes 294920 | tf_op jit(solution)/shard_map/ppermute | solution.py:492
  61.4 8.6 %collective-permute-start.7 = (bf16[128,512]{1,0:T(8,128)(2,1)S(1)}, bf16[128,512]{1,0:T(8,128)(2,1)S(1)}, u32[]{:S(2)}, u32[]{:S(2)}) collective-permute-start(bf16[128,512]{1,0:T(8,128)(2,1)S(1)} %get-tuple-element.34), channel_id=1, source_target_pairs={{0,6},{2,0},{4,2},{6,4},{1,7},{3,1},{5,3},{7,5},{8,14},{10,8},{12,... | collective-permute-start | bytes 393224 | tf_op jit(solution)/shard_map/ppermute | solution.py:494
  64.9 17.0 %collective-permute-start.18 = (bf16[96,1536]{1,0:T(8,128)(2,1)S(1)}, bf16[96,1536]{1,0:T(8,128)(2,1)S(1)}, u32[]{:S(2)}, u32[]{:S(2)}) collective-permute-start(bf16[96,1536]{1,0:T(8,128)(2,1)S(1)} %joined.3.refs_0_), channel_id=1, source_target_pairs={{0,2},{2,4},{4,6},{6,0},{1,3},{3,5},{5,7},{7,1},{8,10},{10,12},{12... | collective-permute-start | bytes 884744 | tf_op jit(solution)/shard_map/ppermute | solution.py:251
  64.9 23.2 %collective-permute-start.24 = (bf16[96,1536]{1,0:T(8,128)(2,1)S(1)}, bf16[96,1536]{1,0:T(8,128)(2,1)S(1)}, u32[]{:S(2)}, u32[]{:S(2)}) collective-permute-start(bf16[96,1536]{1,0:T(8,128)(2,1)S(1)} %joined.3.refs_0_), channel_id=1, source_target_pairs={{0,1},{1,0},{2,3},{3,2},{4,5},{5,4},{6,7},{7,6},{8,9},{9,8},{10,11... | collective-permute-start | bytes 884744 | tf_op jit(solution)/shard_map/ppermute | solution.py:256
  70.0 6.7 %collective-permute-start.8 = (bf16[128,512]{1,0:T(8,128)(2,1)S(1)}, bf16[128,512]{1,0:T(8,128)(2,1)S(1)}, u32[]{:S(2)}, u32[]{:S(2)}) collective-permute-start(bf16[128,512]{1,0:T(8,128)(2,1)S(1)} %get-tuple-element.35), channel_id=1, source_target_pairs={{0,4},{2,6},{4,0},{6,2},{1,5},{3,7},{5,1},{7,3},{8,12},{10,14},{12... | collective-permute-start | bytes 393224 | tf_op jit(solution)/shard_map/ppermute | solution.py:494
  71.1 9.2 %collective-permute-start.9 = (bf16[128,512]{1,0:T(8,128)(2,1)S(1)}, bf16[128,512]{1,0:T(8,128)(2,1)S(1)}, u32[]{:S(2)}, u32[]{:S(2)}) collective-permute-start(bf16[128,512]{1,0:T(8,128)(2,1)S(1)} %get-tuple-element.36), channel_id=1, source_target_pairs={{0,2},{2,4},{4,6},{6,0},{1,3},{3,5},{5,7},{7,1},{8,10},{10,12},{12... | collective-permute-start | bytes 393224 | tf_op jit(solution)/shard_map/ppermute | solution.py:494
  73.4 19.9 %collective-permute-start.20 = (bf16[96,1536]{1,0:T(8,128)(2,1)S(1)}, bf16[96,1536]{1,0:T(8,128)(2,1)S(1)}, u32[]{:S(2)}, u32[]{:S(2)}) collective-permute-start(bf16[96,1536]{1,0:T(8,128)(2,1)S(1)} %collective-permute-done.17.refs_1_), channel_id=1, source_target_pairs={{0,2},{2,4},{4,6},{6,0},{1,3},{3,5},{5,7},{7,1},{8,10},{10,12},{12... | collective-permute-start | bytes 884744 | tf_op jit(solution)/shard_map/ppermute | solution.py:251
  73.5 49.7 %slice-start.1 = ((s8[4718592]{0:T(1024)(128)(4,1)}), s8[524288]{0:T(1024)(128)(4,1)S(1)}, s32[]{:S(2)}) async-start(s8[4718592]{0:T(1024)(128)(4,1)} %bitcast.12), calls=%async_computation.1 | async-start | bytes 1048576
  73.6 49.6 %copy-start.2 = (bf16[1,32,1536]{2,1,0:T(8,128)(2,1)S(1)}, bf16[1,32,1536]{2,1,0:T(8,128)(2,1)}, u32[]{:S(2)}) copy-start(bf16[1,32,1536]{2,1,0:T(8,128)(2,1)} %param.14) | copy-start | bytes 294916
  73.6 49.6 %copy-start.3 = (f32[4,1536]{1,0:T(4,128)S(1)}, f32[4,1536]{1,0:T(4,128)}, u32[]{:S(2)}) copy-start(f32[4,1536]{1,0:T(4,128)} %gate_ref.1) | copy-start | bytes 73732
  76.7 17.0 %collective-permute-start.35 = (bf16[192,768]{1,0:T(8,128)(2,1)S(1)}, bf16[192,768]{1,0:T(8,128)(2,1)S(1)}, u32[]{:S(2)}, u32[]{:S(2)}) collective-permute-start(bf16[192,768]{1,0:T(8,128)(2,1)S(1)} %get-tuple-element.45), channel_id=1, source_target_pairs={{0,48},{48,0},{16,32},{32,16},{1,49},{49,1},{17,33},{33,17},{2,50}... | collective-permute-start | bytes 884744 | tf_op jit(solution)/shard_map/ppermute | solution.py:446
  80.3 13.5 %collective-permute-start.36 = (bf16[192,768]{1,0:T(8,128)(2,1)S(1)}, bf16[192,768]{1,0:T(8,128)(2,1)S(1)}, u32[]{:S(2)}, u32[]{:S(2)}) collective-permute-start(bf16[192,768]{1,0:T(8,128)(2,1)S(1)} %get-tuple-element.46), channel_id=1, source_target_pairs={{0,16},{16,0},{32,48},{48,32},{1,17},{17,1},{33,49},{49,33},{2,18}... | collective-permute-start | bytes 884744 | tf_op jit(solution)/shard_map/ppermute | solution.py:447
  81.8 8.2 %collective-permute-start.10 = (bf16[32,384]{1,0:T(8,128)(2,1)S(1)}, bf16[32,384]{1,0:T(8,128)(2,1)S(1)}, u32[]{:S(2)}, u32[]{:S(2)}) collective-permute-start(bf16[32,384]{1,0:T(8,128)(2,1)S(1)} %get-tuple-element.38), channel_id=1, source_target_pairs={{0,1},{1,0},{2,3},{3,2},{4,5},{5,4},{6,7},{7,6},{8,9},{9,8},{10,11... | collective-permute-start | bytes 73736 | tf_op jit(solution)/shard_map/ppermute | solution.py:499
  88.1 3.4 %collective-permute-start.11 = (bf16[32,384]{1,0:T(8,128)(2,1)S(1)}, bf16[32,384]{1,0:T(8,128)(2,1)S(1)}, u32[]{:S(2)}, u32[]{:S(2)}) collective-permute-start(bf16[32,384]{1,0:T(8,128)(2,1)S(1)} %get-tuple-element.39), channel_id=1, source_target_pairs={{0,8},{8,0},{1,9},{9,1},{2,10},{10,2},{3,11},{11,3},{4,12},{12,4},... | collective-permute-start | bytes 73736 | tf_op jit(solution)/shard_map/ppermute | solution.py:500
  90.0 3.3 %collective-permute-start.12 = (bf16[32,384]{1,0:T(8,128)(2,1)S(1)}, bf16[32,384]{1,0:T(8,128)(2,1)S(1)}, u32[]{:S(2)}, u32[]{:S(2)}) collective-permute-start(bf16[32,384]{1,0:T(8,128)(2,1)S(1)} %get-tuple-element.40), channel_id=1, source_target_pairs={{0,9},{9,0},{1,8},{8,1},{2,11},{11,2},{3,10},{10,3},{4,13},{13,4},... | collective-permute-start | bytes 73736 | tf_op jit(solution)/shard_map/ppermute | solution.py:501
  91.5 7.9 %collective-permute-start.21 = (bf16[96,1536]{1,0:T(8,128)(2,1)S(1)}, bf16[96,1536]{1,0:T(8,128)(2,1)S(1)}, u32[]{:S(2)}, u32[]{:S(2)}) collective-permute-start(bf16[96,1536]{1,0:T(8,128)(2,1)S(1)} %collective-permute-done.17.refs_1_), channel_id=1, source_target_pairs={{0,6},{2,0},{4,2},{6,4},{1,7},{3,1},{5,3},{7,5},{8,14},{10,8},{12,... | collective-permute-start | bytes 884744 | tf_op jit(solution)/shard_map/ppermute | solution.py:252
  93.3 12.5 %collective-permute-start.22 = (bf16[96,1536]{1,0:T(8,128)(2,1)S(1)}, bf16[96,1536]{1,0:T(8,128)(2,1)S(1)}, u32[]{:S(2)}, u32[]{:S(2)}) collective-permute-start(bf16[96,1536]{1,0:T(8,128)(2,1)S(1)} %collective-permute-done.19.refs_3_), channel_id=1, source_target_pairs={{0,6},{2,0},{4,2},{6,4},{1,7},{3,1},{5,3},{7,5},{8,14},{10,8},{12,... | collective-permute-start | bytes 884744 | tf_op jit(solution)/shard_map/ppermute | solution.py:253
  93.3 12.5 %collective-permute-start.25 = (bf16[96,1536]{1,0:T(8,128)(2,1)S(1)}, bf16[96,1536]{1,0:T(8,128)(2,1)S(1)}, u32[]{:S(2)}, u32[]{:S(2)}) collective-permute-start(bf16[96,1536]{1,0:T(8,128)(2,1)S(1)} %collective-permute-done.17.refs_1_), channel_id=1, source_target_pairs={{0,1},{1,0},{2,3},{3,2},{4,5},{5,4},{6,7},{7,6},{8,9},{9,8},{10,11... | collective-permute-start | bytes 884744 | tf_op jit(solution)/shard_map/ppermute | solution.py:256
  93.7 13.7 %collective-permute-start.27 = (bf16[96,1536]{1,0:T(8,128)(2,1)S(1)}, bf16[96,1536]{1,0:T(8,128)(2,1)S(1)}, u32[]{:S(2)}, u32[]{:S(2)}) collective-permute-start(bf16[96,1536]{1,0:T(8,128)(2,1)S(1)} %collective-permute-done.19.refs_3_), channel_id=1, source_target_pairs={{0,1},{1,0},{2,3},{3,2},{4,5},{5,4},{6,7},{7,6},{8,9},{9,8},{10,11... | collective-permute-start | bytes 884744 | tf_op jit(solution)/shard_map/ppermute | solution.py:256
  93.8 15.7 %collective-permute-start.23 = (bf16[96,1536]{1,0:T(8,128)(2,1)S(1)}, bf16[96,1536]{1,0:T(8,128)(2,1)S(1)}, u32[]{:S(2)}, u32[]{:S(2)}) collective-permute-start(bf16[96,1536]{1,0:T(8,128)(2,1)S(1)} %collective-permute-done.20.refs_4_), channel_id=1, source_target_pairs={{0,2},{2,4},{4,6},{6,0},{1,3},{3,5},{5,7},{7,1},{8,10},{10,12},{12... | collective-permute-start | bytes 884744 | tf_op jit(solution)/shard_map/ppermute | solution.py:254
  99.4 10.2 %collective-permute-start.37 = (bf16[2,24,1536]{2,1,0:T(8,128)(2,1)S(1)}, bf16[2,24,1536]{2,1,0:T(8,128)(2,1)S(1)}, u32[]{:S(2)}, u32[]{:S(2)}) collective-permute-start(bf16[2,24,1536]{2,1,0:T(8,128)(2,1)S(1)} %get-tuple-element.48), channel_id=1, source_target_pairs={{0,2},{2,4},{4,6},{6,0},{1,3},{3,5},{5,7},{7,1},{8,10},{10,12},{12... | collective-permute-start | bytes 442376 | tf_op jit(solution)/shard_map/ppermute | solution.py:449
  105.7 5.5 %collective-permute-start.38 = (bf16[2,24,1536]{2,1,0:T(8,128)(2,1)S(1)}, bf16[2,24,1536]{2,1,0:T(8,128)(2,1)S(1)}, u32[]{:S(2)}, u32[]{:S(2)}) collective-permute-start(bf16[2,24,1536]{2,1,0:T(8,128)(2,1)S(1)} %get-tuple-element.49), channel_id=1, source_target_pairs={{0,4},{2,6},{4,0},{6,2},{1,5},{3,7},{5,1},{7,3},{8,12},{10,14},{12... | collective-permute-start | bytes 442376 | tf_op jit(solution)/shard_map/ppermute | solution.py:449
  105.7 8.2 %collective-permute-start.39 = (bf16[2,24,1536]{2,1,0:T(8,128)(2,1)S(1)}, bf16[2,24,1536]{2,1,0:T(8,128)(2,1)S(1)}, u32[]{:S(2)}, u32[]{:S(2)}) collective-permute-start(bf16[2,24,1536]{2,1,0:T(8,128)(2,1)S(1)} %get-tuple-element.50), channel_id=1, source_target_pairs={{0,6},{2,0},{4,2},{6,4},{1,7},{3,1},{5,3},{7,5},{8,14},{10,8},{12,... | collective-permute-start | bytes 442376 | tf_op jit(solution)/shard_map/ppermute | solution.py:449
  107.4 9.1 %collective-permute-start.26 = (bf16[96,1536]{1,0:T(8,128)(2,1)S(1)}, bf16[96,1536]{1,0:T(8,128)(2,1)S(1)}, u32[]{:S(2)}, u32[]{:S(2)}) collective-permute-start(bf16[96,1536]{1,0:T(8,128)(2,1)S(1)} %collective-permute-done.18.refs_2_), channel_id=1, source_target_pairs={{0,1},{1,0},{2,3},{3,2},{4,5},{5,4},{6,7},{7,6},{8,9},{9,8},{10,11... | collective-permute-start | bytes 884744 | tf_op jit(solution)/shard_map/ppermute | solution.py:256
  109.5 12.4 %collective-permute-start.28 = (bf16[96,1536]{1,0:T(8,128)(2,1)S(1)}, bf16[96,1536]{1,0:T(8,128)(2,1)S(1)}, u32[]{:S(2)}, u32[]{:S(2)}) collective-permute-start(bf16[96,1536]{1,0:T(8,128)(2,1)S(1)} %collective-permute-done.20.refs_4_), channel_id=1, source_target_pairs={{0,1},{1,0},{2,3},{3,2},{4,5},{5,4},{6,7},{7,6},{8,9},{9,8},{10,11... | collective-permute-start | bytes 884744 | tf_op jit(solution)/shard_map/ppermute | solution.py:256
  109.6 12.4 %collective-permute-start.29 = (bf16[96,1536]{1,0:T(8,128)(2,1)S(1)}, bf16[96,1536]{1,0:T(8,128)(2,1)S(1)}, u32[]{:S(2)}, u32[]{:S(2)}) collective-permute-start(bf16[96,1536]{1,0:T(8,128)(2,1)S(1)} %collective-permute-done.21.refs_5_), channel_id=1, source_target_pairs={{0,1},{1,0},{2,3},{3,2},{4,5},{5,4},{6,7},{7,6},{8,9},{9,8},{10,11... | collective-permute-start | bytes 884744 | tf_op jit(solution)/shard_map/ppermute | solution.py:256
  111.2 11.2 %collective-permute-start.30 = (bf16[96,1536]{1,0:T(8,128)(2,1)S(1)}, bf16[96,1536]{1,0:T(8,128)(2,1)S(1)}, u32[]{:S(2)}, u32[]{:S(2)}) collective-permute-start(bf16[96,1536]{1,0:T(8,128)(2,1)S(1)} %collective-permute-done.22.refs_6_), channel_id=1, source_target_pairs={{0,1},{1,0},{2,3},{3,2},{4,5},{5,4},{6,7},{7,6},{8,9},{9,8},{10,11... | collective-permute-start | bytes 884744 | tf_op jit(solution)/shard_map/ppermute | solution.py:256
  113.9 11.5 %collective-permute-start.31 = (bf16[96,1536]{1,0:T(8,128)(2,1)S(1)}, bf16[96,1536]{1,0:T(8,128)(2,1)S(1)}, u32[]{:S(2)}, u32[]{:S(2)}) collective-permute-start(bf16[96,1536]{1,0:T(8,128)(2,1)S(1)} %collective-permute-done.23.refs_7_), channel_id=1, source_target_pairs={{0,1},{1,0},{2,3},{3,2},{4,5},{5,4},{6,7},{7,6},{8,9},{9,8},{10,11... | collective-permute-start | bytes 884744 | tf_op jit(solution)/shard_map/ppermute | solution.py:256
  116.5 18.1 %collective-permute-start.40 = (f32[12,1536]{1,0:T(8,128)S(1)}, f32[12,1536]{1,0:T(8,128)S(1)}, u32[]{:S(2)}, u32[]{:S(2)}) collective-permute-start(f32[12,1536]{1,0:T(8,128)S(1)} %get-tuple-element.51), channel_id=1, source_target_pairs={{0,0},{1,64},{8,8},{9,72},{64,1},{65,65},{72,9},{73,73},{2,2},{3,6... | collective-permute-start | bytes 221192 | tf_op jit(solution)/shard_map/ppermute | solution.py:456
  121.9 12.7 %collective-permute-start.41 = (f32[12,1536]{1,0:T(8,128)S(1)}, f32[12,1536]{1,0:T(8,128)S(1)}, u32[]{:S(2)}, u32[]{:S(2)}) collective-permute-start(f32[12,1536]{1,0:T(8,128)S(1)} %get-tuple-element.52), channel_id=1, source_target_pairs={{0,1},{1,65},{8,9},{9,73},{64,0},{65,64},{72,8},{73,72},{2,3},{3,6... | collective-permute-start | bytes 221192 | tf_op jit(solution)/shard_map/ppermute | solution.py:456
  122.0 12.6 %collective-permute-start.42 = (f32[12,1536]{1,0:T(8,128)S(1)}, f32[12,1536]{1,0:T(8,128)S(1)}, u32[]{:S(2)}, u32[]{:S(2)}) collective-permute-start(f32[12,1536]{1,0:T(8,128)S(1)} %get-tuple-element.53), channel_id=1, source_target_pairs={{0,8},{1,72},{8,0},{9,64},{64,9},{65,73},{72,1},{73,65},{2,10},{3,... | collective-permute-start | bytes 221192 | tf_op jit(solution)/shard_map/ppermute | solution.py:456
  122.5 12.2 %collective-permute-start.43 = (f32[12,1536]{1,0:T(8,128)S(1)}, f32[12,1536]{1,0:T(8,128)S(1)}, u32[]{:S(2)}, u32[]{:S(2)}) collective-permute-start(f32[12,1536]{1,0:T(8,128)S(1)} %get-tuple-element.54), channel_id=1, source_target_pairs={{0,9},{1,73},{8,1},{9,65},{64,8},{65,72},{72,0},{73,64},{2,11},{3,... | collective-permute-start | bytes 221192 | tf_op jit(solution)/shard_map/ppermute | solution.py:456

commit v4 on v0

--- a/solution.py
+++ b/solution.py
@@ -222,7 +222,7 @@
     )(place, cot, *[in_vmem(p) for _, p in pieces])
 
 
-def joined(arrays):
+def joined(arrays, first_in_vmem=False):
     rows = [a.shape[0] for a in arrays]
 
     def kernel(*refs):
@@ -231,19 +231,20 @@
             out_ref[at : at + n, :] = ref[...]
             at += n
 
-    return pl.pallas_call(
-        kernel,
-        out_shape=jax.ShapeDtypeStruct((sum(rows), arrays[0].shape[1]), arrays[0].dtype),
+    place_first = in_vmem if first_in_vmem else in_hbm
+    return pl.pallas_call(
+        kernel,
+        out_shape=pltpu.VMEM((sum(rows), arrays[0].shape[1]), arrays[0].dtype),
         compiler_params=room(),
         name="joined",
-    )(in_hbm(arrays[0]), *[in_vmem(a) for a in arrays[1:]])
+    )(place_first(arrays[0]), *[in_vmem(a) for a in arrays[1:]])
 
 
 def weight_pieces(weight):
     on_x = [weight] + [lax.ppermute(weight, "x", turn(k)) for k in (1, 2, 3)]
     on_x = joined(on_x)
     far = lax.ppermute(on_x, "zh", SWAP)
-    near = joined([on_x, far])
+    near = joined([on_x, far], True)
     far = lax.ppermute(near, "zl", SWAP)
     pieces = {(0, 0): near, (1, 0): far}
     for f in range(2):
@@ -343,38 +344,46 @@
 def cut_along_y(place, keep_l, keep_r, got_l, got_r, last_l, last_r):
     half = keep_l.shape[2]
 
-    def kernel(place_ref, kl, kr, gl, gr, ll, lr, own, one, two, three, total):
+    def kernel(place_ref, kl, kr, gl, gr, ll, lr, own, pair, away, total):
         total[:, :half] = kl[0] + gl[0].astype(F32) + ll[...].astype(F32)
         total[:, half:] = kr[0] + gr[0].astype(F32) + lr[...].astype(F32)
         y = place_ref[1]
-        for k, ref in enumerate((own, one, two, three)):
-            at = ((y + k) % 4) * 24
+        for ref, first, yy in ((own, 0, y), (pair, 0, y ^ 1), (away, 0, 3 - y), (away, 2, 3 - (y ^ 1))):
             for z in range(2):
-                rows = total[pl.ds(pl.multiple_of(z * 96 + at, 8), 24), :]
-                ref[z] = rows.astype(ref.dtype)
+                rows = total[pl.ds(pl.multiple_of(z * 96 + yy * 24, 8), 24), :]
+                ref[first + z] = rows.astype(ref.dtype)
 
     first = pl.BlockSpec((1, 192, half), lambda i: (0, 0, 0))
-    out = pl.BlockSpec((2, 24, 2 * half), lambda i: (0, 0, 0))
+    sizes = ((2, F32), (2, F32), (4, BF))
     return pl.pallas_call(
         kernel,
         grid=(1,),
         in_specs=[scalars()] + [first] * 2 + [pl.BlockSpec(memory_space=pltpu.VMEM)] * 4,
-        out_specs=[out] * 4,
-        out_shape=[jax.ShapeDtypeStruct((2, 24, 2 * half), F32)]
-        + [jax.ShapeDtypeStruct((2, 24, 2 * half), BF)] * 3,
+        out_specs=[pl.BlockSpec((n, 24, 2 * half), lambda i: (0, 0, 0)) for n, _ in sizes],
+        out_shape=[jax.ShapeDtypeStruct((n, 24, 2 * half), t) for n, t in sizes],
         scratch_shapes=[pltpu.VMEM((192, 2 * half), F32)],
         compiler_params=room(),
         name="cut_along_y",
     )(place, keep_l, keep_r, *[in_vmem(a) for a in (got_l, got_r, last_l, last_r)])
 
 
-def cut_to_owners(place, own, others):
+def for_pair(pair, got):
+    def kernel(pair_ref, got_ref, out_ref):
+        out_ref[...] = (pair_ref[...] + got_ref[2:4].astype(F32)).astype(BF)
+
+    return pl.pallas_call(
+        kernel,
+        out_shape=jax.ShapeDtypeStruct(pair.shape, BF),
+        compiler_params=room(),
+        name="for_pair",
+    )(pair, in_vmem(got))
+
+
+def cut_to_owners(place, own, got, last):
     width = own.shape[2]
 
-    def kernel(place_ref, own_ref, a, b, d, *outs):
-        total = own_ref[...]
-        for ref in (a, b, d):
-            total = total + ref[...].astype(F32)
+    def kernel(place_ref, own_ref, got_ref, last_ref, *outs):
+        total = own_ref[...] + got_ref[0:2].astype(F32) + last_ref[...].astype(F32)
         spot = place_ref[0] * 2 + place_ref[3]
         for here in range(4):
 
@@ -386,11 +395,11 @@
 
     return pl.pallas_call(
         kernel,
-        in_specs=[scalars()] + [pl.BlockSpec()] * 4,
+        in_specs=[scalars()] + [pl.BlockSpec()] * 3,
         out_shape=[jax.ShapeDtypeStruct((12, width), F32)] * 4,
         compiler_params=room(),
         name="cut_to_owners",
-    )(place, own, *[in_vmem(a) for a in others])
+    )(place, own, in_vmem(got), in_vmem(last))
 
 
 def added(arrays):
@@ -423,9 +432,10 @@
     on_l, on_r = onward_of(keep_l, keep_r, got_l, got_r)
     last_l = lax.ppermute(on_l, "x", wrap)
     last_r = lax.ppermute(on_r, "x", near)
-    own, *others = cut_along_y(place, keep_l, keep_r, got_l, got_r, last_l, last_r)
-    others = [lax.ppermute(a, "y", turn(k)) for a, k in zip(others, (1, 2, 3))]
-    cuts = cut_to_owners(place, own, others)
+    own, pair, away = cut_along_y(place, keep_l, keep_r, got_l, got_r, last_l, last_r)
+    got = lax.ppermute(away, "y", wrap)
+    last = lax.ppermute(for_pair(pair, got), "y", near)
+    cuts = cut_to_owners(place, own, got, last)
 
     def owner(far_z, far_c):
         spots = [(h, z, k) for h in range(2) for z in range(2) for k in range(2)]

time: 136 us -> 150 us (1.10)
  waiting for transfers between devices: 38.4 us -> 57.2 us
  starting transfers between devices: 62.1 us -> 58.6 us
    ppermute x3, waiting for transfers between devices: 3.62 us -> 17.6 us  [step(): lax.ppermute(partial[k], 'y', turn(-k))]
    ppermute x1, waiting for transfers between devices: 0.01 us -> 4.42 us  [weight_gradient(): got = lax.ppermute(theirs, 'c', SWAP)]
    ppermute x1, starting transfers between devices: 5.89 us -> 2.07 us  [step(): lax.ppermute(mixed[1], 'c', SWAP)]
    ppermute x3, waiting for transfers between devices: 7.24 us -> 3.67 us  [step(): all_queries = [own] + [lax.ppermute(own, 'y', turn(k)) for k in (1, 2, 3)]]
    ppermute x1, waiting for transfers between devices: 1.15 us -> 4.6 us  [weight_pieces(): far = lax.ppermute(on_x, 'zh', SWAP)]
    ppermute x3, waiting for transfers between devices: 13.5 us -> 16.8 us  [weight_pieces(): on_x = [weight] + [lax.ppermute(weight, 'x', turn(k)) for k in (1, 2, 3)]]
    ppermute x8, starting transfers between devices: 12.5 us -> 15.8 us  [weight_pieces(): lax.ppermute(p, 'c', SWAP)]
    ppermute x3, starting transfers between devices: 4.89 us -> 1.87 us  [weight_pieces(): on_x = [weight] + [lax.ppermute(weight, 'x', turn(k)) for k in (1, 2, 3)]]
  transfers between devices with their start and end apart: 44 -> 43, of which waited for: 12 -> 13; matrix products, arithmetic and copies ran while one was open for 0% -> 0% of each run, Pallas kernels for 19% -> 13%
where the time goes in v4:
time: 150 us
  starting transfers between devices  58.6 us (39%)
  waiting for transfers between devices  57.2 us (38%)
  Pallas kernels  25 us (17%)
  matrix products  6.56 us (4%)
  between operations  2.25 us (2%)
    ppermute x3, waiting for transfers between devices, step(): lax.ppermute(partial[k], 'y', turn(-k))  17.6 us
    ppermute x3, waiting for transfers between devices, weight_pieces(): on_x = [weight] + [lax.ppermute(weight, 'x', turn(k)) for k in (1, 2, 3)]  16.8 us
    ppermute x8, starting transfers between devices, weight_pieces(): lax.ppermute(p, 'c', SWAP)  15.8 us
    pallas_call x1, Pallas kernels, grad_of_input(): pl.pallas_call(kernel, grid=(rows // block,), out_shape=jax.ShapeDtypeStr...  9.03 us
    ppermute x3, starting transfers between devices, step(): all_queries = [own] + [lax.ppermute(own, 'y', turn(k)) for k in (1, 2, 3)]  6.73 us
    dot_general x1, matrix products, weight_gradient(): lax.dot_general(theirs, critic_cot, (((0,), (0,)), ((), ())), preferred_e...  6.56 us
    ppermute x4, starting transfers between devices, weight_gradient(): lax.ppermute(a, ('zh', 'zl', 'c'), owner(n // 2, n % 2))  5.95 us
    pallas_call x1, Pallas kernels, product_and_split(): pl.pallas_call(kernel, grid_spec=pltpu.PrefetchScalarGridSpec(num_scalar_...  5.54 us
  transfers between devices with their start and end apart: 43, of which 13 were waited for; matrix products, arithmetic and copies ran while one was open for 0% of the time, Pallas kernels for 13%

profile of v4, /device:TPU:1, one launch (start us, length us, event | category | flops | bytes accessed | tf_op | source)
XLA Modules:
  0.0 149.6 jit_solution(16638758018198846656)
XLA Ops:
  0.6 6.6 %multiply_convert_fusion = bf16[768,1536]{1,0:T(8,128)(2,1)} fusion(bf16[1024,1536]{1,0:T(8,128)(2,1)} %cot_ref.3, bf16[1024,1536]{1,0:T(8,128)(2,1)} %in_ref.1, s32[]{:T(128)S(6)} %select_n.3), kind=kOutput, calls=%fused_computation | convolution fusion | flops 2418278400 | bytes 7077892 | tf_op jit(solution)/shard_map/dot_general | solution.py:421
  7.2 1.4 collective-permute-start.32
  8.6 0.1 stack.23.place_ref
  8.7 4.4 %collective-permute-done.32.got_ref = bf16[768,1536]{1,0:T(8,128)(2,1)} collective-permute-done((bf16[768,1536]{1,0:T(8,128)(2,1)}, bf16[768,1536]{1,0:T(8,128)(2,1)}, u32[]{:S(2)}, u32[]{:S(2)}) %collective-permute-start.32) | collective-permute-done | bytes 2359328 | tf_op jit(solution)/shard_map/ppermute | solution.py:426
  13.1 5.5 %product_and_split.1 = (bf16[2,192,768]{2,1,0:T(8,128)(2,1)S(1)}, bf16[2,192,768]{2,1,0:T(8,128)(2,1)S(1)}, f32[2,192,768]{2,1,0:T(8,128)S(1)}, f32[2,192,768]{2,1,0:T(8,128)S(1)}) custom-call(s32[5]{0:T(128)S(1)} %stack.23.place_ref, bf16[1024,1536]{1,0:T(8,128)(2,1)} %in_ref.1, bf16[1024,1536]{1,0:T(8,128)(2,1)S(1)} %copy-done, ...), custom_call_target="tpu_custom_call" | custom-call | tf_op jit(solution)/shard_map/product_and_split/pallas_call | solution.py:307
  18.6 1.4 collective-permute-start.33
  20.0 1.8 %collective-permute-start.34 = (bf16[2,192,768]{2,1,0:T(8,128)(2,1)S(1)}, bf16[2,192,768]{2,1,0:T(8,128)(2,1)S(1)}, u32[]{:S(2)}, u32[]{:S(2)}) collective-permute-start(bf16[2,192,768]{2,1,0:T(8,128)(2,1)S(1)} %get-tuple-element.43), channel_id=1, source_target_pairs={{0,48},{48,0},{16,32},{32,16},{1,49},{49,1},{17,33},{33,17},{2,50}... | collective-permute-start | bytes 1769480 | tf_op jit(solution)/shard_map/ppermute | solution.py:431
  22.5 1.3 packed.1
  23.8 1.0 collective-permute-start.2
  24.8 0.3 collective-permute-start.13
  25.2 0.4 collective-permute-start
  25.5 11.0 %collective-permute-done.13.refs_1_ = bf16[12,1536]{1,0:T(8,128)(2,1)S(1)} collective-permute-done((bf16[12,1536]{1,0:T(8,128)(2,1)S(1)}, bf16[12,1536]{1,0:T(8,128)(2,1)S(1)}, u32[]{:S(2)}, u32[]{:S(2)}) %collective-permute-start.13) | collective-permute-done | bytes 36896 | tf_op jit(solution)/shard_map/ppermute | solution.py:244
  36.5 1.2 collective-permute-start.14
  37.8 3.2 %collective-permute-done.14.refs_2_ = bf16[12,1536]{1,0:T(8,128)(2,1)S(1)} collective-permute-done((bf16[12,1536]{1,0:T(8,128)(2,1)S(1)}, bf16[12,1536]{1,0:T(8,128)(2,1)S(1)}, u32[]{:S(2)}, u32[]{:S(2)}) %collective-permute-start.14) | collective-permute-done | bytes 36896 | tf_op jit(solution)/shard_map/ppermute | solution.py:244
  41.0 0.3 collective-permute-start.15
  41.3 2.6 %collective-permute-done.15.refs_3_ = bf16[12,1536]{1,0:T(8,128)(2,1)S(1)} collective-permute-done((bf16[12,1536]{1,0:T(8,128)(2,1)S(1)}, bf16[12,1536]{1,0:T(8,128)(2,1)S(1)}, u32[]{:S(2)}, u32[]{:S(2)}) %collective-permute-start.15) | collective-permute-done | bytes 36896 | tf_op jit(solution)/shard_map/ppermute | solution.py:244
  43.9 1.6 %collective-permute-start.1 = (bf16[304,384]{1,0:T(8,128)(2,1)S(1)}, bf16[304,384]{1,0:T(8,128)(2,1)S(1)}, u32[]{:S(2)}, u32[]{:S(2)}) collective-permute-start(bf16[304,384]{1,0:T(8,128)(2,1)S(1)} %get-tuple-element.30), channel_id=1, source_target_pairs={{0,8},{8,0},{1,9},{9,1},{2,10},{10,2},{3,11},{11,3},{4,12},{12,4},... | collective-permute-start | bytes 700424 | tf_op jit(solution)/shard_map/ppermute | solution.py:472
  45.6 0.8 joined.2.refs_0_
  46.4 3.5 %collective-permute-start.16 = (bf16[48,1536]{1,0:T(8,128)(2,1)S(1)}, bf16[48,1536]{1,0:T(8,128)(2,1)S(1)}, u32[]{:S(2)}, u32[]{:S(2)}) collective-permute-start(bf16[48,1536]{1,0:T(8,128)(2,1)S(1)} %joined.2.refs_0_), channel_id=1, source_target_pairs={{0,64},{64,0},{1,65},{65,1},{2,66},{66,2},{3,67},{67,3},{4,68},{68... | collective-permute-start | bytes 442376 | tf_op jit(solution)/shard_map/ppermute | solution.py:246
  49.9 2.8 %collective-permute-done.3.refs_3_ = bf16[304,384]{1,0:T(8,128)(2,1)S(1)} collective-permute-done((bf16[304,384]{1,0:T(8,128)(2,1)S(1)}, bf16[304,384]{1,0:T(8,128)(2,1)S(1)}, u32[]{:S(2)}, u32[]{:S(2)}) %collective-permute-start.3) | collective-permute-done | bytes 233504 | tf_op jit(solution)/shard_map/ppermute | solution.py:473
  52.7 1.4 collective-permute-start.4
  54.1 4.6 %collective-permute-done.16.refs_1_ = bf16[48,1536]{1,0:T(8,128)(2,1)S(1)} collective-permute-done((bf16[48,1536]{1,0:T(8,128)(2,1)S(1)}, bf16[48,1536]{1,0:T(8,128)(2,1)S(1)}, u32[]{:S(2)}, u32[]{:S(2)}) %collective-permute-start.16) | collective-permute-done | bytes 147488 | tf_op jit(solution)/shard_map/ppermute | solution.py:246
  58.7 0.1 collective-permute-start.17
  58.8 0.1 onward.1
  59.0 1.9 %collective-permute-start.35 = (bf16[192,768]{1,0:T(8,128)(2,1)S(1)}, bf16[192,768]{1,0:T(8,128)(2,1)S(1)}, u32[]{:S(2)}, u32[]{:S(2)}) collective-permute-start(bf16[192,768]{1,0:T(8,128)(2,1)S(1)} %get-tuple-element.44), channel_id=1, source_target_pairs={{0,48},{48,0},{16,32},{32,16},{1,49},{49,1},{17,33},{33,17},{2,50}... | collective-permute-start | bytes 884744 | tf_op jit(solution)/shard_map/ppermute | solution.py:433
  60.9 2.9 %collective-permute-start.5 = (bf16[128,384]{1,0:T(8,128)(2,1)S(1)}, bf16[128,384]{1,0:T(8,128)(2,1)S(1)}, u32[]{:S(2)}, u32[]{:S(2)}) collective-permute-start(bf16[128,384]{1,0:T(8,128)(2,1)S(1)} %own_queries.1.refs_4_), channel_id=1, source_target_pairs={{0,4},{2,6},{4,0},{6,2},{1,5},{3,7},{5,1},{7,3},{8,12},{10,14},{12... | collective-permute-start | bytes 294920 | tf_op jit(solution)/shard_map/ppermute | solution.py:480
  63.8 0.8 collective-permute-start.19
  64.6 1.8 %collective-permute-done.5.refs_6_ = bf16[128,384]{1,0:T(8,128)(2,1)S(1)} collective-permute-done((bf16[128,384]{1,0:T(8,128)(2,1)S(1)}, bf16[128,384]{1,0:T(8,128)(2,1)S(1)}, u32[]{:S(2)}, u32[]{:S(2)}) %collective-permute-start.5) | collective-permute-done | bytes 98336 | tf_op jit(solution)/shard_map/ppermute | solution.py:480
  66.3 2.5 %collective-permute-start.6 = (bf16[128,384]{1,0:T(8,128)(2,1)S(1)}, bf16[128,384]{1,0:T(8,128)(2,1)S(1)}, u32[]{:S(2)}, u32[]{:S(2)}) collective-permute-start(bf16[128,384]{1,0:T(8,128)(2,1)S(1)} %own_queries.1.refs_4_), channel_id=1, source_target_pairs={{0,6},{2,0},{4,2},{6,4},{1,7},{3,1},{5,3},{7,5},{8,14},{10,8},{12,... | collective-permute-start | bytes 294920 | tf_op jit(solution)/shard_map/ppermute | solution.py:480
  68.8 1.9 %collective-permute-done.6.refs_7_ = bf16[128,384]{1,0:T(8,128)(2,1)S(1)} collective-permute-done((bf16[128,384]{1,0:T(8,128)(2,1)S(1)}, bf16[128,384]{1,0:T(8,128)(2,1)S(1)}, u32[]{:S(2)}, u32[]{:S(2)}) %collective-permute-start.6) | collective-permute-done | bytes 98336 | tf_op jit(solution)/shard_map/ppermute | solution.py:480
  70.7 3.4 %attend.1 = (bf16[128,512]{1,0:T(8,128)(2,1)S(1)}, bf16[128,512]{1,0:T(8,128)(2,1)S(1)}, bf16[128,512]{1,0:T(8,128)(2,1)S(1)}, bf16[128,512]{1,0:T(8,128)(2,1)S(1)}) custom-call(bf16[304,384]{1,0:T(8,128)(2,1)S(1)} %get-tuple-element.28.refs_0_, bf16[304,384]{1,0:T(8,128)(2,1)S(1)} %collective-permute-done.refs_1_, ...), custom_call_target="tpu_custom_call" | custom-call | tf_op jit(solution)/shard_map/attend/pallas_call | solution.py:112
  74.1 3.0 %collective-permute-start.7 = (bf16[128,512]{1,0:T(8,128)(2,1)S(1)}, bf16[128,512]{1,0:T(8,128)(2,1)S(1)}, u32[]{:S(2)}, u32[]{:S(2)}) collective-permute-start(bf16[128,512]{1,0:T(8,128)(2,1)S(1)} %get-tuple-element.33), channel_id=1, source_target_pairs={{0,6},{2,0},{4,2},{6,4},{1,7},{3,1},{5,3},{7,5},{8,14},{10,8},{12,... | collective-permute-start | bytes 393224 | tf_op jit(solution)/shard_map/ppermute | solution.py:482
  77.2 1.3 collective-permute-start.8
  78.4 11.0 %collective-permute-start.24 = (bf16[96,1536]{1,0:T(8,128)(2,1)S(1)}, bf16[96,1536]{1,0:T(8,128)(2,1)S(1)}, u32[]{:S(2)}, u32[]{:S(2)}) collective-permute-start(bf16[96,1536]{1,0:T(8,128)(2,1)S(1)} %joined.3.refs_0_), channel_id=1, source_target_pairs={{0,1},{1,0},{2,3},{3,2},{4,5},{5,4},{6,7},{7,6},{8,9},{9,8},{10,11... | collective-permute-start | bytes 884744 | tf_op jit(solution)/shard_map/ppermute | solution.py:256
  89.4 0.9 cut_along_y.1
  90.3 2.3 %collective-permute-start.20 = (bf16[96,1536]{1,0:T(8,128)(2,1)S(1)}, bf16[96,1536]{1,0:T(8,128)(2,1)S(1)}, u32[]{:S(2)}, u32[]{:S(2)}) collective-permute-start(bf16[96,1536]{1,0:T(8,128)(2,1)S(1)} %collective-permute-done.17.refs_1_), channel_id=1, source_target_pairs={{0,2},{2,4},{4,6},{6,0},{1,3},{3,5},{5,7},{7,1},{8,10},{10,12},{12... | collective-permute-start | bytes 884744 | tf_op jit(solution)/shard_map/ppermute | solution.py:251
  92.7 0.4 collective-permute-start.37
  93.1 17.6 %collective-permute-done.9.refs_3_ = bf16[128,512]{1,0:T(8,128)(2,1)S(1)} collective-permute-done((bf16[128,512]{1,0:T(8,128)(2,1)S(1)}, bf16[128,512]{1,0:T(8,128)(2,1)S(1)}, u32[]{:S(2)}, u32[]{:S(2)}) %collective-permute-start.9) | collective-permute-done | bytes 131104 | tf_op jit(solution)/shard_map/ppermute | solution.py:482
  110.7 0.5 merged.1
  111.2 2.1 %collective-permute-start.10 = (bf16[32,384]{1,0:T(8,128)(2,1)S(1)}, bf16[32,384]{1,0:T(8,128)(2,1)S(1)}, u32[]{:S(2)}, u32[]{:S(2)}) collective-permute-start(bf16[32,384]{1,0:T(8,128)(2,1)S(1)} %get-tuple-element.37), channel_id=1, source_target_pairs={{0,1},{1,0},{2,3},{3,2},{4,5},{5,4},{6,7},{7,6},{8,9},{9,8},{10,11... | collective-permute-start | bytes 73736 | tf_op jit(solution)/shard_map/ppermute | solution.py:487
  113.2 1.2 collective-permute-start.11
  114.5 1.1 collective-permute-start.12
  115.6 0.6 collective-permute-done.11.c_ref
  116.2 0.6 collective-permute-start.22
  116.8 1.2 collective-permute-done.12.d_ref
  118.0 0.1 collective-permute-start.25
  118.1 0.4 collective-permute-start.27
  118.6 1.5 collective-permute-start.23
  120.1 0.8 collective-permute-start.38
  120.9 4.5 %collective-permute-done.22.refs_6_ = bf16[96,1536]{1,0:T(8,128)(2,1)S(1)} collective-permute-done((bf16[96,1536]{1,0:T(8,128)(2,1)S(1)}, bf16[96,1536]{1,0:T(8,128)(2,1)S(1)}, u32[]{:S(2)}, u32[]{:S(2)}) %collective-permute-start.22) | collective-permute-done | bytes 294944 | tf_op jit(solution)/shard_map/ppermute | solution.py:253
  125.4 1.7 %collective-permute-start.26 = (bf16[96,1536]{1,0:T(8,128)(2,1)S(1)}, bf16[96,1536]{1,0:T(8,128)(2,1)S(1)}, u32[]{:S(2)}, u32[]{:S(2)}) collective-permute-start(bf16[96,1536]{1,0:T(8,128)(2,1)S(1)} %collective-permute-done.18.refs_2_), channel_id=1, source_target_pairs={{0,1},{1,0},{2,3},{3,2},{4,5},{5,4},{6,7},{7,6},{8,9},{9,8},{10,11... | collective-permute-start | bytes 884744 | tf_op jit(solution)/shard_map/ppermute | solution.py:256
  127.1 0.5 collective-permute-start.29
  127.6 0.7 collective-permute-done.23.refs_7_
  128.3 0.9 collective-permute-start.30
  129.2 0.0 collective-permute-done.38.last_ref
  129.2 1.2 collective-permute-start.31
  130.4 0.6 cut_to_owners.1
  131.1 1.9 %collective-permute-start.39 = (f32[12,1536]{1,0:T(8,128)S(1)}, f32[12,1536]{1,0:T(8,128)S(1)}, u32[]{:S(2)}, u32[]{:S(2)}) collective-permute-start(f32[12,1536]{1,0:T(8,128)S(1)} %get-tuple-element.49), channel_id=1, source_target_pairs={{0,0},{1,64},{8,8},{9,72},{64,1},{65,65},{72,9},{73,73},{2,2},{3,6... | collective-permute-start | bytes 221192 | tf_op jit(solution)/shard_map/ppermute | solution.py:444
  133.0 0.1 collective-permute-start.40
  133.1 3.9 %collective-permute-start.41 = (f32[12,1536]{1,0:T(8,128)S(1)}, f32[12,1536]{1,0:T(8,128)S(1)}, u32[]{:S(2)}, u32[]{:S(2)}) collective-permute-start(f32[12,1536]{1,0:T(8,128)S(1)} %get-tuple-element.51), channel_id=1, source_target_pairs={{0,8},{1,72},{8,0},{9,64},{64,9},{65,73},{72,1},{73,65},{2,10},{3,... | collective-permute-start | bytes 221192 | tf_op jit(solution)/shard_map/ppermute | solution.py:444
  137.0 0.1 collective-permute-start.42
  137.8 2.1 %streamed.1 = bf16[32,1536]{1,0:T(8,128)(2,1)} custom-call(s32[5]{0:T(128)S(1)} %stack.23.place_ref, s32[1]{0:T(128)S(6)} %copy.18.step_ref, bf16[32,1536]{1,0:T(8,128)(2,1)S(1)} %bitcast.15, f32[4,1536]{1,0:T(4,128)S(1)} %copy-done.2, bf16[32,384]{1,0:T(8,128)(2,1)S(1)} %get-tuple-element.36.a_ref, bf16[32,384]{1,0:T(8,128)(2,1)S(1)} %collective-permute-done.10.b_ref, ...), custom_call_target="tpu_custom_call" | custom-call | tf_op jit(solution)/shard_map/streamed/pallas_call | solution.py:163
  139.9 9.0 %grad_of_input.1 = bf16[1024,1536]{1,0:T(8,128)(2,1)} custom-call(s32[5]{0:T(128)S(1)} %stack.23.place_ref, bf16[1024,1536]{1,0:T(8,128)(2,1)S(1)} %copy-done, bf16[96,1536]{1,0:T(8,128)(2,1)S(1)} %joined.3.refs_0_, bf16[96,1536]{1,0:T(8,128)(2,1)S(1)} %collective-permute-done.17.refs_1_, bf16[96,1536]{1,0:T(8,128)(2,1)S(1)} %collective-permute-done.18.refs_2_, ...), custom_call_target="tpu_custom_call" | custom-call | tf_op jit(solution)/shard_map/grad_of_input/pallas_call | solution.py:209
  149.0 0.7 added.1
  (53 shorter events, 0.2 us)
Async XLA Ops:
  0.6 12.5 %copy-start = (bf16[1024,1536]{1,0:T(8,128)(2,1)S(1)}, bf16[1024,1536]{1,0:T(8,128)(2,1)}, u32[]{:S(2)}) copy-start(bf16[1024,1536]{1,0:T(8,128)(2,1)} %cot_ref.3) | copy-start | bytes 9437188
  7.2 5.9 %collective-permute-start.32 = (bf16[768,1536]{1,0:T(8,128)(2,1)}, bf16[768,1536]{1,0:T(8,128)(2,1)}, u32[]{:S(2)}, u32[]{:S(2)}) collective-permute-start(bf16[768,1536]{1,0:T(8,128)(2,1)} %multiply_convert_fusion), channel_id=1, source_target_pairs={{0,1},{1,0},{2,3},{3,2},{4,5},{5,4},{6,7},{7,6},{8,9},{9,8},{10,11... | collective-permute-start | bytes 7077896 | tf_op jit(solution)/shard_map/ppermute | solution.py:426
  8.7 13.8 %copy-start.3 = (s32[1,96]{1,0:T(1,128)S(1)}, s32[1,96]{1,0:T(1,128)}, u32[]{:S(2)}) copy-start(s32[1,96]{1,0:T(1,128)} %frames_ref.1) | copy-start | bytes 1156
  8.7 16.2 %copy-start.4 = (bf16[12,1536]{1,0:T(8,128)(2,1)S(1)}, bf16[12,1536]{1,0:T(8,128)(2,1)}, u32[]{:S(2)}) copy-start(bf16[12,1536]{1,0:T(8,128)(2,1)} %refs_0_.1) | copy-start | bytes 110596
  13.1 124.6 %slice-start = ((s8[4718592]{0:T(1024)(128)(4,1)}), s8[4194304]{0:T(1024)(128)(4,1)S(1)}, s32[]{:S(2)}) async-start(s8[4718592]{0:T(1024)(128)(4,1)} %bitcast.13), calls=%async_computation | async-start | bytes 8388608
  18.6 40.2 %collective-permute-start.33 = (bf16[2,192,768]{2,1,0:T(8,128)(2,1)S(1)}, bf16[2,192,768]{2,1,0:T(8,128)(2,1)S(1)}, u32[]{:S(2)}, u32[]{:S(2)}) collective-permute-start(bf16[2,192,768]{2,1,0:T(8,128)(2,1)S(1)} %get-tuple-element.42), channel_id=1, source_target_pairs={{0,16},{16,0},{32,48},{48,32},{1,17},{17,1},{33,49},{49,33},{2,18}... | collective-permute-start | bytes 1769480 | tf_op jit(solution)/shard_map/ppermute | solution.py:430
  20.0 38.8 %collective-permute-start.34 = (bf16[2,192,768]{2,1,0:T(8,128)(2,1)S(1)}, bf16[2,192,768]{2,1,0:T(8,128)(2,1)S(1)}, u32[]{:S(2)}, u32[]{:S(2)}) collective-permute-start(bf16[2,192,768]{2,1,0:T(8,128)(2,1)S(1)} %get-tuple-element.43), channel_id=1, source_target_pairs={{0,48},{48,0},{16,32},{32,16},{1,49},{49,1},{17,33},{33,17},{2,50}... | collective-permute-start | bytes 1769480 | tf_op jit(solution)/shard_map/ppermute | solution.py:431
  23.8 21.7 %collective-permute-start.2 = (bf16[304,384]{1,0:T(8,128)(2,1)S(1)}, bf16[304,384]{1,0:T(8,128)(2,1)S(1)}, u32[]{:S(2)}, u32[]{:S(2)}) collective-permute-start(bf16[304,384]{1,0:T(8,128)(2,1)S(1)} %get-tuple-element.31), channel_id=1, source_target_pairs={{0,1},{1,0},{2,3},{3,2},{4,5},{5,4},{6,7},{7,6},{8,9},{9,8},{10,11... | collective-permute-start | bytes 700424 | tf_op jit(solution)/shard_map/ppermute | solution.py:473
  24.8 11.7 %collective-permute-start.13 = (bf16[12,1536]{1,0:T(8,128)(2,1)S(1)}, bf16[12,1536]{1,0:T(8,128)(2,1)S(1)}, u32[]{:S(2)}, u32[]{:S(2)}) collective-permute-start(bf16[12,1536]{1,0:T(8,128)(2,1)S(1)} %copy-done.4), channel_id=1, source_target_pairs={{0,16},{16,32},{32,48},{48,0},{1,17},{17,33},{33,49},{49,1},{2,18}... | collective-permute-start | bytes 110600 | tf_op jit(solution)/shard_map/ppermute | solution.py:244
  25.2 21.3 %collective-permute-start = (bf16[304,384]{1,0:T(8,128)(2,1)S(1)}, bf16[304,384]{1,0:T(8,128)(2,1)S(1)}, u32[]{:S(2)}, u32[]{:S(2)}) collective-permute-start(bf16[304,384]{1,0:T(8,128)(2,1)S(1)} %get-tuple-element.29), channel_id=1, source_target_pairs={{0,1},{1,0},{2,3},{3,2},{4,5},{5,4},{6,7},{7,6},{8,9},{9,8},{10,11... | collective-permute-start | bytes 700424 | tf_op jit(solution)/shard_map/ppermute | solution.py:472
  36.5 4.4 %collective-permute-start.14 = (bf16[12,1536]{1,0:T(8,128)(2,1)S(1)}, bf16[12,1536]{1,0:T(8,128)(2,1)S(1)}, u32[]{:S(2)}, u32[]{:S(2)}) collective-permute-start(bf16[12,1536]{1,0:T(8,128)(2,1)S(1)} %copy-done.4), channel_id=1, source_target_pairs={{0,32},{16,48},{32,0},{48,16},{1,33},{17,49},{33,1},{49,17},{2,34}... | collective-permute-start | bytes 110600 | tf_op jit(solution)/shard_map/ppermute | solution.py:244
  41.0 2.9 %collective-permute-start.15 = (bf16[12,1536]{1,0:T(8,128)(2,1)S(1)}, bf16[12,1536]{1,0:T(8,128)(2,1)S(1)}, u32[]{:S(2)}, u32[]{:S(2)}) collective-permute-start(bf16[12,1536]{1,0:T(8,128)(2,1)S(1)} %copy-done.4), channel_id=1, source_target_pairs={{0,48},{16,0},{32,16},{48,32},{1,49},{17,1},{33,17},{49,33},{2,50}... | collective-permute-start | bytes 110600 | tf_op jit(solution)/shard_map/ppermute | solution.py:244
  43.9 6.0 %collective-permute-start.1 = (bf16[304,384]{1,0:T(8,128)(2,1)S(1)}, bf16[304,384]{1,0:T(8,128)(2,1)S(1)}, u32[]{:S(2)}, u32[]{:S(2)}) collective-permute-start(bf16[304,384]{1,0:T(8,128)(2,1)S(1)} %get-tuple-element.30), channel_id=1, source_target_pairs={{0,8},{8,0},{1,9},{9,1},{2,10},{10,2},{3,11},{11,3},{4,12},{12,4},... | collective-permute-start | bytes 700424 | tf_op jit(solution)/shard_map/ppermute | solution.py:472
  45.6 7.1 %collective-permute-start.3 = (bf16[304,384]{1,0:T(8,128)(2,1)S(1)}, bf16[304,384]{1,0:T(8,128)(2,1)S(1)}, u32[]{:S(2)}, u32[]{:S(2)}) collective-permute-start(bf16[304,384]{1,0:T(8,128)(2,1)S(1)} %collective-permute-done.2), channel_id=1, source_target_pairs={{0,8},{8,0},{1,9},{9,1},{2,10},{10,2},{3,11},{11,3},{4,12},{12,4},... | collective-permute-start | bytes 700424 | tf_op jit(solution)/shard_map/ppermute | solution.py:473
  46.4 12.3 %collective-permute-start.16 = (bf16[48,1536]{1,0:T(8,128)(2,1)S(1)}, bf16[48,1536]{1,0:T(8,128)(2,1)S(1)}, u32[]{:S(2)}, u32[]{:S(2)}) collective-permute-start(bf16[48,1536]{1,0:T(8,128)(2,1)S(1)} %joined.2.refs_0_), channel_id=1, source_target_pairs={{0,64},{64,0},{1,65},{65,1},{2,66},{66,2},{3,67},{67,3},{4,68},{68... | collective-permute-start | bytes 442376 | tf_op jit(solution)/shard_map/ppermute | solution.py:246
  52.7 85.0 %slice-start.1 = ((s8[4718592]{0:T(1024)(128)(4,1)}), s8[524288]{0:T(1024)(128)(4,1)S(1)}, s32[]{:S(2)}) async-start(s8[4718592]{0:T(1024)(128)(4,1)} %bitcast.13), calls=%async_computation.1 | async-start | bytes 1048576
  52.7 11.0 %collective-permute-start.4 = (bf16[128,384]{1,0:T(8,128)(2,1)S(1)}, bf16[128,384]{1,0:T(8,128)(2,1)S(1)}, u32[]{:S(2)}, u32[]{:S(2)}) collective-permute-start(bf16[128,384]{1,0:T(8,128)(2,1)S(1)} %own_queries.1.refs_4_), channel_id=1, source_target_pairs={{0,2},{2,4},{4,6},{6,0},{1,3},{3,5},{5,7},{7,1},{8,10},{10,12},{12... | collective-permute-start | bytes 294920 | tf_op jit(solution)/shard_map/ppermute | solution.py:480
  58.7 18.4 %collective-permute-start.17 = (bf16[96,1536]{1,0:T(8,128)(2,1)S(1)}, bf16[96,1536]{1,0:T(8,128)(2,1)S(1)}, u32[]{:S(2)}, u32[]{:S(2)}) collective-permute-start(bf16[96,1536]{1,0:T(8,128)(2,1)S(1)} %joined.3.refs_0_), channel_id=1, source_target_pairs={{0,8},{8,0},{1,9},{9,1},{2,10},{10,2},{3,11},{11,3},{4,12},{12,4},... | collective-permute-start | bytes 884744 | tf_op jit(solution)/shard_map/ppermute | solution.py:248
  59.0 18.2 %collective-permute-start.35 = (bf16[192,768]{1,0:T(8,128)(2,1)S(1)}, bf16[192,768]{1,0:T(8,128)(2,1)S(1)}, u32[]{:S(2)}, u32[]{:S(2)}) collective-permute-start(bf16[192,768]{1,0:T(8,128)(2,1)S(1)} %get-tuple-element.44), channel_id=1, source_target_pairs={{0,48},{48,0},{16,32},{32,16},{1,49},{49,1},{17,33},{33,17},{2,50}... | collective-permute-start | bytes 884744 | tf_op jit(solution)/shard_map/ppermute | solution.py:433
  60.9 5.5 %collective-permute-start.5 = (bf16[128,384]{1,0:T(8,128)(2,1)S(1)}, bf16[128,384]{1,0:T(8,128)(2,1)S(1)}, u32[]{:S(2)}, u32[]{:S(2)}) collective-permute-start(bf16[128,384]{1,0:T(8,128)(2,1)S(1)} %own_queries.1.refs_4_), channel_id=1, source_target_pairs={{0,4},{2,6},{4,0},{6,2},{1,5},{3,7},{5,1},{7,3},{8,12},{10,14},{12... | collective-permute-start | bytes 294920 | tf_op jit(solution)/shard_map/ppermute | solution.py:480
  63.8 14.7 %collective-permute-start.36 = (bf16[192,768]{1,0:T(8,128)(2,1)S(1)}, bf16[192,768]{1,0:T(8,128)(2,1)S(1)}, u32[]{:S(2)}, u32[]{:S(2)}) collective-permute-start(bf16[192,768]{1,0:T(8,128)(2,1)S(1)} %get-tuple-element.45), channel_id=1, source_target_pairs={{0,16},{16,0},{32,48},{48,32},{1,17},{17,1},{33,49},{49,33},{2,18}... | collective-permute-start | bytes 884744 | tf_op jit(solution)/shard_map/ppermute | solution.py:434
  63.8 26.5 %collective-permute-start.19 = (bf16[96,1536]{1,0:T(8,128)(2,1)S(1)}, bf16[96,1536]{1,0:T(8,128)(2,1)S(1)}, u32[]{:S(2)}, u32[]{:S(2)}) collective-permute-start(bf16[96,1536]{1,0:T(8,128)(2,1)S(1)} %joined.3.refs_0_), channel_id=1, source_target_pairs={{0,6},{2,0},{4,2},{6,4},{1,7},{3,1},{5,3},{7,5},{8,14},{10,8},{12,... | collective-permute-start | bytes 884744 | tf_op jit(solution)/shard_map/ppermute | solution.py:252
  66.3 4.4 %collective-permute-start.6 = (bf16[128,384]{1,0:T(8,128)(2,1)S(1)}, bf16[128,384]{1,0:T(8,128)(2,1)S(1)}, u32[]{:S(2)}, u32[]{:S(2)}) collective-permute-start(bf16[128,384]{1,0:T(8,128)(2,1)S(1)} %own_queries.1.refs_4_), channel_id=1, source_target_pairs={{0,6},{2,0},{4,2},{6,4},{1,7},{3,1},{5,3},{7,5},{8,14},{10,8},{12,... | collective-permute-start | bytes 294920 | tf_op jit(solution)/shard_map/ppermute | solution.py:480
  74.1 63.6 %copy-start.1 = (bf16[1,32,1536]{2,1,0:T(8,128)(2,1)S(1)}, bf16[1,32,1536]{2,1,0:T(8,128)(2,1)}, u32[]{:S(2)}) copy-start(bf16[1,32,1536]{2,1,0:T(8,128)(2,1)} %param.14) | copy-start | bytes 294916
  74.1 63.6 %copy-start.2 = (f32[4,1536]{1,0:T(4,128)S(1)}, f32[4,1536]{1,0:T(4,128)}, u32[]{:S(2)}) copy-start(f32[4,1536]{1,0:T(4,128)} %gate_ref.1) | copy-start | bytes 73732
  74.1 18.5 %collective-permute-start.7 = (bf16[128,512]{1,0:T(8,128)(2,1)S(1)}, bf16[128,512]{1,0:T(8,128)(2,1)S(1)}, u32[]{:S(2)}, u32[]{:S(2)}) collective-permute-start(bf16[128,512]{1,0:T(8,128)(2,1)S(1)} %get-tuple-element.33), channel_id=1, source_target_pairs={{0,6},{2,0},{4,2},{6,4},{1,7},{3,1},{5,3},{7,5},{8,14},{10,8},{12,... | collective-permute-start | bytes 393224 | tf_op jit(solution)/shard_map/ppermute | solution.py:482
  77.1 34.0 %collective-permute-start.18 = (bf16[96,1536]{1,0:T(8,128)(2,1)S(1)}, bf16[96,1536]{1,0:T(8,128)(2,1)S(1)}, u32[]{:S(2)}, u32[]{:S(2)}) collective-permute-start(bf16[96,1536]{1,0:T(8,128)(2,1)S(1)} %joined.3.refs_0_), channel_id=1, source_target_pairs={{0,2},{2,4},{4,6},{6,0},{1,3},{3,5},{5,7},{7,1},{8,10},{10,12},{12... | collective-permute-start | bytes 884744 | tf_op jit(solution)/shard_map/ppermute | solution.py:251
  77.2 15.9 %collective-permute-start.8 = (bf16[128,512]{1,0:T(8,128)(2,1)S(1)}, bf16[128,512]{1,0:T(8,128)(2,1)S(1)}, u32[]{:S(2)}, u32[]{:S(2)}) collective-permute-start(bf16[128,512]{1,0:T(8,128)(2,1)S(1)} %get-tuple-element.34), channel_id=1, source_target_pairs={{0,4},{2,6},{4,0},{6,2},{1,5},{3,7},{5,1},{7,3},{8,12},{10,14},{12... | collective-permute-start | bytes 393224 | tf_op jit(solution)/shard_map/ppermute | solution.py:482
  78.4 34.8 %collective-permute-start.24 = (bf16[96,1536]{1,0:T(8,128)(2,1)S(1)}, bf16[96,1536]{1,0:T(8,128)(2,1)S(1)}, u32[]{:S(2)}, u32[]{:S(2)}) collective-permute-start(bf16[96,1536]{1,0:T(8,128)(2,1)S(1)} %joined.3.refs_0_), channel_id=1, source_target_pairs={{0,1},{1,0},{2,3},{3,2},{4,5},{5,4},{6,7},{7,6},{8,9},{9,8},{10,11... | collective-permute-start | bytes 884744 | tf_op jit(solution)/shard_map/ppermute | solution.py:256
  90.3 27.8 %collective-permute-start.20 = (bf16[96,1536]{1,0:T(8,128)(2,1)S(1)}, bf16[96,1536]{1,0:T(8,128)(2,1)S(1)}, u32[]{:S(2)}, u32[]{:S(2)}) collective-permute-start(bf16[96,1536]{1,0:T(8,128)(2,1)S(1)} %collective-permute-done.17.refs_1_), channel_id=1, source_target_pairs={{0,2},{2,4},{4,6},{6,0},{1,3},{3,5},{5,7},{7,1},{8,10},{10,12},{12... | collective-permute-start | bytes 884744 | tf_op jit(solution)/shard_map/ppermute | solution.py:251
  92.7 25.9 %collective-permute-start.37 = (bf16[4,24,1536]{2,1,0:T(8,128)(2,1)S(1)}, bf16[4,24,1536]{2,1,0:T(8,128)(2,1)S(1)}, u32[]{:S(2)}, u32[]{:S(2)}) collective-permute-start(bf16[4,24,1536]{2,1,0:T(8,128)(2,1)S(1)} %get-tuple-element.47), channel_id=1, source_target_pairs={{0,6},{6,0},{2,4},{4,2},{1,7},{7,1},{3,5},{5,3},{8,14},{14,8},{10,... | collective-permute-start | bytes 884744 | tf_op jit(solution)/shard_map/ppermute | solution.py:436
  93.1 17.6 %collective-permute-start.9 = (bf16[128,512]{1,0:T(8,128)(2,1)S(1)}, bf16[128,512]{1,0:T(8,128)(2,1)S(1)}, u32[]{:S(2)}, u32[]{:S(2)}) collective-permute-start(bf16[128,512]{1,0:T(8,128)(2,1)S(1)} %get-tuple-element.35), channel_id=1, source_target_pairs={{0,2},{2,4},{4,6},{6,0},{1,3},{3,5},{5,7},{7,1},{8,10},{10,12},{12... | collective-permute-start | bytes 393224 | tf_op jit(solution)/shard_map/ppermute | solution.py:482
  110.7 9.4 %collective-permute-start.21 = (bf16[96,1536]{1,0:T(8,128)(2,1)S(1)}, bf16[96,1536]{1,0:T(8,128)(2,1)S(1)}, u32[]{:S(2)}, u32[]{:S(2)}) collective-permute-start(bf16[96,1536]{1,0:T(8,128)(2,1)S(1)} %collective-permute-done.17.refs_1_), channel_id=1, source_target_pairs={{0,6},{2,0},{4,2},{6,4},{1,7},{3,1},{5,3},{7,5},{8,14},{10,8},{12,... | collective-permute-start | bytes 884744 | tf_op jit(solution)/shard_map/ppermute | solution.py:252
  111.2 3.3 %collective-permute-start.10 = (bf16[32,384]{1,0:T(8,128)(2,1)S(1)}, bf16[32,384]{1,0:T(8,128)(2,1)S(1)}, u32[]{:S(2)}, u32[]{:S(2)}) collective-permute-start(bf16[32,384]{1,0:T(8,128)(2,1)S(1)} %get-tuple-element.37), channel_id=1, source_target_pairs={{0,1},{1,0},{2,3},{3,2},{4,5},{5,4},{6,7},{7,6},{8,9},{9,8},{10,11... | collective-permute-start | bytes 73736 | tf_op jit(solution)/shard_map/ppermute | solution.py:487
  113.2 3.0 %collective-permute-start.11 = (bf16[32,384]{1,0:T(8,128)(2,1)S(1)}, bf16[32,384]{1,0:T(8,128)(2,1)S(1)}, u32[]{:S(2)}, u32[]{:S(2)}) collective-permute-start(bf16[32,384]{1,0:T(8,128)(2,1)S(1)} %get-tuple-element.38), channel_id=1, source_target_pairs={{0,8},{8,0},{1,9},{9,1},{2,10},{10,2},{3,11},{11,3},{4,12},{12,4},... | collective-permute-start | bytes 73736 | tf_op jit(solution)/shard_map/ppermute | solution.py:488
  114.5 3.5 %collective-permute-start.12 = (bf16[32,384]{1,0:T(8,128)(2,1)S(1)}, bf16[32,384]{1,0:T(8,128)(2,1)S(1)}, u32[]{:S(2)}, u32[]{:S(2)}) collective-permute-start(bf16[32,384]{1,0:T(8,128)(2,1)S(1)} %get-tuple-element.39), channel_id=1, source_target_pairs={{0,9},{9,0},{1,8},{8,1},{2,11},{11,2},{3,10},{10,3},{4,13},{13,4},... | collective-permute-start | bytes 73736 | tf_op jit(solution)/shard_map/ppermute | solution.py:489
  116.2 9.2 %collective-permute-start.22 = (bf16[96,1536]{1,0:T(8,128)(2,1)S(1)}, bf16[96,1536]{1,0:T(8,128)(2,1)S(1)}, u32[]{:S(2)}, u32[]{:S(2)}) collective-permute-start(bf16[96,1536]{1,0:T(8,128)(2,1)S(1)} %collective-permute-done.19.refs_3_), channel_id=1, source_target_pairs={{0,6},{2,0},{4,2},{6,4},{1,7},{3,1},{5,3},{7,5},{8,14},{10,8},{12,... | collective-permute-start | bytes 884744 | tf_op jit(solution)/shard_map/ppermute | solution.py:253
  118.0 9.0 %collective-permute-start.25 = (bf16[96,1536]{1,0:T(8,128)(2,1)S(1)}, bf16[96,1536]{1,0:T(8,128)(2,1)S(1)}, u32[]{:S(2)}, u32[]{:S(2)}) collective-permute-start(bf16[96,1536]{1,0:T(8,128)(2,1)S(1)} %collective-permute-done.17.refs_1_), channel_id=1, source_target_pairs={{0,1},{1,0},{2,3},{3,2},{4,5},{5,4},{6,7},{7,6},{8,9},{9,8},{10,11... | collective-permute-start | bytes 884744 | tf_op jit(solution)/shard_map/ppermute | solution.py:256
  118.1 8.9 %collective-permute-start.27 = (bf16[96,1536]{1,0:T(8,128)(2,1)S(1)}, bf16[96,1536]{1,0:T(8,128)(2,1)S(1)}, u32[]{:S(2)}, u32[]{:S(2)}) collective-permute-start(bf16[96,1536]{1,0:T(8,128)(2,1)S(1)} %collective-permute-done.19.refs_3_), channel_id=1, source_target_pairs={{0,1},{1,0},{2,3},{3,2},{4,5},{5,4},{6,7},{7,6},{8,9},{9,8},{10,11... | collective-permute-start | bytes 884744 | tf_op jit(solution)/shard_map/ppermute | solution.py:256
  118.6 9.7 %collective-permute-start.23 = (bf16[96,1536]{1,0:T(8,128)(2,1)S(1)}, bf16[96,1536]{1,0:T(8,128)(2,1)S(1)}, u32[]{:S(2)}, u32[]{:S(2)}) collective-permute-start(bf16[96,1536]{1,0:T(8,128)(2,1)S(1)} %collective-permute-done.20.refs_4_), channel_id=1, source_target_pairs={{0,2},{2,4},{4,6},{6,0},{1,3},{3,5},{5,7},{7,1},{8,10},{10,12},{12... | collective-permute-start | bytes 884744 | tf_op jit(solution)/shard_map/ppermute | solution.py:254
  120.1 9.1 %collective-permute-start.38 = (bf16[2,24,1536]{2,1,0:T(8,128)(2,1)S(1)}, bf16[2,24,1536]{2,1,0:T(8,128)(2,1)S(1)}, u32[]{:S(2)}, u32[]{:S(2)}) collective-permute-start(bf16[2,24,1536]{2,1,0:T(8,128)(2,1)S(1)} %for_pair.1), channel_id=1, source_target_pairs={{0,2},{2,0},{4,6},{6,4},{1,3},{3,1},{5,7},{7,5},{8,10},{10,8},{12,... | collective-permute-start | bytes 442376 | tf_op jit(solution)/shard_map/ppermute | solution.py:437
  125.4 5.7 %collective-permute-start.26 = (bf16[96,1536]{1,0:T(8,128)(2,1)S(1)}, bf16[96,1536]{1,0:T(8,128)(2,1)S(1)}, u32[]{:S(2)}, u32[]{:S(2)}) collective-permute-start(bf16[96,1536]{1,0:T(8,128)(2,1)S(1)} %collective-permute-done.18.refs_2_), channel_id=1, source_target_pairs={{0,1},{1,0},{2,3},{3,2},{4,5},{5,4},{6,7},{7,6},{8,9},{9,8},{10,11... | collective-permute-start | bytes 884744 | tf_op jit(solution)/shard_map/ppermute | solution.py:256
  127.1 5.9 %collective-permute-start.28 = (bf16[96,1536]{1,0:T(8,128)(2,1)S(1)}, bf16[96,1536]{1,0:T(8,128)(2,1)S(1)}, u32[]{:S(2)}, u32[]{:S(2)}) collective-permute-start(bf16[96,1536]{1,0:T(8,128)(2,1)S(1)} %collective-permute-done.20.refs_4_), channel_id=1, source_target_pairs={{0,1},{1,0},{2,3},{3,2},{4,5},{5,4},{6,7},{7,6},{8,9},{9,8},{10,11... | collective-permute-start | bytes 884744 | tf_op jit(solution)/shard_map/ppermute | solution.py:256
  127.1 6.0 %collective-permute-start.29 = (bf16[96,1536]{1,0:T(8,128)(2,1)S(1)}, bf16[96,1536]{1,0:T(8,128)(2,1)S(1)}, u32[]{:S(2)}, u32[]{:S(2)}) collective-permute-start(bf16[96,1536]{1,0:T(8,128)(2,1)S(1)} %collective-permute-done.21.refs_5_), channel_id=1, source_target_pairs={{0,1},{1,0},{2,3},{3,2},{4,5},{5,4},{6,7},{7,6},{8,9},{9,8},{10,11... | collective-permute-start | bytes 884744 | tf_op jit(solution)/shard_map/ppermute | solution.py:256
  128.3 8.7 %collective-permute-start.30 = (bf16[96,1536]{1,0:T(8,128)(2,1)S(1)}, bf16[96,1536]{1,0:T(8,128)(2,1)S(1)}, u32[]{:S(2)}, u32[]{:S(2)}) collective-permute-start(bf16[96,1536]{1,0:T(8,128)(2,1)S(1)} %collective-permute-done.22.refs_6_), channel_id=1, source_target_pairs={{0,1},{1,0},{2,3},{3,2},{4,5},{5,4},{6,7},{7,6},{8,9},{9,8},{10,11... | collective-permute-start | bytes 884744 | tf_op jit(solution)/shard_map/ppermute | solution.py:256
  129.2 10.7 %collective-permute-start.31 = (bf16[96,1536]{1,0:T(8,128)(2,1)S(1)}, bf16[96,1536]{1,0:T(8,128)(2,1)S(1)}, u32[]{:S(2)}, u32[]{:S(2)}) collective-permute-start(bf16[96,1536]{1,0:T(8,128)(2,1)S(1)} %collective-permute-done.23.refs_7_), channel_id=1, source_target_pairs={{0,1},{1,0},{2,3},{3,2},{4,5},{5,4},{6,7},{7,6},{8,9},{9,8},{10,11... | collective-permute-start | bytes 884744 | tf_op jit(solution)/shard_map/ppermute | solution.py:256
  131.1 17.9 %collective-permute-start.39 = (f32[12,1536]{1,0:T(8,128)S(1)}, f32[12,1536]{1,0:T(8,128)S(1)}, u32[]{:S(2)}, u32[]{:S(2)}) collective-permute-start(f32[12,1536]{1,0:T(8,128)S(1)} %get-tuple-element.49), channel_id=1, source_target_pairs={{0,0},{1,64},{8,8},{9,72},{64,1},{65,65},{72,9},{73,73},{2,2},{3,6... | collective-permute-start | bytes 221192 | tf_op jit(solution)/shard_map/ppermute | solution.py:444
  133.0 15.9 %collective-permute-start.40 = (f32[12,1536]{1,0:T(8,128)S(1)}, f32[12,1536]{1,0:T(8,128)S(1)}, u32[]{:S(2)}, u32[]{:S(2)}) collective-permute-start(f32[12,1536]{1,0:T(8,128)S(1)} %get-tuple-element.50), channel_id=1, source_target_pairs={{0,1},{1,65},{8,9},{9,73},{64,0},{65,64},{72,8},{73,72},{2,3},{3,6... | collective-permute-start | bytes 221192 | tf_op jit(solution)/shard_map/ppermute | solution.py:444
  133.1 15.8 %collective-permute-start.41 = (f32[12,1536]{1,0:T(8,128)S(1)}, f32[12,1536]{1,0:T(8,128)S(1)}, u32[]{:S(2)}, u32[]{:S(2)}) collective-permute-start(f32[12,1536]{1,0:T(8,128)S(1)} %get-tuple-element.51), channel_id=1, source_target_pairs={{0,8},{1,72},{8,0},{9,64},{64,9},{65,73},{72,1},{73,65},{2,10},{3,... | collective-permute-start | bytes 221192 | tf_op jit(solution)/shard_map/ppermute | solution.py:444
  137.0 12.0 %collective-permute-start.42 = (f32[12,1536]{1,0:T(8,128)S(1)}, f32[12,1536]{1,0:T(8,128)S(1)}, u32[]{:S(2)}, u32[]{:S(2)}) collective-permute-start(f32[12,1536]{1,0:T(8,128)S(1)} %get-tuple-element.52), channel_id=1, source_target_pairs={{0,9},{1,73},{8,1},{9,65},{64,8},{65,72},{72,0},{73,64},{2,11},{3,... | collective-permute-start | bytes 221192 | tf_op jit(solution)/shard_map/ppermute | solution.py:444
